TPU v7x, 32 devices: a whole 2x2x4 slice. The times are simulated.
32 devices in a mesh: batch: 4 (over y, core), expert: 2 (over x), tensor: 4 (over z).
Axes of the slice: x: 2, y: 2, z: 4, core: 2. Of those that a mesh axis runs over, the one named last changes fastest.
Arguments:
- tokens: bfloat16 [2, 1024, 4096], P('expert', 'batch', 'tensor'), may hold values from -8 to 8
- gain: bfloat16 [4096], P('tensor'), may hold values from 0.5 to 1.5
- phi: bfloat16 [4096, 128], P('tensor'), may hold values from -1 to 1
- w_gate: bfloat16 [2, 4096, 14336], P('expert', None, ('batch', 'tensor')), may hold values from -0.125 to 0.125
- w_up: bfloat16 [2, 4096, 14336], P('expert', None, ('batch', 'tensor')), may hold values from -0.125 to 0.125
- w_down: bfloat16 [2, 14336, 4096], P('expert', ('batch', 'tensor')), may hold values from -0.09375 to 0.09375
Outputs:
- moe_out: bfloat16 [2, 1024, 4096], P('expert', 'batch', 'tensor')
All inputs are finite; a program needn't handle non-finite values.
Results may differ from a plain program's by a relative error of at most 0.025.
Values may be sent and summed in bfloat16 or wider, within the bound.
No kernel may reach another device: no remote copies, remote signals or barrier semaphores. Data moves between devices by JAX's collectives and lax.ppermute only.
A program may use at most 128 MiB of HBM per device.

v0:
```python
import jax
import jax.numpy as jnp
from jax import lax
from jax.sharding import PartitionSpec as P

D = 4096
P_SIZE = 64


def local(tokens, gain, phi, w_gate, w_up, w_down):
    tokens_f = tokens[0].astype(jnp.float32)
    gain_f = gain.astype(jnp.float32)
    scaled = (tokens_f * gain_f[None, :]).astype(jnp.bfloat16)
    squares = jnp.sum(tokens_f * tokens_f, axis=1)
    partial_logits = jnp.dot(scaled, phi, preferred_element_type=jnp.float32)
    squares, partial_logits = lax.psum((squares, partial_logits), "tensor")
    inv_rms = lax.rsqrt(squares / D + 1e-06)
    logits = partial_logits * inv_rms[:, None]
    normed = (tokens_f * gain_f[None, :] * inv_rms[:, None]).astype(jnp.bfloat16)
    combine = jax.nn.softmax(logits, axis=1).astype(jnp.bfloat16)
    column_max = lax.pmax(jnp.max(logits, axis=0), "batch")
    column_total = lax.psum(jnp.sum(jnp.exp(logits - column_max[None, :]), axis=0), "batch")
    dispatch = (jnp.exp(logits - column_max[None, :]) / column_total[None, :]).astype(jnp.bfloat16)
    slot_partial = jnp.einsum("ts,td->sd", dispatch, normed, preferred_element_type=jnp.float32)
    per_device = w_gate.shape[0]
    experts = phi.shape[1] // P_SIZE
    width_share = tokens.shape[2]
    slot_partial = slot_partial.reshape(experts, P_SIZE, width_share)
    quarter = lax.psum_scatter(
        slot_partial.astype(jnp.bfloat16), "batch", scatter_dimension=1, tiled=True
    )
    exchanged = lax.all_to_all(quarter, "expert", split_axis=0, concat_axis=0, tiled=True)
    arrived = lax.all_gather(exchanged, "batch", axis=1, tiled=True)
    groups = arrived.shape[0] // per_device
    arrived = arrived.reshape(groups, per_device, P_SIZE, width_share)
    hidden_share = w_gate.shape[2]
    shard_piece = lax.all_gather(arrived, "tensor", axis=3, tiled=True)
    gate_next = jnp.einsum(
        "gxpd,xdf->gxpf", shard_piece, w_gate, preferred_element_type=jnp.float32
    )
    up_next = jnp.einsum("gxpd,xdf->gxpf", shard_piece, w_up, preferred_element_type=jnp.float32)
    hidden = (jax.nn.silu(gate_next) * up_next).astype(jnp.bfloat16)
    batch_count = lax.axis_size("batch")
    tensor_count = lax.axis_size("tensor")
    hidden = hidden.reshape(groups, per_device, batch_count, P_SIZE // batch_count, hidden_share)
    down_split = w_down.reshape(per_device, hidden_share, tensor_count, D // tensor_count)
    partials = jnp.einsum(
        "gxbqf,xftd->btgxqd", hidden, down_split, preferred_element_type=jnp.float32
    )
    partials = partials.reshape(
        batch_count * tensor_count, groups, per_device, P_SIZE // batch_count, width_share
    ).astype(jnp.bfloat16)
    summed = lax.psum_scatter(
        partials, ("batch", "tensor"), scatter_dimension=0, tiled=True
    ).astype(jnp.float32)
    slot_out = summed[0].astype(jnp.bfloat16)
    returned = lax.all_to_all(slot_out, "expert", split_axis=0, concat_axis=0, tiled=True)
    returned = returned.reshape(experts, P_SIZE // batch_count, width_share)
    returned = lax.all_gather(returned, "batch", axis=1, tiled=True)
    moe_out = jnp.dot(
        combine, returned.reshape(experts * P_SIZE, width_share), preferred_element_type=jnp.float32
    )
    return moe_out.astype(jnp.bfloat16)[None]


def solution(mesh):
    placed = (
        P("expert", "batch", "tensor"),
        P("tensor"),
        P("tensor", None),
        P("expert", None, ("batch", "tensor")),
        P("expert", None, ("batch", "tensor")),
        P("expert", ("batch", "tensor"), None),
    )
    return jax.shard_map(
        local, mesh=mesh, in_specs=placed, out_specs=P("expert", "batch", "tensor"), check_vma=False
    )
```

profile of v0, /device:TPU:0, one launch (start us, length us, event | category | flops | bytes accessed | tf_op | source)
XLA Modules:
  0.0 256.1 jit_solution(10075163442809833708)
XLA Ops:
  6.5 0.0 copy-start
  6.5 0.0 all-reduce.4.cloned.1.call-start
  6.5 0.7 convert_element_type.74
  7.3 0.2 copy-done
  7.5 2.0 fusion.30
  9.5 0.0 all-reduce.4.cloned.1.call-update
  9.5 0.0 reduce-scatter.5.cloned.1.call-start
  9.6 1.2 fusion.25
  10.8 13.5 %psum.22 = f32[256]{0:T(256)S(1)} all-reduce(f32[256]{0:T(256)S(1)} %fusion.25), channel_id=1, replica_groups=mesh['batch'=4,'expert'=2,'tensor'=4] {'tensor'}, use_global_device_ids=true, to_apply=%region_2.0 | all-reduce | flops 256 | bytes 2048 | tf_op jit(solution)/shard_map/psum | solution.py:16
  24.3 22.9 %all-reduce.4.cloned.1.call-done = f32[256,128]{1,0:T(8,128)} async-done(((f32[256,128]{1,0:T(8,128)}), f32[256,128]{1,0:T(8,128)}) %all-reduce.4.cloned.1.call-update) | async-done | bytes 131088 | tf_op jit(solution)/shard_map/psum | solution.py:16
  47.1 1.1 multiply_reduce_fusion.1
  48.2 1.1 fusion.35
  49.4 5.7 %pmax.7 = f32[128]{0:T(128)S(1)} all-reduce(f32[128]{0:T(128)S(1)} %get-tuple-element.6), channel_id=1, replica_groups=mesh['batch'=4,'expert'=2,'tensor'=4] {'batch'}, use_global_device_ids=true, to_apply=%region_6.0 | all-reduce | flops 128 | bytes 1024 | tf_op jit(solution)/shard_map/pmax | solution.py:21
  55.0 1.0 fusion.36
  56.1 6.6 %psum.23 = f32[128]{0:T(128)S(1)} all-reduce(f32[128]{0:T(128)S(1)} %fusion.36), channel_id=1, replica_groups=mesh['batch'=4,'expert'=2,'tensor'=4] {'batch'}, use_global_device_ids=true, to_apply=%region_8.0 | all-reduce | flops 128 | bytes 1024 | tf_op jit(solution)/shard_map/psum | solution.py:22
  62.6 1.0 fusion.40
  63.7 0.1 copy.11
  63.8 2.1 convolution_convert_fusion.1
  65.8 0.0 reduce-scatter.5.cloned.1.call-update
  65.8 0.0 all-gather.4.cloned.1.call-start
  65.9 19.3 %reduce-scatter.5.cloned.1.call-done = bf16[2,16,1024]{2,1,0:T(8,128)(2,1)} async-done(((bf16[2,64,1024]{2,1,0:T(8,128)(2,1)}), bf16[2,16,1024]{2,1,0:T(8,128)(2,1)}) %reduce-scatter.5.cloned.1.call-update) | async-done | bytes 65552 | tf_op jit(solution)/shard_map/reduce_scatter | solution.py:29
  85.2 7.4 %all_to_all.10 = bf16[2,16,1024]{2,1,0:T(8,128)(2,1)S(1)} all-to-all(bf16[2,16,1024]{2,1,0:T(8,128)(2,1)} %reduce-scatter.5.cloned.1.call-done), channel_id=1, replica_groups=mesh['batch'=4,'expert'=2,'tensor'=4] {'expert'}, dimensions={0} | all-to-all | bytes 131072 | tf_op jit(solution)/shard_map/all_to_all | solution.py:32
  92.6 6.2 %all_gather.9 = bf16[2,64,1024]{2,1,0:T(8,128)(2,1)} all-gather(bf16[2,16,1024]{2,1,0:T(8,128)(2,1)S(1)} %all_to_all.10), channel_id=1, replica_groups=mesh['batch'=4,'expert'=2,'tensor'=4] {'batch'}, dimensions={1}, use_global_device_ids=true | all-gather | bytes 327680 | tf_op jit(solution)/shard_map/all_gather | solution.py:33
  98.8 0.0 all-gather.4.cloned.1.call-update
  98.8 0.0 all-reduce.6.cloned.1.call-start
  98.9 12.9 %reshape.85 = bf16[896,4,1024]{2,1,0:T(4,128)(2,1)} reshape(bf16[1,896,4096]{2,1,0:T(8,128)(2,1)} %param.11) | data formatting | bytes 14680064 | tf_op jit(solution)/shard_map/reshape.6
  111.7 14.3 %all-gather.4.cloned.1.call-done = bf16[2,64,4096]{2,1,0:T(8,128)(2,1)} async-done(((bf16[2,64,1024]{2,1,0:T(8,128)(2,1)}), bf16[2,64,4096]{2,1,0:T(8,128)(2,1)}) %all-gather.4.cloned.1.call-update) | async-done | bytes 1048592 | tf_op jit(solution)/shard_map/all_gather | solution.py:37
  126.0 0.0 copy-start.2
  126.0 0.0 slice-start
  126.1 4.8 %fusion.12 = f32[2,1,64,896]{3,2,0,1:T(8,128)S(1)} fusion(bf16[2,64,4096]{2,1,0:T(8,128)(2,1)} %all-gather.4.cloned.1.call-done, bf16[1,4096,896]{2,1,0:T(8,128)(2,1)} %param.9), kind=kOutput, calls=%fused_computation.13 | convolution fusion | flops 939524096 | bytes 8847360 | tf_op jit(solution)/shard_map/gxpd,xdf->gxpf/dot_general | solution.py:38
  130.9 0.0 copy-done.2
  130.9 0.0 slice-start.1
  130.9 4.5 %fusion.21 = bf16[2,1,64,896]{3,2,0,1:T(8,128)(2,1)S(1)} fusion(bf16[2,64,4096]{2,1,0:T(8,128)(2,1)S(1)} %copy-done.2, bf16[1,4096,896]{2,1,0:T(8,128)(2,1)} %param.10, f32[2,1,64,896]{3,2,0,1:T(8,128)S(1)} %fusion.12), kind=kOutput, calls=%fused_computation.17 | convolution fusion | flops 940212224 | bytes 9076736 | tf_op jit(solution)/shard_map/gxpd,xdf->gxpf/dot_general | solution.py:41
  135.4 0.0 slice-done
  135.4 0.0 slice-done.1
  135.5 0.0 copy-start.3
  135.5 0.0 copy-start.1
  135.5 5.7 %fusion.6 = bf16[2,4,16,4,1024]{4,2,3,1,0:T(8,128)(2,1)} fusion(bf16[2,4,16,896,1]{3,2,4,1,0:T(8,128)(2,1)S(1)} %bitcast.91, bf16[896,4,1024,1,1]{2,1,0,4,3:T(4,128)(2,1)S(1)} %bitcast.87), kind=kOutput, calls=%fused_computation.6 | convolution fusion | flops 940048384 | bytes 8617984 | tf_op jit(solution)/shard_map/gxbqf,xftd->btgxqd/dot_general | solution.py:47
  141.2 0.0 all-reduce.6.cloned.1.call-update
  141.2 0.0 copy-done.3
  141.2 0.6 dynamic-slice
  141.8 92.7 %all-reduce.6.cloned.1.call-done = bf16[16,2,1,16,1024]{4,3,0,1,2:T(8,128)(2,1)} async-done(((bf16[16,2,1,16,1024]{4,3,0,1,2:T(8,128)(2,1)}), bf16[16,2,1,16,1024]{4,3,0,1,2:T(8,128)(2,1)}) %all-reduce.6.cloned.1.call-update) | async-done | bytes 1048592
  234.5 1.5 dynamic-slice_bitcast_fusion
  236.0 6.6 %all_to_all.11 = bf16[2,1,16,1024]{3,2,1,0:T(8,128)(2,1)S(1)} all-to-all(bf16[2,1,16,1024]{3,2,1,0:T(8,128)(2,1)S(1)} %dynamic-slice_bitcast_fusion), channel_id=1, replica_groups=mesh['batch'=4,'expert'=2,'tensor'=4] {'expert'}, dimensions={0} | all-to-all | bytes 131072 | tf_op jit(solution)/shard_map/all_to_all | solution.py:57
  242.6 5.8 %all-gather.1 = bf16[2,1,64,1024]{3,2,1,0:T(8,128)(2,1)S(1)} all-gather(bf16[2,1,16,1024]{3,2,1,0:T(8,128)(2,1)S(1)} %all_to_all.11), channel_id=3, replica_groups=mesh['batch'=4,'expert'=2,'tensor'=4] {'batch'}, dimensions={2}, use_global_device_ids=true | all-gather | bytes 327680 | tf_op jit(solution)/shard_map/all_gather | solution.py:59
  248.4 0.0 copy-done.1
  248.4 1.2 fusion.11
  (2 shorter events, 0.0 us)
Async XLA Ops:
  6.5 1.0 copy-start
  6.5 40.6 %all-reduce.4.cloned.1.call-start = ((), (), s32[]{:S(2)}) async-start(), calls=%async_computation.3 | async-start | bytes 262144 | tf_op jit(solution)/shard_map/psum | solution.py:16
  9.5 75.6 %reduce-scatter.5.cloned.1.call-start = ((), (), s32[]{:S(2)}) async-start(), calls=%async_computation.4 | async-start | bytes 327680 | tf_op jit(solution)/shard_map/reduce_scatter | solution.py:29
  65.8 60.2 %all-gather.4.cloned.1.call-start = ((), (), s32[]{:S(2)}) async-start(), calls=%async_computation.5 | async-start | bytes 1310720 | tf_op jit(solution)/shard_map/all_gather | solution.py:37
  98.8 135.7 %all-reduce.6.cloned.1.call-start = ((), (), s32[]{:S(2)}) async-start(), calls=%async_computation.6 | async-start | bytes 2097152
  126.0 4.8 %copy-start.2 = (bf16[2,64,4096]{2,1,0:T(8,128)(2,1)S(1)}, bf16[2,64,4096]{2,1,0:T(8,128)(2,1)}, u32[]{:S(2)}) copy-start(bf16[2,64,4096]{2,1,0:T(8,128)(2,1)} %all-gather.4.cloned.1.call-done) | copy-start | bytes 3145732
  126.0 9.4 %slice-start = ((s8[7340032]{0:T(1024)(128)(4,1)}), s8[4194304]{0:T(1024)(128)(4,1)S(1)}, s32[]{:S(2)}) async-start(s8[7340032]{0:T(1024)(128)(4,1)} %bitcast.85), calls=%async_computation.7 | async-start | bytes 8388608
  130.9 4.6 %slice-start.1 = ((s8[7340032]{0:T(1024)(128)(4,1)}), s8[3145728]{0:T(1024)(128)(4,1)S(1)}, s32[]{:S(2)}) async-start(s8[7340032]{0:T(1024)(128)(4,1)} %bitcast.85), calls=%async_computation.8 | async-start | bytes 6291456
  135.5 5.7 %copy-start.3 = (u32[32]{0:T(128)S(1)}, u32[32]{0:T(128)}, u32[]{:S(2)}) copy-start(u32[32]{0:T(128)} %constant.19) | copy-start | bytes 388
  135.5 112.9 %copy-start.1 = (f32[256,128]{1,0:T(8,128)S(1)}, f32[256,128]{1,0:T(8,128)}, u32[]{:S(2)}) copy-start(f32[256,128]{1,0:T(8,128)} %all-reduce.4.cloned.1.call-done) | copy-start | bytes 393220
Sparse Core Ops, SparseCore 0:
  9.6 37.4 all-reduce.3
  66.0 19.1 reduce-scatter.4
  98.9 27.0 all-gather.3
  141.3 93.1 all-reduce.5
where the time goes:
time: 257 us; the launch traced here: 256 us
  waiting for transfers between devices  149 us (58%)
  blocking collectives  51.7 us (20%)
  matrix products  20.3 us (8%)
  local copies, waits for them, and re-layouts  15.3 us (6%)
  between operations  13.2 us (5%)
  other arithmetic  6.2 us (2%)
    unnamed x5, waiting for transfers between devices  92.7 us
    psum x1, waiting for transfers between devices, local(): squares, partial_logits = lax.psum((squares, partial_logits), 'tensor')  22.9 us
    reduce_scatter x1, waiting for transfers between devices, local(): lax.psum_scatter(slot_partial.astype(jnp.bfloat16), 'batch', scatter_dime...  19.3 us
    all_gather x1, waiting for transfers between devices, local(): shard_piece = lax.all_gather(arrived, 'tensor', axis=3, tiled=True)  14.3 us
    psum x1, blocking collectives, local(): squares, partial_logits = lax.psum((squares, partial_logits), 'tensor')  13.5 us
    another operation x1, local copies, waits for them, and re-layouts  12.9 us
    all_to_all x1, blocking collectives, local(): lax.all_to_all(quarter, 'expert', split_axis=0, concat_axis=0, tiled=True)  7.4 us
    all_to_all x1, blocking collectives, local(): lax.all_to_all(slot_out, 'expert', split_axis=0, concat_axis=0, tiled=True)  6.64 us
  transfers between devices with their start and end apart: 4, of which 4 were waited for; matrix products, arithmetic and copies ran while one was open for 6% of the time, Pallas kernels for 0%

commit v1 on v0

v1 whole, which is shorter than its diff:
```python
import functools

import jax
import jax.numpy as jnp
from jax import lax
from jax.experimental import pallas as pl
from jax.experimental.pallas import tpu as pltpu
from jax.sharding import PartitionSpec as P

BF16, F32 = jnp.bfloat16, jnp.float32
VMEM = pl.BlockSpec(memory_space=pltpu.VMEM)
SMEM = pl.BlockSpec(memory_space=pltpu.SMEM)


def call(body, shapes, *args, cost=(1 << 30, 1 << 22), name=None):
    specs = [SMEM if a.dtype == jnp.int32 else VMEM for a in args]
    return pl.pallas_call(
        body,
        out_shape=shapes,
        in_specs=specs,
        out_specs=jax.tree.map(lambda _: VMEM, shapes),
        cost_estimate=pl.CostEstimate(flops=cost[0], bytes_accessed=cost[1], transcendentals=0),
        compiler_params=pltpu.CompilerParams(vmem_limit_bytes=24 << 20),
        name=name,
    )(*args)


def shape(dims, dtype):
    return jax.ShapeDtypeStruct(tuple(dims), dtype)


def swap(x, axes, bit):
    count = lax.axis_size(axes)
    return lax.ppermute(x, axes, [(i, i ^ bit) for i in range(count)])


def logits_body(tok_ref, gain_ref, phi_ref, scaled_ref, part_ref):
    tok = tok_ref[...].astype(F32)
    scaled = (tok * gain_ref[...].astype(F32)).astype(BF16)
    scaled_ref[...] = scaled
    slots = phi_ref.shape[1]
    part = jnp.dot(scaled, phi_ref[...], preferred_element_type=F32)
    part_ref[:slots] = part.T
    squares = jnp.sum(tok * tok, axis=1, keepdims=True)
    part_ref[slots:] = jnp.broadcast_to(squares, (tok.shape[0], 128)).T[:8]


def logits_of(part_refs, width):
    total = part_refs[0][...]
    for ref in part_refs[1:]:
        total = total + ref[...]
    slots = total.shape[0] - 8
    inv_rms = lax.rsqrt(total[slots : slots + 1] / width + 1e-06)
    return total[:slots] * inv_rms, inv_rms


def slots_body(width, n, *refs):
    part_refs, scaled_ref, message_ref = refs[:n], refs[n], refs[n + 1]
    logits, inv_rms = logits_of(part_refs, width)
    top = jnp.max(logits, axis=1, keepdims=True)
    raised = jnp.exp(logits - top)
    total = jnp.sum(raised, axis=1, keepdims=True)
    weights = (raised * (inv_rms / total)).astype(BF16)
    pieces, rows, wide = message_ref.shape
    share = scaled_ref.shape[1]
    slot = jnp.dot(weights, scaled_ref[...], preferred_element_type=F32)
    message_ref[:, :, :share] = slot.astype(BF16).reshape(pieces, rows, share)
    mass = top + jnp.log(total)
    high = mass.astype(BF16)
    rest = mass - high.astype(F32)
    middle = rest.astype(BF16)
    low = (rest - middle.astype(F32)).astype(BF16)
    lane = lax.broadcasted_iota(jnp.int32, (logits.shape[0], wide - share), 1)
    stats = jnp.where(
        lane == 0,
        high.astype(F32),
        jnp.where(lane == 1, middle.astype(F32), jnp.where(lane == 2, low.astype(F32), 0.0)),
    )
    message_ref[:, :, share:] = stats.astype(BF16).reshape(pieces, rows, wide - share)


def combine_body(width, n, experts, batches, where_ref, *refs):
    part_refs, out_ref, held = refs[:n], refs[n], refs[n + 1]
    logits, _ = logits_of(part_refs, width)
    raised = jnp.exp(logits - jnp.max(logits, axis=0, keepdims=True))
    held[...] = raised / jnp.sum(raised, axis=0, keepdims=True)
    rows = logits.shape[0] // (experts * batches)
    blocks = []
    for r in range(batches):
        for h in range(experts):
            at = ((where_ref[1] ^ h) * batches + (where_ref[0] ^ r)) * rows
            blocks.append(held[pl.ds(pl.multiple_of(at, rows), rows)])
    out_ref[...] = jnp.concatenate(blocks, axis=0).T.astype(BF16)


def gather_body(groups, batches, where_ref, message_ref, out_ref):
    rows, share = message_ref.shape[1], out_ref.shape[1]
    for h in range(groups):
        first = (where_ref[1] ^ h) * batches
        pieces = [message_ref[first + b].astype(F32) for b in range(batches)]
        mass = [
            p[:, share : share + 1] + p[:, share + 1 : share + 2] + p[:, share + 2 : share + 3]
            for p in pieces
        ]
        top = functools.reduce(jnp.maximum, mass)
        raised = [jnp.exp(m - top) for m in mass]
        total = functools.reduce(jnp.add, raised)
        out = sum(p[:, :share] * (w / total) for p, w in zip(pieces, raised))
        out_ref[h * rows : (h + 1) * rows] = out.astype(BF16)


def gate_up_body(batches, where_ref, *refs):
    steps = pl.num_programs(0)
    count = len(refs) - 5
    pieces, (gate_ref, up_ref, out_ref, gate, up) = refs[:count], refs[count:]
    step = pl.program_id(0)
    for s in range(count // batches):

        @pl.when(step == s)
        def _():
            x = jnp.concatenate([pieces[s * batches + r][...] for r in range(batches)], axis=0)
            g = jnp.dot(x, gate_ref[0], preferred_element_type=F32)
            u = jnp.dot(x, up_ref[0], preferred_element_type=F32)
            gate[...] = g if s == 0 else gate[...] + g
            up[...] = u if s == 0 else up[...] + u

    @pl.when(step == steps - 1)
    def _():
        g = gate[...]
        out_ref[...] = (g / (1.0 + jnp.exp(-g)) * up[...]).astype(BF16)


def gate_up(where, pieces, w_gate, w_up, batches):
    share = pieces[0].shape[1]
    rows = pieces[0].shape[0] * batches
    hidden = w_gate.shape[2]
    full = pl.BlockSpec(pieces[0].shape, lambda s, w: (0, 0))
    weight = pl.BlockSpec((1, share, hidden), lambda s, w: (0, w[2] ^ s, 0))
    return pl.pallas_call(
        functools.partial(gate_up_body, batches),
        grid_spec=pltpu.PrefetchScalarGridSpec(
            num_scalar_prefetch=1,
            grid=(len(pieces) // batches,),
            in_specs=[full] * len(pieces) + [weight, weight],
            out_specs=pl.BlockSpec((rows, hidden), lambda s, w: (0, 0)),
            scratch_shapes=[pltpu.VMEM((rows, hidden), F32)] * 2,
        ),
        out_shape=shape((rows, hidden), BF16),
        cost_estimate=pl.CostEstimate(
            flops=4 * rows * hidden * w_gate.shape[1], bytes_accessed=4 * w_gate.size, transcendentals=0
        ),
        compiler_params=pltpu.CompilerParams(vmem_limit_bytes=32 << 20),
        name="gate_up",
    )(where, *pieces, w_gate, w_up)


def down_body(batches, where_ref, hidden_ref, down_ref, *out_refs):
    out = jnp.dot(hidden_ref[...], down_ref[0], preferred_element_type=F32).astype(BF16)
    rows = out.shape[0] // batches
    for r in range(batches):
        out_refs[r][...] = out[r * rows : (r + 1) * rows]


def down(where, hidden, w_down, s, share, batches):
    rows, depth = hidden.shape
    cut = 2
    block = share // cut
    each = rows // batches
    return pl.pallas_call(
        functools.partial(down_body, batches),
        grid_spec=pltpu.PrefetchScalarGridSpec(
            num_scalar_prefetch=1,
            grid=(cut,),
            in_specs=[
                pl.BlockSpec((rows, depth), lambda j, w: (0, 0)),
                pl.BlockSpec((1, depth, block), lambda j, w: (0, 0, (w[2] ^ s) * cut + j)),
            ],
            out_specs=[pl.BlockSpec((each, block), lambda j, w: (0, j))] * batches,
        ),
        out_shape=[shape((each, share), BF16)] * batches,
        cost_estimate=pl.CostEstimate(
            flops=2 * rows * depth * share, bytes_accessed=2 * depth * share, transcendentals=0
        ),
        compiler_params=pltpu.CompilerParams(vmem_limit_bytes=24 << 20),
        name="down",
    )(where, hidden, w_down)


def output_body(combine_ref, *refs):
    pieces, out_ref = refs[:-1], refs[-1]
    slots = jnp.concatenate([p[...] for p in pieces], axis=0)
    out_ref[...] = jnp.dot(combine_ref[...], slots, preferred_element_type=F32).astype(BF16)


def add(*xs):
    return functools.reduce(jnp.add, [x.astype(F32) for x in xs]).astype(BF16)


def local(tokens, gain, phi, w_gate, w_up, w_down):
    batches, experts, tensors = (lax.axis_size(a) for a in ("batch", "expert", "tensor"))
    for n in (batches, experts, tensors):
        assert n & (n - 1) == 0
    assert tokens.shape[0] == 1 and w_gate.shape[0] == 1
    where = jnp.stack([lax.axis_index(a) for a in ("batch", "expert", "tensor")]).astype(jnp.int32)
    width = w_gate.shape[1]
    count, share = tokens.shape[1:]
    slots = phi.shape[1]
    rows = slots // (experts * batches)

    scaled, part = call(
        logits_body,
        [shape((count, share), BF16), shape((slots + 8, count), F32)],
        tokens[0],
        gain[None],
        phi,
        name="logits",
    )
    parts = [part] + [swap(part, "tensor", s) for s in range(1, tensors)]
    message = call(
        functools.partial(slots_body, width, tensors),
        shape((experts * batches, rows, share + 128), BF16),
        *parts,
        scaled,
        name="slots",
    )
    combine = pl.pallas_call(
        functools.partial(combine_body, width, tensors, experts, batches),
        out_shape=shape((count, slots), BF16),
        in_specs=[SMEM] + [VMEM] * tensors,
        out_specs=VMEM,
        scratch_shapes=[pltpu.VMEM((slots, count), F32)],
        cost_estimate=pl.CostEstimate(flops=1 << 30, bytes_accessed=1 << 22, transcendentals=0),
        compiler_params=pltpu.CompilerParams(vmem_limit_bytes=24 << 20),
        name="combine",
    )(where, *parts)
    message = lax.all_to_all(message, ("expert", "batch"), split_axis=0, concat_axis=0, tiled=True)
    own = call(
        functools.partial(gather_body, experts, batches),
        shape((experts * rows, share), BF16),
        where,
        message,
        name="gather",
    )
    pieces = []
    for s in range(tensors):
        group = {0: own if s == 0 else swap(own, "tensor", s)}
        bit = batches >> 1
        while bit:
            group.update({r | bit: swap(group[r], "batch", bit) for r in list(group)})
            bit >>= 1
        pieces += [group[r] for r in range(batches)]
    hidden = gate_up(where, pieces, w_gate, w_up, batches)

    arrived = [[] for _ in range(experts)]
    for s in reversed(range(tensors)):
        partial = dict(enumerate(down(where, hidden, w_down, s, share, batches)))
        bit = 1
        while bit < batches:
            partial = {
                r: add(partial[r], swap(partial[r | bit], "batch", bit)) for r in partial if not r & bit
            }
            bit <<= 1
        for h in range(experts):
            piece = partial[0][h * rows : (h + 1) * rows]
            if h or s:
                piece = swap(piece, ("expert", "tensor"), h * tensors + s)
            arrived[h].append(piece)
    out = jnp.concatenate([add(*a) for a in arrived], axis=0)
    gathered = [out] + [swap(out, "batch", r) for r in range(1, batches)]
    return call(
        output_body, shape((count, share), BF16), combine, *gathered, name="output"
    )[None]


def solution(mesh):
    placed = (
        P("expert", "batch", "tensor"),
        P("tensor"),
        P("tensor", None),
        P("expert", None, ("batch", "tensor")),
        P("expert", None, ("batch", "tensor")),
        P("expert", ("batch", "tensor"), None),
    )
    return jax.shard_map(
        local, mesh=mesh, in_specs=placed, out_specs=P("expert", "batch", "tensor"), check_vma=False
    )
```

time: 257 us -> 98.2 us (0.38)
  waiting for transfers between devices: 149 us -> 36.8 us
  blocking collectives: 51.7 us -> 0 us
  starting transfers between devices: 0.13 us -> 38.2 us
  matrix products: 20.3 us -> 0 us
  Pallas kernels: 0 us -> 13.3 us
  between operations: 13.2 us -> 0.27 us
  local copies, waits for them, and re-layouts: 15.3 us -> 8.88 us
  other arithmetic: 6.2 us -> 0.31 us
    unnamed x5 -> x0, waiting for transfers between devices: 92.7 us -> none
    ppermute x0 -> x40, starting transfers between devices: none -> 34.5 us  [swap(): return lax.ppermute(x, axes, [(i, i ^ bit) for i in range(count)])]
    ppermute x0 -> x40, waiting for transfers between devices: none -> 30.5 us  [swap(): return lax.ppermute(x, axes, [(i, i ^ bit) for i in range(count)])]
    psum x1 -> x0, waiting for transfers between devices: 22.9 us -> none  [local(): squares, partial_logits = lax.psum((squares, partial_logits), 'tensor')]
    dot_general x6 -> x0, matrix products: 20.3 us -> none  [the longest x1 5.68 us: local(): jnp.einsum('gxbqf,xftd->btgxqd', hidden, down_split, preferred_element_ty...]
    psum x2 -> x0, blocking collectives: 20.1 us -> none  [the longest x1 13.5 us: local(): squares, partial_logits = lax.psum((squares, partial_logits), 'tensor')]
    reduce_scatter x1 -> x0, waiting for transfers between devices: 19.3 us -> none  [local(): lax.psum_scatter(slot_partial.astype(jnp.bfloat16), 'batch', scatter_dime...]
    all_gather x1 -> x0, waiting for transfers between devices: 14.3 us -> none  [local(): shard_piece = lax.all_gather(arrived, 'tensor', axis=3, tiled=True)]
  transfers between devices with their start and end apart: 4 -> 41, of which waited for: 4 -> 19; matrix products, arithmetic and copies ran while one was open for 6% -> 0% of each run, Pallas kernels for 0% -> 5%
where the time goes in v1:
time: 98.2 us; the launch traced here: 97.9 us
  starting transfers between devices  38.2 us (39%)
  waiting for transfers between devices  36.8 us (37%)
  Pallas kernels  13.3 us (14%)
  local copies, waits for them, and re-layouts  8.88 us (9%)
    ppermute x40, starting transfers between devices, swap(): return lax.ppermute(x, axes, [(i, i ^ bit) for i in range(count)])  34.5 us
    ppermute x40, waiting for transfers between devices, swap(): return lax.ppermute(x, axes, [(i, i ^ bit) for i in range(count)])  30.5 us
    unnamed x12, local copies, waits for them, and re-layouts  8.17 us
    all_to_all x1, waiting for transfers between devices, local(): lax.all_to_all(message, ('expert', 'batch'), split_axis=0, concat_axis=0,...  6.32 us
    pallas_call x4, Pallas kernels, down(): pl.pallas_call(functools.partial(down_body, batches), grid_spec=pltpu.Pre...  5.61 us
    all_to_all x1, starting transfers between devices, local(): lax.all_to_all(message, ('expert', 'batch'), split_axis=0, concat_axis=0,...  3.72 us
    pallas_call x1, Pallas kernels, gate_up(): pl.pallas_call(functools.partial(gate_up_body, batches), grid_spec=pltpu....  3.64 us
    pallas_call x4, Pallas kernels, call(): pl.pallas_call(body, out_shape=shapes, in_specs=specs, out_specs=jax.tree...  3.35 us
  transfers between devices with their start and end apart: 41, of which 19 were waited for; matrix products, arithmetic and copies ran while one was open for 0% of the time, Pallas kernels for 5%

profile of v1, /device:TPU:0, one launch (start us, length us, event | category | flops | bytes accessed | tf_op | source)
XLA Modules:
  0.0 97.9 jit_solution(1673505543932941510)
XLA Ops:
  0.0 0.7 broadcast_in_dim.6.gain_ref
  0.7 1.0 %copy-done.2 = bf16[1,256,1024]{2,1,0:T(8,128)(2,1)S(1)} copy-done((bf16[1,256,1024]{2,1,0:T(8,128)(2,1)S(1)}, bf16[1,256,1024]{2,1,0:T(8,128)(2,1)}, u32[]{:S(2)}) %copy-start.2) | copy-done | bytes 524312
  1.7 0.9 copy-done.3
  2.7 0.4 logits.1
  3.1 5.1 %collective-permute-start.2 = (f32[136,256]{1,0:T(8,128)S(1)}, f32[136,256]{1,0:T(8,128)S(1)}, u32[]{:S(2)}, u32[]{:S(2)}) collective-permute-start(f32[136,256]{1,0:T(8,128)S(1)} %get-tuple-element.23.refs_0_), channel_id=1, source_target_pairs={{0,3},{1,2},{2,1},{3,0},{4,7},{5,6},{6,5},{7,4},{8,11},{9,10},{10,... | collective-permute-start | bytes 417800 | tf_op jit(solution)/shard_map/ppermute | solution.py:34
  8.2 0.6 collective-permute-start
  8.8 4.0 %collective-permute-done.2.refs_3_ = f32[136,256]{1,0:T(8,128)S(1)} collective-permute-done((f32[136,256]{1,0:T(8,128)S(1)}, f32[136,256]{1,0:T(8,128)S(1)}, u32[]{:S(2)}, u32[]{:S(2)}) %collective-permute-start.2) | collective-permute-done | bytes 139296 | tf_op jit(solution)/shard_map/ppermute | solution.py:34
  12.8 7.2 %collective-permute-done.1.refs_2_ = f32[136,256]{1,0:T(8,128)S(1)} collective-permute-done((f32[136,256]{1,0:T(8,128)S(1)}, f32[136,256]{1,0:T(8,128)S(1)}, u32[]{:S(2)}, u32[]{:S(2)}) %collective-permute-start.1) | collective-permute-done | bytes 139296 | tf_op jit(solution)/shard_map/ppermute | solution.py:34
  20.0 1.1 %slots.1 = bf16[8,16,1152]{2,1,0:T(8,128)(2,1)} custom-call(f32[136,256]{1,0:T(8,128)S(1)} %get-tuple-element.23.refs_0_, f32[136,256]{1,0:T(8,128)S(1)} %collective-permute-done.refs_1_, f32[136,256]{1,0:T(8,128)S(1)} %collective-permute-done.1.refs_2_, f32[136,256]{1,0:T(8,128)S(1)} %collective-permute-done.2.refs_3_, ...), custom_call_target="tpu_custom_call" | custom-call | flops 1073741824 | bytes 4194304 | tf_op jit(solution)/shard_map/slots/pallas_call | solution.py:17
  21.1 3.7 %all-to-all-start = ((bf16[8,16,1152]{2,1,0:T(8,128)(2,1)}), bf16[8,16,1152]{2,1,0:T(8,128)(2,1)S(1)}, u32[]{:S(2)}, u32[]{:S(2)}) async-start(bf16[8,16,1152]{2,1,0:T(8,128)(2,1)} %slots.1), calls=%async_computation | async-start | bytes 589824 | tf_op jit(solution)/shard_map/all_to_all | solution.py:236
  24.9 6.3 %all-to-all-done.message_ref = bf16[8,16,1152]{2,1,0:T(8,128)(2,1)S(1)} async-done(((bf16[8,16,1152]{2,1,0:T(8,128)(2,1)}), bf16[8,16,1152]{2,1,0:T(8,128)(2,1)S(1)}, u32[]{:S(2)}, u32[]{:S(2)}) %all-to-all-start) | async-done | bytes 294944 | tf_op jit(solution)/shard_map/all_to_all | solution.py:236
  31.2 0.8 gather.1.refs_0_
  32.0 2.6 %collective-permute-start.14 = (bf16[32,1024]{1,0:T(8,128)(2,1)S(1)}, bf16[32,1024]{1,0:T(8,128)(2,1)S(1)}, u32[]{:S(2)}, u32[]{:S(2)}) collective-permute-start(bf16[32,1024]{1,0:T(8,128)(2,1)S(1)} %gather.1.refs_0_), channel_id=1, source_target_pairs={{0,3},{1,2},{2,1},{3,0},{4,7},{5,6},{6,5},{7,4},{8,11},{9,10},{10,... | collective-permute-start | bytes 196616 | tf_op jit(solution)/shard_map/ppermute | solution.py:34
  34.6 1.9 %collective-permute-start.6 = (bf16[32,1024]{1,0:T(8,128)(2,1)S(1)}, bf16[32,1024]{1,0:T(8,128)(2,1)S(1)}, u32[]{:S(2)}, u32[]{:S(2)}) collective-permute-start(bf16[32,1024]{1,0:T(8,128)(2,1)S(1)} %gather.1.refs_0_), channel_id=1, source_target_pairs={{0,1},{1,0},{2,3},{3,2},{4,5},{5,4},{6,7},{7,6},{8,9},{9,8},{10,11... | collective-permute-start | bytes 196616 | tf_op jit(solution)/shard_map/ppermute | solution.py:34
  36.5 1.5 %collective-permute-start.4 = (bf16[32,1024]{1,0:T(8,128)(2,1)S(1)}, bf16[32,1024]{1,0:T(8,128)(2,1)S(1)}, u32[]{:S(2)}, u32[]{:S(2)}) collective-permute-start(bf16[32,1024]{1,0:T(8,128)(2,1)S(1)} %gather.1.refs_0_), channel_id=1, source_target_pairs={{0,16},{8,24},{16,0},{24,8},{1,17},{9,25},{17,1},{25,9},{2,18},{10... | collective-permute-start | bytes 196616 | tf_op jit(solution)/shard_map/ppermute | solution.py:34
  37.9 0.5 collective-permute-done.14.refs_12_
  38.4 1.2 %collective-permute-start.16 = (bf16[32,1024]{1,0:T(8,128)(2,1)S(1)}, bf16[32,1024]{1,0:T(8,128)(2,1)S(1)}, u32[]{:S(2)}, u32[]{:S(2)}) collective-permute-start(bf16[32,1024]{1,0:T(8,128)(2,1)S(1)} %collective-permute-done.14.refs_12_), channel_id=1, source_target_pairs={{0,16},{8,24},{16,0},{24,8},{1,17},{9,25},{17,1},{25,9},{2,18},{10... | collective-permute-start | bytes 196616 | tf_op jit(solution)/shard_map/ppermute | solution.py:34
  39.6 0.8 collective-permute-done.10.refs_8_
  40.4 1.2 %collective-permute-start.12 = (bf16[32,1024]{1,0:T(8,128)(2,1)S(1)}, bf16[32,1024]{1,0:T(8,128)(2,1)S(1)}, u32[]{:S(2)}, u32[]{:S(2)}) collective-permute-start(bf16[32,1024]{1,0:T(8,128)(2,1)S(1)} %collective-permute-done.10.refs_8_), channel_id=1, source_target_pairs={{0,16},{8,24},{16,0},{24,8},{1,17},{9,25},{17,1},{25,9},{2,18},{10... | collective-permute-start | bytes 196616 | tf_op jit(solution)/shard_map/ppermute | solution.py:34
  41.6 0.2 collective-permute-start.11
  41.8 1.0 %collective-permute-start.8 = (bf16[32,1024]{1,0:T(8,128)(2,1)S(1)}, bf16[32,1024]{1,0:T(8,128)(2,1)S(1)}, u32[]{:S(2)}, u32[]{:S(2)}) collective-permute-start(bf16[32,1024]{1,0:T(8,128)(2,1)S(1)} %collective-permute-done.6.refs_4_), channel_id=1, source_target_pairs={{0,16},{8,24},{16,0},{24,8},{1,17},{9,25},{17,1},{25,9},{2,18},{10... | collective-permute-start | bytes 196616 | tf_op jit(solution)/shard_map/ppermute | solution.py:34
  42.8 0.2 collective-permute-start.7
  43.0 0.3 collective-permute-start.5
  43.3 1.8 %collective-permute-done.12.refs_10_ = bf16[32,1024]{1,0:T(8,128)(2,1)S(1)} collective-permute-done((bf16[32,1024]{1,0:T(8,128)(2,1)S(1)}, bf16[32,1024]{1,0:T(8,128)(2,1)S(1)}, u32[]{:S(2)}, u32[]{:S(2)}) %collective-permute-start.12) | collective-permute-done | bytes 65568 | tf_op jit(solution)/shard_map/ppermute | solution.py:34
  45.1 0.5 collective-permute-start.13
  45.7 0.7 collective-permute-done.8.refs_6_
  46.6 1.0 %collective-permute-done.9.refs_7_ = bf16[32,1024]{1,0:T(8,128)(2,1)S(1)} collective-permute-done((bf16[32,1024]{1,0:T(8,128)(2,1)S(1)}, bf16[32,1024]{1,0:T(8,128)(2,1)S(1)}, u32[]{:S(2)}, u32[]{:S(2)}) %collective-permute-start.9) | collective-permute-done | bytes 65568 | tf_op jit(solution)/shard_map/ppermute | solution.py:34
  47.6 3.1 %copy-done = bf16[1,4096,896]{2,1,0:T(8,128)(2,1)S(1)} copy-done((bf16[1,4096,896]{2,1,0:T(8,128)(2,1)S(1)}, bf16[1,4096,896]{2,1,0:T(8,128)(2,1)}, u32[]{:S(2)}) %copy-start) | copy-done | bytes 7340056
  50.7 3.1 %copy-done.1 = bf16[1,4096,896]{2,1,0:T(8,128)(2,1)S(1)} copy-done((bf16[1,4096,896]{2,1,0:T(8,128)(2,1)S(1)}, bf16[1,4096,896]{2,1,0:T(8,128)(2,1)}, u32[]{:S(2)}) %copy-start.1) | copy-done | bytes 7340056
  53.8 3.6 %gate_up.1.hidden_ref = bf16[128,896]{1,0:T(8,128)(2,1)S(1)} custom-call(s32[3]{0:T(128)S(1)} %pad_add_fusion.where_ref, bf16[32,1024]{1,0:T(8,128)(2,1)S(1)} %gather.1.refs_0_, bf16[32,1024]{1,0:T(8,128)(2,1)S(1)} %collective-permute-done.3.refs_1_, bf16[32,1024]{1,0:T(8,128)(2,1)S(1)} %collective-permute-done.4.refs_2_, ...), custom_call_target="tpu_custom_call" | custom-call | flops 1879048192 | bytes 14680064 | tf_op jit(solution)/shard_map/gate_up/pallas_call | solution.py:139
  57.4 1.4 %down.7 = (bf16[32,1024]{1,0:T(8,128)(2,1)S(1)}, bf16[32,1024]{1,0:T(8,128)(2,1)S(1)}, bf16[32,1024]{1,0:T(8,128)(2,1)S(1)}, bf16[32,1024]{1,0:T(8,128)(2,1)S(1)}) custom-call(s32[3]{0:T(128)S(1)} %pad_add_fusion.where_ref, bf16[128,896]{1,0:T(8,128)(2,1)S(1)} %gate_up.1.hidden_ref, bf16[1,896,4096]{2,1,0:T(8,128)(2,1)S(1)} %bitcast.6), custom_call_target="tpu_custom_call" | custom-call | flops 234881024 | bytes 1835008 | tf_op jit(solution)/shard_map/down/pallas_call | solution.py:169
  58.8 0.2 collective-permute-start.30
  59.1 0.3 collective-permute-start.31
  59.4 1.4 %down.6 = (bf16[32,1024]{1,0:T(8,128)(2,1)S(1)}, bf16[32,1024]{1,0:T(8,128)(2,1)S(1)}, bf16[32,1024]{1,0:T(8,128)(2,1)S(1)}, bf16[32,1024]{1,0:T(8,128)(2,1)S(1)}) custom-call(s32[3]{0:T(128)S(1)} %pad_add_fusion.where_ref, bf16[128,896]{1,0:T(8,128)(2,1)S(1)} %gate_up.1.hidden_ref, bf16[1,896,4096]{2,1,0:T(8,128)(2,1)S(1)} %bitcast.6), custom_call_target="tpu_custom_call" | custom-call | flops 234881024 | bytes 1835008 | tf_op jit(solution)/shard_map/down/pallas_call | solution.py:169
  61.1 0.3 collective-permute-start.27
  61.4 1.4 %down.4 = (bf16[32,1024]{1,0:T(8,128)(2,1)S(1)}, bf16[32,1024]{1,0:T(8,128)(2,1)S(1)}, bf16[32,1024]{1,0:T(8,128)(2,1)S(1)}, bf16[32,1024]{1,0:T(8,128)(2,1)S(1)}) custom-call(s32[3]{0:T(128)S(1)} %pad_add_fusion.where_ref, bf16[128,896]{1,0:T(8,128)(2,1)S(1)} %gate_up.1.hidden_ref, bf16[1,896,4096]{2,1,0:T(8,128)(2,1)S(1)} %bitcast.6), custom_call_target="tpu_custom_call" | custom-call | flops 234881024 | bytes 1835008 | tf_op jit(solution)/shard_map/down/pallas_call | solution.py:169
  62.8 0.2 collective-permute-start.18
  63.0 1.4 %down.5 = (bf16[32,1024]{1,0:T(8,128)(2,1)S(1)}, bf16[32,1024]{1,0:T(8,128)(2,1)S(1)}, bf16[32,1024]{1,0:T(8,128)(2,1)S(1)}, bf16[32,1024]{1,0:T(8,128)(2,1)S(1)}) custom-call(s32[3]{0:T(128)S(1)} %pad_add_fusion.where_ref, bf16[128,896]{1,0:T(8,128)(2,1)S(1)} %gate_up.1.hidden_ref, bf16[1,896,4096]{2,1,0:T(8,128)(2,1)S(1)} %bitcast.6), custom_call_target="tpu_custom_call" | custom-call | flops 234881024 | bytes 1835008 | tf_op jit(solution)/shard_map/down/pallas_call | solution.py:169
  64.5 0.4 collective-permute-start.19
  64.9 0.2 collective-permute-start.22
  65.2 0.6 collective-permute-done.19
  65.8 0.3 collective-permute-start.23
  66.1 0.9 collective-permute-done.23
  67.0 1.2 %collective-permute-start.28 = (bf16[32,1024]{1,0:T(8,128)(2,1)S(1)}, bf16[32,1024]{1,0:T(8,128)(2,1)S(1)}, u32[]{:S(2)}, u32[]{:S(2)}) collective-permute-start(bf16[32,1024]{1,0:T(8,128)(2,1)S(1)} %add_convert_fusion.4), channel_id=1, source_target_pairs={{0,16},{8,24},{16,0},{24,8},{1,17},{9,25},{17,1},{25,9},{2,18},{10... | collective-permute-start | bytes 196616 | tf_op jit(solution)/shard_map/ppermute | solution.py:34
  68.2 0.9 collective-permute-start.32
  69.2 2.6 %collective-permute-done.28 = bf16[32,1024]{1,0:T(8,128)(2,1)S(1)} collective-permute-done((bf16[32,1024]{1,0:T(8,128)(2,1)S(1)}, bf16[32,1024]{1,0:T(8,128)(2,1)S(1)}, u32[]{:S(2)}, u32[]{:S(2)}) %collective-permute-start.28) | collective-permute-done | bytes 65568 | tf_op jit(solution)/shard_map/ppermute | solution.py:34
  71.8 1.4 %collective-permute-start.20 = (bf16[32,1024]{1,0:T(8,128)(2,1)S(1)}, bf16[32,1024]{1,0:T(8,128)(2,1)S(1)}, u32[]{:S(2)}, u32[]{:S(2)}) collective-permute-start(bf16[32,1024]{1,0:T(8,128)(2,1)S(1)} %add_convert_fusion.10), channel_id=1, source_target_pairs={{0,16},{8,24},{16,0},{24,8},{1,17},{9,25},{17,1},{25,9},{2,18},{10... | collective-permute-start | bytes 196616 | tf_op jit(solution)/shard_map/ppermute | solution.py:34
  73.2 0.7 collective-permute-start.24
  73.9 2.1 %collective-permute-done.20 = bf16[32,1024]{1,0:T(8,128)(2,1)S(1)} collective-permute-done((bf16[32,1024]{1,0:T(8,128)(2,1)S(1)}, bf16[32,1024]{1,0:T(8,128)(2,1)S(1)}, u32[]{:S(2)}, u32[]{:S(2)}) %collective-permute-start.20) | collective-permute-done | bytes 65568 | tf_op jit(solution)/shard_map/ppermute | solution.py:34
  76.0 0.5 collective-permute-start.29
  76.6 2.5 %collective-permute-start.21 = (bf16[16,1024]{1,0:T(8,128)(2,1)S(1)}, bf16[16,1024]{1,0:T(8,128)(2,1)S(1)}, u32[]{:S(2)}, u32[]{:S(2)}) collective-permute-start(bf16[16,1024]{1,0:T(8,128)(2,1)S(1)} %get-tuple-element.41), channel_id=1, source_target_pairs={{0,3},{1,2},{2,1},{3,0},{4,7},{5,6},{6,5},{7,4},{8,11},{9,10},{10,... | collective-permute-start | bytes 98312 | tf_op jit(solution)/shard_map/ppermute | solution.py:34
  79.1 0.6 collective-permute-start.25
  79.8 1.6 %collective-permute-start.36 = (bf16[16,1024]{1,0:T(8,128)(2,1)S(1)}, bf16[16,1024]{1,0:T(8,128)(2,1)S(1)}, u32[]{:S(2)}, u32[]{:S(2)}) collective-permute-start(bf16[16,1024]{1,0:T(8,128)(2,1)S(1)} %slice.39), channel_id=1, source_target_pairs={{0,4},{1,5},{2,6},{3,7},{4,0},{5,1},{6,2},{7,3},{8,12},{9,13},{10,... | collective-permute-start | bytes 98312 | tf_op jit(solution)/shard_map/ppermute | solution.py:34
  81.4 1.3 %collective-permute-start.35 = (bf16[16,1024]{1,0:T(8,128)(2,1)S(1)}, bf16[16,1024]{1,0:T(8,128)(2,1)S(1)}, u32[]{:S(2)}, u32[]{:S(2)}) collective-permute-start(bf16[16,1024]{1,0:T(8,128)(2,1)S(1)} %get-tuple-element.46), channel_id=1, source_target_pairs={{0,5},{1,4},{2,7},{3,6},{4,1},{5,0},{6,3},{7,2},{8,13},{9,12},{10,... | collective-permute-start | bytes 98312 | tf_op jit(solution)/shard_map/ppermute | solution.py:34
  82.8 3.2 %collective-permute-start.33 = (bf16[16,1024]{1,0:T(8,128)(2,1)S(1)}, bf16[16,1024]{1,0:T(8,128)(2,1)S(1)}, u32[]{:S(2)}, u32[]{:S(2)}) collective-permute-start(bf16[16,1024]{1,0:T(8,128)(2,1)S(1)} %get-tuple-element.42), channel_id=1, source_target_pairs={{0,7},{1,6},{2,5},{3,4},{4,3},{5,2},{6,1},{7,0},{8,15},{9,14},{10,... | collective-permute-start | bytes 98312 | tf_op jit(solution)/shard_map/ppermute | solution.py:34
  86.0 0.3 collective-permute-done.35
  86.3 3.1 %collective-permute-done.33 = bf16[16,1024]{1,0:T(8,128)(2,1)S(1)} collective-permute-done((bf16[16,1024]{1,0:T(8,128)(2,1)S(1)}, bf16[16,1024]{1,0:T(8,128)(2,1)S(1)}, u32[]{:S(2)}, u32[]{:S(2)}) %collective-permute-start.33) | collective-permute-done | bytes 32800 | tf_op jit(solution)/shard_map/ppermute | solution.py:34
  89.4 2.3 %collective-permute-done.34 = bf16[16,1024]{1,0:T(8,128)(2,1)S(1)} collective-permute-done((bf16[16,1024]{1,0:T(8,128)(2,1)S(1)}, bf16[16,1024]{1,0:T(8,128)(2,1)S(1)}, u32[]{:S(2)}, u32[]{:S(2)}) %collective-permute-start.34) | collective-permute-done | bytes 32800 | tf_op jit(solution)/shard_map/ppermute | solution.py:34
  91.7 0.7 collective-permute-start.38
  92.5 1.1 %collective-permute-start.37 = (bf16[32,1024]{1,0:T(8,128)(2,1)S(1)}, bf16[32,1024]{1,0:T(8,128)(2,1)S(1)}, u32[]{:S(2)}, u32[]{:S(2)}) collective-permute-start(bf16[32,1024]{1,0:T(8,128)(2,1)S(1)} %pad_maximum_fusion.refs_0_), channel_id=1, source_target_pairs={{0,8},{8,0},{16,24},{24,16},{1,9},{9,1},{17,25},{25,17},{2,10},{10... | collective-permute-start | bytes 196616 | tf_op jit(solution)/shard_map/ppermute | solution.py:34
  93.6 0.7 combine.1.combine_ref
  94.3 1.1 %collective-permute-done.39.refs_3_ = bf16[32,1024]{1,0:T(8,128)(2,1)S(1)} collective-permute-done((bf16[32,1024]{1,0:T(8,128)(2,1)S(1)}, bf16[32,1024]{1,0:T(8,128)(2,1)S(1)}, u32[]{:S(2)}, u32[]{:S(2)}) %collective-permute-start.39) | collective-permute-done | bytes 65568 | tf_op jit(solution)/shard_map/ppermute | solution.py:34
  95.5 1.3 %collective-permute-done.38.refs_2_ = bf16[32,1024]{1,0:T(8,128)(2,1)S(1)} collective-permute-done((bf16[32,1024]{1,0:T(8,128)(2,1)S(1)}, bf16[32,1024]{1,0:T(8,128)(2,1)S(1)}, u32[]{:S(2)}, u32[]{:S(2)}) %collective-permute-start.38) | collective-permute-done | bytes 65568 | tf_op jit(solution)/shard_map/ppermute | solution.py:34
  96.8 1.1 %output.1 = bf16[256,1024]{1,0:T(8,128)(2,1)} custom-call(bf16[256,128]{1,0:T(8,128)(2,1)S(1)} %combine.1.combine_ref, bf16[32,1024]{1,0:T(8,128)(2,1)S(1)} %pad_maximum_fusion.refs_0_, bf16[32,1024]{1,0:T(8,128)(2,1)S(1)} %collective-permute-done.37.refs_1_, bf16[32,1024]{1,0:T(8,128)(2,1)S(1)} %collective-permute-done.38.refs_2_, ...), custom_call_target="tpu_custom_call" | custom-call | flops 1073741824 | bytes 4194304 | tf_op jit(solution)/shard_map/output/pallas_call | solution.py:17
  (58 shorter events, 0.9 us)
Async XLA Ops:
  0.7 1.0 %copy-start.2 = (bf16[1,256,1024]{2,1,0:T(8,128)(2,1)S(1)}, bf16[1,256,1024]{2,1,0:T(8,128)(2,1)}, u32[]{:S(2)}) copy-start(bf16[1,256,1024]{2,1,0:T(8,128)(2,1)} %param.6) | copy-start | bytes 1572868
  1.7 0.9 copy-start.3
  3.1 9.8 %collective-permute-start.2 = (f32[136,256]{1,0:T(8,128)S(1)}, f32[136,256]{1,0:T(8,128)S(1)}, u32[]{:S(2)}, u32[]{:S(2)}) collective-permute-start(f32[136,256]{1,0:T(8,128)S(1)} %get-tuple-element.23.refs_0_), channel_id=1, source_target_pairs={{0,3},{1,2},{2,1},{3,0},{4,7},{5,6},{6,5},{7,4},{8,11},{9,10},{10,... | collective-permute-start | bytes 417800 | tf_op jit(solution)/shard_map/ppermute | solution.py:34
  8.2 11.8 %collective-permute-start.1 = (f32[136,256]{1,0:T(8,128)S(1)}, f32[136,256]{1,0:T(8,128)S(1)}, u32[]{:S(2)}, u32[]{:S(2)}) collective-permute-start(f32[136,256]{1,0:T(8,128)S(1)} %get-tuple-element.23.refs_0_), channel_id=1, source_target_pairs={{0,2},{1,3},{2,0},{3,1},{4,6},{5,7},{6,4},{7,5},{8,10},{9,11},{10,... | collective-permute-start | bytes 417800 | tf_op jit(solution)/shard_map/ppermute | solution.py:34
  8.2 11.8 %collective-permute-start = (f32[136,256]{1,0:T(8,128)S(1)}, f32[136,256]{1,0:T(8,128)S(1)}, u32[]{:S(2)}, u32[]{:S(2)}) collective-permute-start(f32[136,256]{1,0:T(8,128)S(1)} %get-tuple-element.23.refs_0_), channel_id=1, source_target_pairs={{0,1},{1,0},{2,3},{3,2},{4,5},{5,4},{6,7},{7,6},{8,9},{9,8},{10,11... | collective-permute-start | bytes 417800 | tf_op jit(solution)/shard_map/ppermute | solution.py:34
  21.1 10.1 %all-to-all-start = ((bf16[8,16,1152]{2,1,0:T(8,128)(2,1)}), bf16[8,16,1152]{2,1,0:T(8,128)(2,1)S(1)}, u32[]{:S(2)}, u32[]{:S(2)}) async-start(bf16[8,16,1152]{2,1,0:T(8,128)(2,1)} %slots.1), calls=%async_computation | async-start | bytes 589824 | tf_op jit(solution)/shard_map/all_to_all | solution.py:236
  31.2 26.2 %slice-start = ((s8[7340032]{0:T(1024)(128)(4,1)}), s8[4194304]{0:T(1024)(128)(4,1)S(1)}, s32[]{:S(2)}) async-start(s8[7340032]{0:T(1024)(128)(4,1)} %bitcast.5), calls=%async_computation.1 | async-start | bytes 8388608
  32.0 25.4 %slice-start.1 = ((s8[7340032]{0:T(1024)(128)(4,1)}), s8[3145728]{0:T(1024)(128)(4,1)S(1)}, s32[]{:S(2)}) async-start(s8[7340032]{0:T(1024)(128)(4,1)} %bitcast.5), calls=%async_computation.2 | async-start | bytes 6291456
  32.0 6.4 %collective-permute-start.14 = (bf16[32,1024]{1,0:T(8,128)(2,1)S(1)}, bf16[32,1024]{1,0:T(8,128)(2,1)S(1)}, u32[]{:S(2)}, u32[]{:S(2)}) collective-permute-start(bf16[32,1024]{1,0:T(8,128)(2,1)S(1)} %gather.1.refs_0_), channel_id=1, source_target_pairs={{0,3},{1,2},{2,1},{3,0},{4,7},{5,6},{6,5},{7,4},{8,11},{9,10},{10,... | collective-permute-start | bytes 196616 | tf_op jit(solution)/shard_map/ppermute | solution.py:34
  34.6 5.8 %collective-permute-start.10 = (bf16[32,1024]{1,0:T(8,128)(2,1)S(1)}, bf16[32,1024]{1,0:T(8,128)(2,1)S(1)}, u32[]{:S(2)}, u32[]{:S(2)}) collective-permute-start(bf16[32,1024]{1,0:T(8,128)(2,1)S(1)} %gather.1.refs_0_), channel_id=1, source_target_pairs={{0,2},{1,3},{2,0},{3,1},{4,6},{5,7},{6,4},{7,5},{8,10},{9,11},{10,... | collective-permute-start | bytes 196616 | tf_op jit(solution)/shard_map/ppermute | solution.py:34
  34.6 5.8 %collective-permute-start.6 = (bf16[32,1024]{1,0:T(8,128)(2,1)S(1)}, bf16[32,1024]{1,0:T(8,128)(2,1)S(1)}, u32[]{:S(2)}, u32[]{:S(2)}) collective-permute-start(bf16[32,1024]{1,0:T(8,128)(2,1)S(1)} %gather.1.refs_0_), channel_id=1, source_target_pairs={{0,1},{1,0},{2,3},{3,2},{4,5},{5,4},{6,7},{7,6},{8,9},{9,8},{10,11... | collective-permute-start | bytes 196616 | tf_op jit(solution)/shard_map/ppermute | solution.py:34
  36.5 5.1 %collective-permute-start.4 = (bf16[32,1024]{1,0:T(8,128)(2,1)S(1)}, bf16[32,1024]{1,0:T(8,128)(2,1)S(1)}, u32[]{:S(2)}, u32[]{:S(2)}) collective-permute-start(bf16[32,1024]{1,0:T(8,128)(2,1)S(1)} %gather.1.refs_0_), channel_id=1, source_target_pairs={{0,16},{8,24},{16,0},{24,8},{1,17},{9,25},{17,1},{25,9},{2,18},{10... | collective-permute-start | bytes 196616 | tf_op jit(solution)/shard_map/ppermute | solution.py:34
  37.9 3.9 %collective-permute-start.3 = (bf16[32,1024]{1,0:T(8,128)(2,1)S(1)}, bf16[32,1024]{1,0:T(8,128)(2,1)S(1)}, u32[]{:S(2)}, u32[]{:S(2)}) collective-permute-start(bf16[32,1024]{1,0:T(8,128)(2,1)S(1)} %gather.1.refs_0_), channel_id=1, source_target_pairs={{0,8},{8,0},{16,24},{24,16},{1,9},{9,1},{17,25},{25,17},{2,10},{10... | collective-permute-start | bytes 196616 | tf_op jit(solution)/shard_map/ppermute | solution.py:34
  38.4 4.4 %collective-permute-start.16 = (bf16[32,1024]{1,0:T(8,128)(2,1)S(1)}, bf16[32,1024]{1,0:T(8,128)(2,1)S(1)}, u32[]{:S(2)}, u32[]{:S(2)}) collective-permute-start(bf16[32,1024]{1,0:T(8,128)(2,1)S(1)} %collective-permute-done.14.refs_12_), channel_id=1, source_target_pairs={{0,16},{8,24},{16,0},{24,8},{1,17},{9,25},{17,1},{25,9},{2,18},{10... | collective-permute-start | bytes 196616 | tf_op jit(solution)/shard_map/ppermute | solution.py:34
  40.4 2.6 %collective-permute-start.15 = (bf16[32,1024]{1,0:T(8,128)(2,1)S(1)}, bf16[32,1024]{1,0:T(8,128)(2,1)S(1)}, u32[]{:S(2)}, u32[]{:S(2)}) collective-permute-start(bf16[32,1024]{1,0:T(8,128)(2,1)S(1)} %collective-permute-done.14.refs_12_), channel_id=1, source_target_pairs={{0,8},{8,0},{16,24},{24,16},{1,9},{9,1},{17,25},{25,17},{2,10},{10... | collective-permute-start | bytes 196616 | tf_op jit(solution)/shard_map/ppermute | solution.py:34
  40.4 4.7 %collective-permute-start.12 = (bf16[32,1024]{1,0:T(8,128)(2,1)S(1)}, bf16[32,1024]{1,0:T(8,128)(2,1)S(1)}, u32[]{:S(2)}, u32[]{:S(2)}) collective-permute-start(bf16[32,1024]{1,0:T(8,128)(2,1)S(1)} %collective-permute-done.10.refs_8_), channel_id=1, source_target_pairs={{0,16},{8,24},{16,0},{24,8},{1,17},{9,25},{17,1},{25,9},{2,18},{10... | collective-permute-start | bytes 196616 | tf_op jit(solution)/shard_map/ppermute | solution.py:34
  41.6 3.5 %collective-permute-start.11 = (bf16[32,1024]{1,0:T(8,128)(2,1)S(1)}, bf16[32,1024]{1,0:T(8,128)(2,1)S(1)}, u32[]{:S(2)}, u32[]{:S(2)}) collective-permute-start(bf16[32,1024]{1,0:T(8,128)(2,1)S(1)} %collective-permute-done.10.refs_8_), channel_id=1, source_target_pairs={{0,8},{8,0},{16,24},{24,16},{1,9},{9,1},{17,25},{25,17},{2,10},{10... | collective-permute-start | bytes 196616 | tf_op jit(solution)/shard_map/ppermute | solution.py:34
  41.8 4.5 %collective-permute-start.8 = (bf16[32,1024]{1,0:T(8,128)(2,1)S(1)}, bf16[32,1024]{1,0:T(8,128)(2,1)S(1)}, u32[]{:S(2)}, u32[]{:S(2)}) collective-permute-start(bf16[32,1024]{1,0:T(8,128)(2,1)S(1)} %collective-permute-done.6.refs_4_), channel_id=1, source_target_pairs={{0,16},{8,24},{16,0},{24,8},{1,17},{9,25},{17,1},{25,9},{2,18},{10... | collective-permute-start | bytes 196616 | tf_op jit(solution)/shard_map/ppermute | solution.py:34
  42.8 3.5 %collective-permute-start.7 = (bf16[32,1024]{1,0:T(8,128)(2,1)S(1)}, bf16[32,1024]{1,0:T(8,128)(2,1)S(1)}, u32[]{:S(2)}, u32[]{:S(2)}) collective-permute-start(bf16[32,1024]{1,0:T(8,128)(2,1)S(1)} %collective-permute-done.6.refs_4_), channel_id=1, source_target_pairs={{0,8},{8,0},{16,24},{24,16},{1,9},{9,1},{17,25},{25,17},{2,10},{10... | collective-permute-start | bytes 196616 | tf_op jit(solution)/shard_map/ppermute | solution.py:34
  43.0 3.3 %collective-permute-start.5 = (bf16[32,1024]{1,0:T(8,128)(2,1)S(1)}, bf16[32,1024]{1,0:T(8,128)(2,1)S(1)}, u32[]{:S(2)}, u32[]{:S(2)}) collective-permute-start(bf16[32,1024]{1,0:T(8,128)(2,1)S(1)} %collective-permute-done.4.refs_2_), channel_id=1, source_target_pairs={{0,8},{8,0},{16,24},{24,16},{1,9},{9,1},{17,25},{25,17},{2,10},{10... | collective-permute-start | bytes 196616 | tf_op jit(solution)/shard_map/ppermute | solution.py:34
  45.1 1.3 %collective-permute-start.17 = (bf16[32,1024]{1,0:T(8,128)(2,1)S(1)}, bf16[32,1024]{1,0:T(8,128)(2,1)S(1)}, u32[]{:S(2)}, u32[]{:S(2)}) collective-permute-start(bf16[32,1024]{1,0:T(8,128)(2,1)S(1)} %collective-permute-done.16.refs_14_), channel_id=1, source_target_pairs={{0,8},{8,0},{16,24},{24,16},{1,9},{9,1},{17,25},{25,17},{2,10},{10... | collective-permute-start | bytes 196616 | tf_op jit(solution)/shard_map/ppermute | solution.py:34
  45.1 1.4 %collective-permute-start.13 = (bf16[32,1024]{1,0:T(8,128)(2,1)S(1)}, bf16[32,1024]{1,0:T(8,128)(2,1)S(1)}, u32[]{:S(2)}, u32[]{:S(2)}) collective-permute-start(bf16[32,1024]{1,0:T(8,128)(2,1)S(1)} %collective-permute-done.12.refs_10_), channel_id=1, source_target_pairs={{0,8},{8,0},{16,24},{24,16},{1,9},{9,1},{17,25},{25,17},{2,10},{10... | collective-permute-start | bytes 196616 | tf_op jit(solution)/shard_map/ppermute | solution.py:34
  46.3 1.3 %collective-permute-start.9 = (bf16[32,1024]{1,0:T(8,128)(2,1)S(1)}, bf16[32,1024]{1,0:T(8,128)(2,1)S(1)}, u32[]{:S(2)}, u32[]{:S(2)}) collective-permute-start(bf16[32,1024]{1,0:T(8,128)(2,1)S(1)} %collective-permute-done.8.refs_6_), channel_id=1, source_target_pairs={{0,8},{8,0},{16,24},{24,16},{1,9},{9,1},{17,25},{25,17},{2,10},{10... | collective-permute-start | bytes 196616 | tf_op jit(solution)/shard_map/ppermute | solution.py:34
  47.6 3.1 %copy-start = (bf16[1,4096,896]{2,1,0:T(8,128)(2,1)S(1)}, bf16[1,4096,896]{2,1,0:T(8,128)(2,1)}, u32[]{:S(2)}) copy-start(bf16[1,4096,896]{2,1,0:T(8,128)(2,1)} %refs_16_.1) | copy-start | bytes 22020100
  50.7 3.1 %copy-start.1 = (bf16[1,4096,896]{2,1,0:T(8,128)(2,1)S(1)}, bf16[1,4096,896]{2,1,0:T(8,128)(2,1)}, u32[]{:S(2)}) copy-start(bf16[1,4096,896]{2,1,0:T(8,128)(2,1)} %refs_17_.1) | copy-start | bytes 22020100
  58.8 20.9 %collective-permute-start.30 = (bf16[32,1024]{1,0:T(8,128)(2,1)S(1)}, bf16[32,1024]{1,0:T(8,128)(2,1)S(1)}, u32[]{:S(2)}, u32[]{:S(2)}) collective-permute-start(bf16[32,1024]{1,0:T(8,128)(2,1)S(1)} %get-tuple-element.38), channel_id=1, source_target_pairs={{0,8},{8,0},{16,24},{24,16},{1,9},{9,1},{17,25},{25,17},{2,10},{10... | collective-permute-start | bytes 196616 | tf_op jit(solution)/shard_map/ppermute | solution.py:34
  59.1 5.4 %collective-permute-start.31 = (bf16[32,1024]{1,0:T(8,128)(2,1)S(1)}, bf16[32,1024]{1,0:T(8,128)(2,1)S(1)}, u32[]{:S(2)}, u32[]{:S(2)}) collective-permute-start(bf16[32,1024]{1,0:T(8,128)(2,1)S(1)} %get-tuple-element.40), channel_id=1, source_target_pairs={{0,8},{8,0},{16,24},{24,16},{1,9},{9,1},{17,25},{25,17},{2,10},{10... | collective-permute-start | bytes 196616 | tf_op jit(solution)/shard_map/ppermute | solution.py:34
  60.8 7.4 %collective-permute-start.26 = (bf16[32,1024]{1,0:T(8,128)(2,1)S(1)}, bf16[32,1024]{1,0:T(8,128)(2,1)S(1)}, u32[]{:S(2)}, u32[]{:S(2)}) collective-permute-start(bf16[32,1024]{1,0:T(8,128)(2,1)S(1)} %get-tuple-element.34), channel_id=1, source_target_pairs={{0,8},{8,0},{16,24},{24,16},{1,9},{9,1},{17,25},{25,17},{2,10},{10... | collective-permute-start | bytes 196616 | tf_op jit(solution)/shard_map/ppermute | solution.py:34
  61.1 3.8 %collective-permute-start.27 = (bf16[32,1024]{1,0:T(8,128)(2,1)S(1)}, bf16[32,1024]{1,0:T(8,128)(2,1)S(1)}, u32[]{:S(2)}, u32[]{:S(2)}) collective-permute-start(bf16[32,1024]{1,0:T(8,128)(2,1)S(1)} %get-tuple-element.36), channel_id=1, source_target_pairs={{0,8},{8,0},{16,24},{24,16},{1,9},{9,1},{17,25},{25,17},{2,10},{10... | collective-permute-start | bytes 196616 | tf_op jit(solution)/shard_map/ppermute | solution.py:34
  62.8 10.4 %collective-permute-start.18 = (bf16[32,1024]{1,0:T(8,128)(2,1)S(1)}, bf16[32,1024]{1,0:T(8,128)(2,1)S(1)}, u32[]{:S(2)}, u32[]{:S(2)}) collective-permute-start(bf16[32,1024]{1,0:T(8,128)(2,1)S(1)} %get-tuple-element.26), channel_id=1, source_target_pairs={{0,8},{8,0},{16,24},{24,16},{1,9},{9,1},{17,25},{25,17},{2,10},{10... | collective-permute-start | bytes 196616 | tf_op jit(solution)/shard_map/ppermute | solution.py:34
  64.5 1.3 %collective-permute-start.19 = (bf16[32,1024]{1,0:T(8,128)(2,1)S(1)}, bf16[32,1024]{1,0:T(8,128)(2,1)S(1)}, u32[]{:S(2)}, u32[]{:S(2)}) collective-permute-start(bf16[32,1024]{1,0:T(8,128)(2,1)S(1)} %get-tuple-element.28), channel_id=1, source_target_pairs={{0,8},{8,0},{16,24},{24,16},{1,9},{9,1},{17,25},{25,17},{2,10},{10... | collective-permute-start | bytes 196616 | tf_op jit(solution)/shard_map/ppermute | solution.py:34
  64.9 11.7 %collective-permute-start.22 = (bf16[32,1024]{1,0:T(8,128)(2,1)S(1)}, bf16[32,1024]{1,0:T(8,128)(2,1)S(1)}, u32[]{:S(2)}, u32[]{:S(2)}) collective-permute-start(bf16[32,1024]{1,0:T(8,128)(2,1)S(1)} %get-tuple-element.30), channel_id=1, source_target_pairs={{0,8},{8,0},{16,24},{24,16},{1,9},{9,1},{17,25},{25,17},{2,10},{10... | collective-permute-start | bytes 196616 | tf_op jit(solution)/shard_map/ppermute | solution.py:34
  65.8 1.3 %collective-permute-start.23 = (bf16[32,1024]{1,0:T(8,128)(2,1)S(1)}, bf16[32,1024]{1,0:T(8,128)(2,1)S(1)}, u32[]{:S(2)}, u32[]{:S(2)}) collective-permute-start(bf16[32,1024]{1,0:T(8,128)(2,1)S(1)} %get-tuple-element.32), channel_id=1, source_target_pairs={{0,8},{8,0},{16,24},{24,16},{1,9},{9,1},{17,25},{25,17},{2,10},{10... | collective-permute-start | bytes 196616 | tf_op jit(solution)/shard_map/ppermute | solution.py:34
  67.0 4.7 %collective-permute-start.28 = (bf16[32,1024]{1,0:T(8,128)(2,1)S(1)}, bf16[32,1024]{1,0:T(8,128)(2,1)S(1)}, u32[]{:S(2)}, u32[]{:S(2)}) collective-permute-start(bf16[32,1024]{1,0:T(8,128)(2,1)S(1)} %add_convert_fusion.4), channel_id=1, source_target_pairs={{0,16},{8,24},{16,0},{24,8},{1,17},{9,25},{17,1},{25,9},{2,18},{10... | collective-permute-start | bytes 196616 | tf_op jit(solution)/shard_map/ppermute | solution.py:34
  68.2 11.5 %collective-permute-start.32 = (bf16[32,1024]{1,0:T(8,128)(2,1)S(1)}, bf16[32,1024]{1,0:T(8,128)(2,1)S(1)}, u32[]{:S(2)}, u32[]{:S(2)}) collective-permute-start(bf16[32,1024]{1,0:T(8,128)(2,1)S(1)} %add_convert_fusion.1), channel_id=1, source_target_pairs={{0,16},{8,24},{16,0},{24,8},{1,17},{9,25},{17,1},{25,9},{2,18},{10... | collective-permute-start | bytes 196616 | tf_op jit(solution)/shard_map/ppermute | solution.py:34
  71.8 4.3 %collective-permute-start.20 = (bf16[32,1024]{1,0:T(8,128)(2,1)S(1)}, bf16[32,1024]{1,0:T(8,128)(2,1)S(1)}, u32[]{:S(2)}, u32[]{:S(2)}) collective-permute-start(bf16[32,1024]{1,0:T(8,128)(2,1)S(1)} %add_convert_fusion.10), channel_id=1, source_target_pairs={{0,16},{8,24},{16,0},{24,8},{1,17},{9,25},{17,1},{25,9},{2,18},{10... | collective-permute-start | bytes 196616 | tf_op jit(solution)/shard_map/ppermute | solution.py:34
  73.2 5.9 %collective-permute-start.24 = (bf16[32,1024]{1,0:T(8,128)(2,1)S(1)}, bf16[32,1024]{1,0:T(8,128)(2,1)S(1)}, u32[]{:S(2)}, u32[]{:S(2)}) collective-permute-start(bf16[32,1024]{1,0:T(8,128)(2,1)S(1)} %add_convert_fusion.7), channel_id=1, source_target_pairs={{0,16},{8,24},{16,0},{24,8},{1,17},{9,25},{17,1},{25,9},{2,18},{10... | collective-permute-start | bytes 196616 | tf_op jit(solution)/shard_map/ppermute | solution.py:34
  76.0 6.7 %collective-permute-start.29 = (bf16[16,1024]{1,0:T(8,128)(2,1)S(1)}, bf16[16,1024]{1,0:T(8,128)(2,1)S(1)}, u32[]{:S(2)}, u32[]{:S(2)}) collective-permute-start(bf16[16,1024]{1,0:T(8,128)(2,1)S(1)} %get-tuple-element.45), channel_id=1, source_target_pairs={{0,1},{1,0},{2,3},{3,2},{4,5},{5,4},{6,7},{7,6},{8,9},{9,8},{10,11... | collective-permute-start | bytes 98312 | tf_op jit(solution)/shard_map/ppermute | solution.py:34
  76.6 9.3 %collective-permute-start.21 = (bf16[16,1024]{1,0:T(8,128)(2,1)S(1)}, bf16[16,1024]{1,0:T(8,128)(2,1)S(1)}, u32[]{:S(2)}, u32[]{:S(2)}) collective-permute-start(bf16[16,1024]{1,0:T(8,128)(2,1)S(1)} %get-tuple-element.41), channel_id=1, source_target_pairs={{0,3},{1,2},{2,1},{3,0},{4,7},{5,6},{6,5},{7,4},{8,11},{9,10},{10,... | collective-permute-start | bytes 98312 | tf_op jit(solution)/shard_map/ppermute | solution.py:34
  79.1 6.8 %collective-permute-start.25 = (bf16[16,1024]{1,0:T(8,128)(2,1)S(1)}, bf16[16,1024]{1,0:T(8,128)(2,1)S(1)}, u32[]{:S(2)}, u32[]{:S(2)}) collective-permute-start(bf16[16,1024]{1,0:T(8,128)(2,1)S(1)} %get-tuple-element.43), channel_id=1, source_target_pairs={{0,2},{1,3},{2,0},{3,1},{4,6},{5,7},{6,4},{7,5},{8,10},{9,11},{10,... | collective-permute-start | bytes 98312 | tf_op jit(solution)/shard_map/ppermute | solution.py:34
  79.8 6.1 %collective-permute-start.36 = (bf16[16,1024]{1,0:T(8,128)(2,1)S(1)}, bf16[16,1024]{1,0:T(8,128)(2,1)S(1)}, u32[]{:S(2)}, u32[]{:S(2)}) collective-permute-start(bf16[16,1024]{1,0:T(8,128)(2,1)S(1)} %slice.39), channel_id=1, source_target_pairs={{0,4},{1,5},{2,6},{3,7},{4,0},{5,1},{6,2},{7,3},{8,12},{9,13},{10,... | collective-permute-start | bytes 98312 | tf_op jit(solution)/shard_map/ppermute | solution.py:34
  81.4 4.8 %collective-permute-start.35 = (bf16[16,1024]{1,0:T(8,128)(2,1)S(1)}, bf16[16,1024]{1,0:T(8,128)(2,1)S(1)}, u32[]{:S(2)}, u32[]{:S(2)}) collective-permute-start(bf16[16,1024]{1,0:T(8,128)(2,1)S(1)} %get-tuple-element.46), channel_id=1, source_target_pairs={{0,5},{1,4},{2,7},{3,6},{4,1},{5,0},{6,3},{7,2},{8,13},{9,12},{10,... | collective-permute-start | bytes 98312 | tf_op jit(solution)/shard_map/ppermute | solution.py:34
  82.8 6.6 %collective-permute-start.33 = (bf16[16,1024]{1,0:T(8,128)(2,1)S(1)}, bf16[16,1024]{1,0:T(8,128)(2,1)S(1)}, u32[]{:S(2)}, u32[]{:S(2)}) collective-permute-start(bf16[16,1024]{1,0:T(8,128)(2,1)S(1)} %get-tuple-element.42), channel_id=1, source_target_pairs={{0,7},{1,6},{2,5},{3,4},{4,3},{5,2},{6,1},{7,0},{8,15},{9,14},{10,... | collective-permute-start | bytes 98312 | tf_op jit(solution)/shard_map/ppermute | solution.py:34
  85.9 5.7 %collective-permute-start.34 = (bf16[16,1024]{1,0:T(8,128)(2,1)S(1)}, bf16[16,1024]{1,0:T(8,128)(2,1)S(1)}, u32[]{:S(2)}, u32[]{:S(2)}) collective-permute-start(bf16[16,1024]{1,0:T(8,128)(2,1)S(1)} %get-tuple-element.44), channel_id=1, source_target_pairs={{0,6},{1,7},{2,4},{3,5},{4,2},{5,3},{6,0},{7,1},{8,14},{9,15},{10,... | collective-permute-start | bytes 98312 | tf_op jit(solution)/shard_map/ppermute | solution.py:34
  91.7 3.8 %collective-permute-start.39 = (bf16[32,1024]{1,0:T(8,128)(2,1)S(1)}, bf16[32,1024]{1,0:T(8,128)(2,1)S(1)}, u32[]{:S(2)}, u32[]{:S(2)}) collective-permute-start(bf16[32,1024]{1,0:T(8,128)(2,1)S(1)} %pad_maximum_fusion.refs_0_), channel_id=1, source_target_pairs={{0,24},{8,16},{16,8},{24,0},{1,25},{9,17},{17,9},{25,1},{2,26},{10... | collective-permute-start | bytes 196616 | tf_op jit(solution)/shard_map/ppermute | solution.py:34
  91.7 5.0 %collective-permute-start.38 = (bf16[32,1024]{1,0:T(8,128)(2,1)S(1)}, bf16[32,1024]{1,0:T(8,128)(2,1)S(1)}, u32[]{:S(2)}, u32[]{:S(2)}) collective-permute-start(bf16[32,1024]{1,0:T(8,128)(2,1)S(1)} %pad_maximum_fusion.refs_0_), channel_id=1, source_target_pairs={{0,16},{8,24},{16,0},{24,8},{1,17},{9,25},{17,1},{25,9},{2,18},{10... | collective-permute-start | bytes 196616 | tf_op jit(solution)/shard_map/ppermute | solution.py:34
  92.5 4.3 %collective-permute-start.37 = (bf16[32,1024]{1,0:T(8,128)(2,1)S(1)}, bf16[32,1024]{1,0:T(8,128)(2,1)S(1)}, u32[]{:S(2)}, u32[]{:S(2)}) collective-permute-start(bf16[32,1024]{1,0:T(8,128)(2,1)S(1)} %pad_maximum_fusion.refs_0_), channel_id=1, source_target_pairs={{0,8},{8,0},{16,24},{24,16},{1,9},{9,1},{17,25},{25,17},{2,10},{10... | collective-permute-start | bytes 196616 | tf_op jit(solution)/shard_map/ppermute | solution.py:34

commit v2 on v1

v2 whole, which is shorter than its diff:
```python
import functools

import jax
import jax.numpy as jnp
from jax import lax
from jax.experimental import pallas as pl
from jax.experimental.pallas import tpu as pltpu
from jax.sharding import PartitionSpec as P


BF16, F32 = jnp.bfloat16, jnp.float32
VMEM = pl.BlockSpec(memory_space=pltpu.VMEM)
SMEM = pl.BlockSpec(memory_space=pltpu.SMEM)


def call(body, shapes, *args, cost=(1 << 30, 1 << 22)):
    specs = [SMEM if a.dtype == jnp.int32 else VMEM for a in args]
    return pl.pallas_call(
        body,
        out_shape=shapes,
        in_specs=specs,
        out_specs=jax.tree.map(lambda _: VMEM, shapes),
        cost_estimate=pl.CostEstimate(flops=cost[0], bytes_accessed=cost[1], transcendentals=0),
        compiler_params=pltpu.CompilerParams(vmem_limit_bytes=6 << 20),
    )(*args)


def shape(dims, dtype):
    return jax.ShapeDtypeStruct(tuple(dims), dtype)


def swap(x, axes, bit):
    count = lax.axis_size(axes)
    return lax.ppermute(x, axes, [(i, i ^ bit) for i in range(count)])


def logits_body(tok_hbm, gain_hbm, phi_hbm, scaled_ref, part_ref, tok_ref, gain_ref, phi_ref, sems):
    copies = [
        pltpu.make_async_copy(tok_hbm, tok_ref, sems.at[0]),
        pltpu.make_async_copy(phi_hbm, phi_ref, sems.at[1]),
        pltpu.make_async_copy(gain_hbm, gain_ref, sems.at[2]),
    ]
    for c in copies:
        c.start()
    for c in copies:
        c.wait()
    tok = tok_ref[0].astype(F32)
    scaled = (tok * gain_ref[...].astype(F32)).astype(BF16)
    scaled_ref[...] = scaled
    slots = phi_ref.shape[1]
    part = jnp.dot(scaled, phi_ref[...], preferred_element_type=F32)
    part_ref[:slots] = part.T
    squares = jnp.sum(tok * tok, axis=1, keepdims=True)
    part_ref[slots:] = jnp.broadcast_to(squares, (tok.shape[0], 128)).T[:8]


def logits_of(part_refs, width):
    total = part_refs[0][...]
    for ref in part_refs[1:]:
        total = total + ref[...]
    slots = total.shape[0] - 8
    inv_rms = lax.rsqrt(total[slots : slots + 1] / width + 1e-06)
    return total[:slots] * inv_rms, inv_rms


def slots_body(width, n, experts, batches, where_ref, *refs):
    part_refs, scaled_ref, message_refs, held = refs[:n], refs[n], refs[n + 1 : -1], refs[-1]
    logits, inv_rms = logits_of(part_refs, width)
    top = jnp.max(logits, axis=1, keepdims=True)
    raised = jnp.exp(logits - top)
    total = jnp.sum(raised, axis=1, keepdims=True)
    weights = (raised * (inv_rms / total)).astype(BF16)
    share = scaled_ref.shape[1]
    rows = held.shape[0] // (experts * batches)
    slot = jnp.dot(weights, scaled_ref[...], preferred_element_type=F32)
    held[:, :share] = slot.astype(BF16)
    mass = top + jnp.log(total)
    high = mass.astype(BF16).astype(F32)
    middle = (mass - high).astype(BF16).astype(F32)
    low = mass - high - middle
    lane = lax.broadcasted_iota(jnp.int32, (held.shape[0], held.shape[1] - share), 1)
    stats = jnp.where(
        lane == 0, high, jnp.where(lane == 1, middle, jnp.where(lane == 2, low, 0.0))
    )
    held[:, share:] = stats.astype(BF16)
    for h in range(experts):
        for r in range(batches):
            at = ((where_ref[1] ^ h) * batches + (where_ref[0] ^ r)) * rows
            message_refs[h * batches + r][...] = held[pl.ds(pl.multiple_of(at, rows), rows)]


def combine_body(width, n, experts, batches, where_ref, *refs):
    part_refs, out_ref, held = refs[:n], refs[n], refs[n + 1]
    logits, _ = logits_of(part_refs, width)
    raised = jnp.exp(logits - jnp.max(logits, axis=0, keepdims=True))
    held[...] = raised / jnp.sum(raised, axis=0, keepdims=True)
    rows = logits.shape[0] // (experts * batches)
    blocks = []
    for r in range(batches):
        for h in range(experts):
            at = ((where_ref[1] ^ h) * batches + (where_ref[0] ^ r)) * rows
            blocks.append(held[pl.ds(pl.multiple_of(at, rows), rows)])
    out_ref[...] = jnp.concatenate(blocks, axis=0).T.astype(BF16)


def gather_body(groups, batches, *refs):
    out_ref = refs[-1]
    rows, share = refs[0].shape[0], out_ref.shape[1]
    for h in range(groups):
        pieces = [refs[h * batches + r][...].astype(F32) for r in range(batches)]
        mass = [
            p[:, share : share + 1] + p[:, share + 1 : share + 2] + p[:, share + 2 : share + 3]
            for p in pieces
        ]
        top = functools.reduce(jnp.maximum, mass)
        raised = [jnp.exp(m - top) for m in mass]
        total = functools.reduce(jnp.add, raised)
        out = sum(p[:, :share] * (w / total) for p, w in zip(pieces, raised))
        out_ref[h * rows : (h + 1) * rows] = out.astype(BF16)


def gate_up_body(s, last, where_ref, *refs):
    low_ref, high_ref, gate_ref, up_ref = refs[:4]
    share = low_ref.shape[1]
    at = pl.ds(pl.multiple_of((where_ref[2] ^ s) * share, share), share)
    x = jnp.concatenate([low_ref[...], high_ref[...]], axis=0)
    g = jnp.dot(x, gate_ref[0, at], preferred_element_type=F32)
    u = jnp.dot(x, up_ref[0, at], preferred_element_type=F32)
    if len(refs) > (5 if last else 6):
        g, u = g + refs[4][...], u + refs[5][...]
    if last:
        refs[-1][...] = (g / (1.0 + jnp.exp(-g)) * u).astype(BF16)
    else:
        refs[-2][...] = g
        refs[-1][...] = u


def down_body(s, where_ref, hidden_ref, down_ref, keep_ref, send_ref):
    share = keep_ref.shape[1]
    at = pl.ds(pl.multiple_of((where_ref[2] ^ s) * share, share), share)
    out = jnp.dot(hidden_ref[...], down_ref[0, :, at], preferred_element_type=F32).astype(BF16)
    half = out.shape[0] // 2
    keep_ref[...] = out[:half]
    send_ref[...] = out[half:]


def output_body(combine_ref, *refs):
    pieces, out_ref = refs[:-1], refs[-1]
    slots = jnp.concatenate([p[...] for p in pieces], axis=0)
    out_ref[...] = jnp.dot(combine_ref[...], slots, preferred_element_type=F32).astype(BF16)


def fetch_body(*refs):
    count = (len(refs) - 1) // 2
    copies = [
        pltpu.make_async_copy(refs[i], refs[count + i], refs[-1].at[i]) for i in range(count)
    ]
    for c in copies:
        c.start()
    for c in copies:
        c.wait()


def fetch(*arrays):
    return pl.pallas_call(
        fetch_body,
        out_shape=[pltpu.VMEM(a.shape, a.dtype) for a in arrays],
        in_specs=[pl.BlockSpec(memory_space=pltpu.HBM)] * len(arrays),
        out_specs=[VMEM] * len(arrays),
        scratch_shapes=[pltpu.SemaphoreType.DMA((len(arrays),))],
        cost_estimate=pl.CostEstimate(flops=1 << 30, bytes_accessed=1 << 25, transcendentals=0),
        compiler_params=pltpu.CompilerParams(vmem_limit_bytes=1 << 20),
        name="fetch",
    )(*(pltpu.with_memory_space_constraint(a, pltpu.HBM) for a in arrays))


def add(*xs):
    return functools.reduce(jnp.add, [x.astype(F32) for x in xs]).astype(BF16)


def local(tokens, gain, phi, w_gate, w_up, w_down):
    batches, experts, tensors = (lax.axis_size(a) for a in ("batch", "expert", "tensor"))
    for n in (batches, experts, tensors):
        assert n & (n - 1) == 0
    assert tokens.shape[0] == 1 and w_gate.shape[0] == 1
    where = jnp.stack([lax.axis_index(a) for a in ("batch", "expert", "tensor")]).astype(jnp.int32)
    width = w_gate.shape[1]
    count, share = tokens.shape[1:]
    slots = phi.shape[1]
    rows = slots // (experts * batches)

    scaled, part = pl.pallas_call(
        logits_body,
        out_shape=[shape((count, share), BF16), shape((slots + 8, count), F32)],
        in_specs=[pl.BlockSpec(memory_space=pltpu.HBM)] * 3,
        out_specs=[VMEM, VMEM],
        scratch_shapes=[
            pltpu.VMEM(tokens.shape, BF16),
            pltpu.VMEM(gain.shape, BF16),
            pltpu.VMEM(phi.shape, BF16),
            pltpu.SemaphoreType.DMA((3,)),
        ],
        cost_estimate=pl.CostEstimate(flops=1 << 30, bytes_accessed=1 << 22, transcendentals=0),
        compiler_params=pltpu.CompilerParams(vmem_limit_bytes=6 << 20),
        name="logits",
    )(*(pltpu.with_memory_space_constraint(x, pltpu.HBM) for x in (tokens, gain, phi)))
    parts = [part] + [swap(part, "tensor", s) for s in range(1, tensors)]
    messages = pl.pallas_call(
        functools.partial(slots_body, width, tensors, experts, batches),
        out_shape=[shape((rows, share + 128), BF16)] * (experts * batches),
        in_specs=[SMEM] + [VMEM] * (tensors + 1),
        out_specs=[VMEM] * (experts * batches),
        scratch_shapes=[pltpu.VMEM((slots, share + 128), BF16)],
        cost_estimate=pl.CostEstimate(flops=1 << 30, bytes_accessed=1 << 22, transcendentals=0),
        compiler_params=pltpu.CompilerParams(vmem_limit_bytes=6 << 20),
        name="slots",
    )(where, *parts, scaled)
    combine = pl.pallas_call(
        functools.partial(combine_body, width, tensors, experts, batches),
        out_shape=shape((count, slots), BF16),
        in_specs=[SMEM] + [VMEM] * tensors,
        out_specs=VMEM,
        scratch_shapes=[pltpu.VMEM((slots, count), F32)],
        cost_estimate=pl.CostEstimate(flops=1 << 30, bytes_accessed=1 << 22, transcendentals=0),
        compiler_params=pltpu.CompilerParams(vmem_limit_bytes=6 << 20),
        name="combine",
    )(where, *parts)
    arrived = [
        m if i == 0 else swap(m, ("batch", "expert"), i % batches * experts + i // batches)
        for i, m in enumerate(messages)
    ]
    own = call(
        functools.partial(gather_body, experts, batches),
        shape((experts * rows, share), BF16),
        *arrived,
    )
    w_gate, w_up, w_down = fetch(w_gate, w_up, w_down)
    hidden_share = w_gate.shape[2]
    all_rows = batches * experts * rows
    carry = []
    for s in [0, *range(tensors - 1, 0, -1)]:
        piece = own if s == 0 else swap(own, "tensor", s)
        bit = batches >> 1
        while bit > 1:
            piece = jnp.concatenate([piece, swap(piece, "batch", bit)], axis=0)
            bit >>= 1
        last = s == min(1, tensors - 1)
        carry = call(
            functools.partial(gate_up_body, s, last),
            shape((all_rows, hidden_share), BF16)
            if last
            else [shape((all_rows, hidden_share), F32)] * 2,
            where,
            piece,
            swap(piece, "batch", 1),
            w_gate,
            w_up,
            *carry,
            cost=(4 * all_rows * hidden_share * share, 1 << 24),
        )
    arrived = []
    for s in reversed(range(tensors)):
        keep, send = call(
            functools.partial(down_body, s),
            [shape((all_rows // 2, share), BF16)] * 2,
            where,
            carry,
            w_down,
            cost=(2 * all_rows * hidden_share * share, 1 << 23),
        )
        total = add(keep, swap(send, "batch", 1))
        bit = 2
        while bit < batches:
            half = total.shape[0] // 2
            other = swap(total[half:], "batch", bit)
            total = add(total[:half], other)
            bit <<= 1
        arrived.append(swap(total, "tensor", s) if s else total)
    total = add(*arrived)
    pieces = [total[h * rows : (h + 1) * rows] for h in range(experts)]
    pieces = [p if h == 0 else swap(p, "expert", h) for h, p in enumerate(pieces)]
    out = jnp.concatenate(pieces, axis=0)
    gathered = [out] + [swap(out, "batch", r) for r in range(1, batches)]
    return call(output_body, shape((count, share), BF16), combine, *gathered)[None]


def solution(mesh):
    placed = (
        P("expert", "batch", "tensor"),
        P("tensor"),
        P("tensor", None),
        P("expert", None, ("batch", "tensor")),
        P("expert", None, ("batch", "tensor")),
        P("expert", ("batch", "tensor"), None),
    )
    return jax.shard_map(
        local, mesh=mesh, in_specs=placed, out_specs=P("expert", "batch", "tensor"), check_vma=False
    )
```

time: 98.2 us -> 90.8 us (0.925)
  local copies, waits for them, and re-layouts: 8.88 us -> 0.07 us
  Pallas kernels: 13.3 us -> 20.9 us
  starting transfers between devices: 38.2 us -> 34.8 us
  waiting for transfers between devices: 36.8 us -> 34.3 us
    unnamed x12 -> x3, local copies, waits for them, and re-layouts: 8.17 us -> 0.02 us
    pallas_call x4 -> x10, Pallas kernels: 3.35 us -> 10.4 us  [call(): pl.pallas_call(body, out_shape=shapes, in_specs=specs, out_specs=jax.tree...]
    all_to_all x1 -> x0, waiting for transfers between devices: 6.32 us -> none  [local(): lax.all_to_all(message, ('expert', 'batch'), split_axis=0, concat_axis=0,...]
    ppermute x40 -> x36, waiting for transfers between devices: 30.5 us -> 34.3 us  [swap(): return lax.ppermute(x, axes, [(i, i ^ bit) for i in range(count)])]
    all_to_all x1 -> x0, starting transfers between devices: 3.72 us -> none  [local(): lax.all_to_all(message, ('expert', 'batch'), split_axis=0, concat_axis=0,...]
    pallas_call x5 -> x3, Pallas kernels: 9.25 us -> 9.78 us  [the longest x1 7.28 us: fetch(): pl.pallas_call(fetch_body, out_shape=[pltpu.VMEM(a.shape, a.dtype) for a...]
    ppermute x40 -> x36, starting transfers between devices: 34.5 us -> 34.8 us  [swap(): return lax.ppermute(x, axes, [(i, i ^ bit) for i in range(count)])]
  transfers between devices with their start and end apart: 41 -> 36, of which waited for: 19 -> 14; matrix products, arithmetic and copies ran while one was open for 0% -> 0% of each run, Pallas kernels for 5% -> 16%
where the time goes in v2:
time: 90.8 us; the launch traced here: 90.6 us
  starting transfers between devices  34.8 us (38%)
  waiting for transfers between devices  34.3 us (38%)
  Pallas kernels  20.9 us (23%)
    ppermute x36, starting transfers between devices, swap(): return lax.ppermute(x, axes, [(i, i ^ bit) for i in range(count)])  34.8 us
    ppermute x36, waiting for transfers between devices, swap(): return lax.ppermute(x, axes, [(i, i ^ bit) for i in range(count)])  34.3 us
    pallas_call x10, Pallas kernels, call(): pl.pallas_call(body, out_shape=shapes, in_specs=specs, out_specs=jax.tree...  10.4 us
    pallas_call x1, Pallas kernels, fetch(): pl.pallas_call(fetch_body, out_shape=[pltpu.VMEM(a.shape, a.dtype) for a...  7.28 us
  transfers between devices with their start and end apart: 36, of which 14 were waited for; matrix products, arithmetic and copies ran while one was open for 0% of the time, Pallas kernels for 16%

profile of v2, /device:TPU:0, one launch (start us, length us, event | category | flops | bytes accessed | tf_op | source)
XLA Modules:
  0.0 90.6 jit_solution(14896438821914928661)
XLA Ops:
  0.0 1.5 %logits.1 = (bf16[256,1024]{1,0:T(8,128)(2,1)S(1)}, f32[136,256]{1,0:T(8,128)S(1)}) custom-call(bf16[1,256,1024]{2,1,0:T(8,128)(2,1)} %tok_hbm.1, bf16[1024]{0:T(1024)(128)(2,1)} %gain_hbm.1, bf16[1024,128]{1,0:T(8,128)(2,1)} %phi_hbm.1), custom_call_target="tpu_custom_call" | custom-call | flops 1073741824 | bytes 4194304 | tf_op jit(solution)/shard_map/logits/pallas_call | solution.py:192
  1.5 5.1 %collective-permute-start.2 = (f32[136,256]{1,0:T(8,128)S(1)}, f32[136,256]{1,0:T(8,128)S(1)}, u32[]{:S(2)}, u32[]{:S(2)}) collective-permute-start(f32[136,256]{1,0:T(8,128)S(1)} %get-tuple-element.32.refs_0_), channel_id=1, source_target_pairs={{0,3},{1,2},{2,1},{3,0},{4,7},{5,6},{6,5},{7,4},{8,11},{9,10},{10,... | collective-permute-start | bytes 417800 | tf_op jit(solution)/shard_map/ppermute | solution.py:34
  6.7 0.0 collective-permute-start.1
  6.7 0.6 collective-permute-start
  7.3 0.1 pad_add_fusion.where_ref
  7.4 3.9 %collective-permute-done.2.refs_3_ = f32[136,256]{1,0:T(8,128)S(1)} collective-permute-done((f32[136,256]{1,0:T(8,128)S(1)}, f32[136,256]{1,0:T(8,128)S(1)}, u32[]{:S(2)}, u32[]{:S(2)}) %collective-permute-start.2) | collective-permute-done | bytes 139296 | tf_op jit(solution)/shard_map/ppermute | solution.py:34
  11.3 7.2 %collective-permute-done.1.refs_2_ = f32[136,256]{1,0:T(8,128)S(1)} collective-permute-done((f32[136,256]{1,0:T(8,128)S(1)}, f32[136,256]{1,0:T(8,128)S(1)}, u32[]{:S(2)}, u32[]{:S(2)}) %collective-permute-start.1) | collective-permute-done | bytes 139296 | tf_op jit(solution)/shard_map/ppermute | solution.py:34
  18.4 1.0 %slots.1 = (bf16[16,1152]{1,0:T(8,128)(2,1)S(1)}, bf16[16,1152]{1,0:T(8,128)(2,1)S(1)}, bf16[16,1152]{1,0:T(8,128)(2,1)S(1)}, bf16[16,1152]{1,0:T(8,128)(2,1)S(1...) custom-call(s32[3]{0:T(128)S(1)} %pad_add_fusion.where_ref, ...), custom_call_target="tpu_custom_call" | custom-call | flops 1073741824 | bytes 4194304 | tf_op jit(solution)/shard_map/slots/pallas_call | solution.py:208
  19.4 0.1 collective-permute-start.3
  19.5 1.6 %collective-permute-start.4 = (bf16[16,1152]{1,0:T(8,128)(2,1)S(1)}, bf16[16,1152]{1,0:T(8,128)(2,1)S(1)}, u32[]{:S(2)}, u32[]{:S(2)}) collective-permute-start(bf16[16,1152]{1,0:T(8,128)(2,1)S(1)} %get-tuple-element.36), channel_id=1, source_target_pairs={{0,16},{4,20},{8,24},{12,28},{16,0},{20,4},{24,8},{28,12},{1,17},{... | collective-permute-start | bytes 110600 | tf_op jit(solution)/shard_map/ppermute | solution.py:34
  21.1 0.3 collective-permute-start.5
  21.4 1.5 %collective-permute-start.6 = (bf16[16,1152]{1,0:T(8,128)(2,1)S(1)}, bf16[16,1152]{1,0:T(8,128)(2,1)S(1)}, u32[]{:S(2)}, u32[]{:S(2)}) collective-permute-start(bf16[16,1152]{1,0:T(8,128)(2,1)S(1)} %get-tuple-element.38), channel_id=1, source_target_pairs={{0,4},{4,0},{8,12},{12,8},{16,20},{20,16},{24,28},{28,24},{1,5},{5... | collective-permute-start | bytes 110600 | tf_op jit(solution)/shard_map/ppermute | solution.py:34
  22.9 0.2 collective-permute-start.7
  23.1 2.4 %collective-permute-start.8 = (bf16[16,1152]{1,0:T(8,128)(2,1)S(1)}, bf16[16,1152]{1,0:T(8,128)(2,1)S(1)}, u32[]{:S(2)}, u32[]{:S(2)}) collective-permute-start(bf16[16,1152]{1,0:T(8,128)(2,1)S(1)} %get-tuple-element.40), channel_id=1, source_target_pairs={{0,20},{4,16},{8,28},{12,24},{16,4},{20,0},{24,12},{28,8},{1,21},{... | collective-permute-start | bytes 110600 | tf_op jit(solution)/shard_map/ppermute | solution.py:34
  25.5 0.2 collective-permute-start.9
  25.8 0.0 collective-permute-done.5.refs_3_
  25.8 0.0 collective-permute-done.6.refs_4_
  25.8 0.6 collective-permute-done.7.refs_5_
  26.4 2.0 %collective-permute-done.8.refs_6_ = bf16[16,1152]{1,0:T(8,128)(2,1)S(1)} collective-permute-done((bf16[16,1152]{1,0:T(8,128)(2,1)S(1)}, bf16[16,1152]{1,0:T(8,128)(2,1)S(1)}, u32[]{:S(2)}, u32[]{:S(2)}) %collective-permute-start.8) | collective-permute-done | bytes 36896 | tf_op jit(solution)/shard_map/ppermute | solution.py:34
  28.4 1.5 %collective-permute-done.9.refs_7_ = bf16[16,1152]{1,0:T(8,128)(2,1)S(1)} collective-permute-done((bf16[16,1152]{1,0:T(8,128)(2,1)S(1)}, bf16[16,1152]{1,0:T(8,128)(2,1)S(1)}, u32[]{:S(2)}, u32[]{:S(2)}) %collective-permute-start.9) | collective-permute-done | bytes 36896 | tf_op jit(solution)/shard_map/ppermute | solution.py:34
  29.9 0.2 shard_map.64
  30.1 0.6 collective-permute-start.19
  30.7 7.3 %fetch.1 = (bf16[1,4096,896]{2,1,0:T(8,128)(2,1)S(1)}, bf16[1,4096,896]{2,1,0:T(8,128)(2,1)S(1)}, bf16[1,896,4096]{2,1,0:T(8,128)(2,1)S(1)}) custom-call(bf16[1,4096,896]{2,1,0:T(8,128)(2,1)} %refs_0_.1, bf16[1,4096,896]{2,1,0:T(8,128)(2,1)} %refs_1_.1, bf16[1,896,4096]{2,1,0:T(8,128)(2,1)} %refs_2_.1), custom_call_target="tpu_custom_call" | custom-call | flops 1073741824 | bytes 33554432 | tf_op jit(solution)/shard_map/fetch/pallas_call | solution.py:165
  38.0 2.6 %collective-permute-start.16 = (bf16[32,1024]{1,0:T(8,128)(2,1)S(1)}, bf16[32,1024]{1,0:T(8,128)(2,1)S(1)}, u32[]{:S(2)}, u32[]{:S(2)}) collective-permute-start(bf16[32,1024]{1,0:T(8,128)(2,1)S(1)} %shard_map.64), channel_id=1, source_target_pairs={{0,3},{1,2},{2,1},{3,0},{4,7},{5,6},{6,5},{7,4},{8,11},{9,10},{10,... | collective-permute-start | bytes 196616 | tf_op jit(solution)/shard_map/ppermute | solution.py:34
  40.5 1.9 %collective-permute-start.10 = (bf16[32,1024]{1,0:T(8,128)(2,1)S(1)}, bf16[32,1024]{1,0:T(8,128)(2,1)S(1)}, u32[]{:S(2)}, u32[]{:S(2)}) collective-permute-start(bf16[32,1024]{1,0:T(8,128)(2,1)S(1)} %shard_map.64), channel_id=1, source_target_pairs={{0,1},{1,0},{2,3},{3,2},{4,5},{5,4},{6,7},{7,6},{8,9},{9,8},{10,11... | collective-permute-start | bytes 196616 | tf_op jit(solution)/shard_map/ppermute | solution.py:34
  42.4 0.1 collective-permute-start.20
  42.5 2.9 %collective-permute-done.10 = bf16[32,1024]{1,0:T(8,128)(2,1)S(1)} collective-permute-done((bf16[32,1024]{1,0:T(8,128)(2,1)S(1)}, bf16[32,1024]{1,0:T(8,128)(2,1)S(1)}, u32[]{:S(2)}, u32[]{:S(2)}) %collective-permute-start.10) | collective-permute-done | bytes 65568 | tf_op jit(solution)/shard_map/ppermute | solution.py:34
  45.4 1.5 %collective-permute-start.11 = (bf16[32,1024]{1,0:T(8,128)(2,1)S(1)}, bf16[32,1024]{1,0:T(8,128)(2,1)S(1)}, u32[]{:S(2)}, u32[]{:S(2)}) collective-permute-start(bf16[32,1024]{1,0:T(8,128)(2,1)S(1)} %collective-permute-done.10), channel_id=1, source_target_pairs={{0,16},{8,24},{16,0},{24,8},{1,17},{9,25},{17,1},{25,9},{2,18},{10... | collective-permute-start | bytes 196616 | tf_op jit(solution)/shard_map/ppermute | solution.py:34
  46.9 1.1 %collective-permute-start.14 = (bf16[32,1024]{1,0:T(8,128)(2,1)S(1)}, bf16[32,1024]{1,0:T(8,128)(2,1)S(1)}, u32[]{:S(2)}, u32[]{:S(2)}) collective-permute-start(bf16[32,1024]{1,0:T(8,128)(2,1)S(1)} %collective-permute-done.13), channel_id=1, source_target_pairs={{0,16},{8,24},{16,0},{24,8},{1,17},{9,25},{17,1},{25,9},{2,18},{10... | collective-permute-start | bytes 196616 | tf_op jit(solution)/shard_map/ppermute | solution.py:34
  48.0 1.1 %collective-permute-start.17 = (bf16[32,1024]{1,0:T(8,128)(2,1)S(1)}, bf16[32,1024]{1,0:T(8,128)(2,1)S(1)}, u32[]{:S(2)}, u32[]{:S(2)}) collective-permute-start(bf16[32,1024]{1,0:T(8,128)(2,1)S(1)} %collective-permute-done.16), channel_id=1, source_target_pairs={{0,16},{8,24},{16,0},{24,8},{1,17},{9,25},{17,1},{25,9},{2,18},{10... | collective-permute-start | bytes 196616 | tf_op jit(solution)/shard_map/ppermute | solution.py:34
  49.1 3.4 %collective-permute-done.17 = bf16[32,1024]{1,0:T(8,128)(2,1)S(1)} collective-permute-done((bf16[32,1024]{1,0:T(8,128)(2,1)S(1)}, bf16[32,1024]{1,0:T(8,128)(2,1)S(1)}, u32[]{:S(2)}, u32[]{:S(2)}) %collective-permute-start.17) | collective-permute-done | bytes 65568 | tf_op jit(solution)/shard_map/ppermute | solution.py:34
  52.6 0.6 collective-permute-start.15
  53.2 0.1 collective-permute-start.12
  53.2 1.3 %shard_map.65 = (f32[128,896]{1,0:T(8,128)S(1)}, f32[128,896]{1,0:T(8,128)S(1)}) custom-call(s32[3]{0:T(128)S(1)} %pad_add_fusion.where_ref, bf16[64,1024]{1,0:T(8,128)(2,1)S(1)} %pad_maximum_fusion.refs_0_, bf16[64,1024]{1,0:T(8,128)(2,1)S(1)} %collective-permute-done.20.refs_1_, bf16[1,4096,896]{2,1,0:T(8,128)(2,1)S(1)} %get-tuple-element.42.refs_2_, ...), custom_call_target="tpu_custom_call" | custom-call | flops 469762048 | bytes 16777216 | tf_op jit(solution)/shard_map/pallas_call | solution.py:18
  54.5 1.3 %shard_map.66 = (f32[128,896]{1,0:T(8,128)S(1)}, f32[128,896]{1,0:T(8,128)S(1)}) custom-call(s32[3]{0:T(128)S(1)} %pad_add_fusion.where_ref, bf16[64,1024]{1,0:T(8,128)(2,1)S(1)} %constant_dynamic-update-slice_fusion.4.refs_0_, bf16[64,1024]{1,0:T(8,128)(2,1)S(1)} %collective-permute-done.18.refs_1_, bf16[1,4096,896]{2,1,0:T(8,128)(2,1)S(1)} %get-tuple-element.42.refs_2_, ...), custom_call_target="tpu_custom_call" | custom-call | flops 469762048 | bytes 16777216 | tf_op jit(solution)/shard_map/pallas_call | solution.py:18
  55.8 1.3 %shard_map.67 = (f32[128,896]{1,0:T(8,128)S(1)}, f32[128,896]{1,0:T(8,128)S(1)}) custom-call(s32[3]{0:T(128)S(1)} %pad_add_fusion.where_ref, bf16[64,1024]{1,0:T(8,128)(2,1)S(1)} %constant_dynamic-update-slice_fusion.2.refs_0_, bf16[64,1024]{1,0:T(8,128)(2,1)S(1)} %collective-permute-done.15.refs_1_, bf16[1,4096,896]{2,1,0:T(8,128)(2,1)S(1)} %get-tuple-element.42.refs_2_, ...), custom_call_target="tpu_custom_call" | custom-call | flops 469762048 | bytes 16777216 | tf_op jit(solution)/shard_map/pallas_call | solution.py:18
  57.1 1.3 %shard_map.68.hidden_ref = bf16[128,896]{1,0:T(8,128)(2,1)S(1)} custom-call(s32[3]{0:T(128)S(1)} %pad_add_fusion.where_ref, bf16[64,1024]{1,0:T(8,128)(2,1)S(1)} %constant_dynamic-update-slice_fusion.refs_0_, bf16[64,1024]{1,0:T(8,128)(2,1)S(1)} %collective-permute-done.12.refs_1_, bf16[1,4096,896]{2,1,0:T(8,128)(2,1)S(1)} %get-tuple-element.42.refs_2_, ...), custom_call_target="tpu_custom_call" | custom-call | flops 469762048 | bytes 16777216 | tf_op jit(solution)/shard_map/pallas_call | solution.py:18
  58.4 1.0 %shard_map.72 = (bf16[64,1024]{1,0:T(8,128)(2,1)S(1)}, bf16[64,1024]{1,0:T(8,128)(2,1)S(1)}) custom-call(s32[3]{0:T(128)S(1)} %pad_add_fusion.where_ref, bf16[128,896]{1,0:T(8,128)(2,1)S(1)} %shard_map.68.hidden_ref, bf16[1,896,4096]{2,1,0:T(8,128)(2,1)S(1)} %get-tuple-element.50.down_ref), custom_call_target="tpu_custom_call" | custom-call | flops 234881024 | bytes 8388608 | tf_op jit(solution)/shard_map/pallas_call | solution.py:18
  59.4 0.6 collective-permute-start.30
  60.0 1.0 %shard_map.71 = (bf16[64,1024]{1,0:T(8,128)(2,1)S(1)}, bf16[64,1024]{1,0:T(8,128)(2,1)S(1)}) custom-call(s32[3]{0:T(128)S(1)} %pad_add_fusion.where_ref, bf16[128,896]{1,0:T(8,128)(2,1)S(1)} %shard_map.68.hidden_ref, bf16[1,896,4096]{2,1,0:T(8,128)(2,1)S(1)} %get-tuple-element.50.down_ref), custom_call_target="tpu_custom_call" | custom-call | flops 234881024 | bytes 8388608 | tf_op jit(solution)/shard_map/pallas_call | solution.py:18
  61.0 0.1 collective-permute-start.27
  61.1 1.0 %shard_map.70 = (bf16[64,1024]{1,0:T(8,128)(2,1)S(1)}, bf16[64,1024]{1,0:T(8,128)(2,1)S(1)}) custom-call(s32[3]{0:T(128)S(1)} %pad_add_fusion.where_ref, bf16[128,896]{1,0:T(8,128)(2,1)S(1)} %shard_map.68.hidden_ref, bf16[1,896,4096]{2,1,0:T(8,128)(2,1)S(1)} %get-tuple-element.50.down_ref), custom_call_target="tpu_custom_call" | custom-call | flops 234881024 | bytes 8388608 | tf_op jit(solution)/shard_map/pallas_call | solution.py:18
  62.1 0.6 collective-permute-start.24
  62.6 1.0 %shard_map.69 = (bf16[64,1024]{1,0:T(8,128)(2,1)S(1)}, bf16[64,1024]{1,0:T(8,128)(2,1)S(1)}) custom-call(s32[3]{0:T(128)S(1)} %pad_add_fusion.where_ref, bf16[128,896]{1,0:T(8,128)(2,1)S(1)} %shard_map.68.hidden_ref, bf16[1,896,4096]{2,1,0:T(8,128)(2,1)S(1)} %get-tuple-element.50.down_ref), custom_call_target="tpu_custom_call" | custom-call | flops 234881024 | bytes 8388608 | tf_op jit(solution)/shard_map/pallas_call | solution.py:18
  63.6 0.1 collective-permute-start.21
  63.8 1.5 %collective-permute-start.31 = (bf16[32,1024]{1,0:T(8,128)(2,1)S(1)}, bf16[32,1024]{1,0:T(8,128)(2,1)S(1)}, u32[]{:S(2)}, u32[]{:S(2)}) collective-permute-start(bf16[32,1024]{1,0:T(8,128)(2,1)S(1)} %slice.47), channel_id=1, source_target_pairs={{0,16},{8,24},{16,0},{24,8},{1,17},{9,25},{17,1},{25,9},{2,18},{10... | collective-permute-start | bytes 196616 | tf_op jit(solution)/shard_map/ppermute | solution.py:34
  65.4 0.6 collective-permute-start.28
  66.0 1.5 %collective-permute-start.25 = (bf16[32,1024]{1,0:T(8,128)(2,1)S(1)}, bf16[32,1024]{1,0:T(8,128)(2,1)S(1)}, u32[]{:S(2)}, u32[]{:S(2)}) collective-permute-start(bf16[32,1024]{1,0:T(8,128)(2,1)S(1)} %slice.43), channel_id=1, source_target_pairs={{0,16},{8,24},{16,0},{24,8},{1,17},{9,25},{17,1},{25,9},{2,18},{10... | collective-permute-start | bytes 196616 | tf_op jit(solution)/shard_map/ppermute | solution.py:34
  67.6 0.6 collective-permute-start.22
  68.3 2.1 %collective-permute-done.28 = bf16[32,1024]{1,0:T(8,128)(2,1)S(1)} collective-permute-done((bf16[32,1024]{1,0:T(8,128)(2,1)S(1)}, bf16[32,1024]{1,0:T(8,128)(2,1)S(1)}, u32[]{:S(2)}, u32[]{:S(2)}) %collective-permute-start.28) | collective-permute-done | bytes 65568 | tf_op jit(solution)/shard_map/ppermute | solution.py:34
  70.4 1.2 %collective-permute-start.29 = (bf16[32,1024]{1,0:T(8,128)(2,1)S(1)}, bf16[32,1024]{1,0:T(8,128)(2,1)S(1)}, u32[]{:S(2)}, u32[]{:S(2)}) collective-permute-start(bf16[32,1024]{1,0:T(8,128)(2,1)S(1)} %add_convert_fusion.6), channel_id=1, source_target_pairs={{0,1},{1,0},{2,3},{3,2},{4,5},{5,4},{6,7},{7,6},{8,9},{9,8},{10,11... | collective-permute-start | bytes 196616 | tf_op jit(solution)/shard_map/ppermute | solution.py:34
  71.6 0.2 collective-permute-done.25
  71.8 1.9 %collective-permute-start.26 = (bf16[32,1024]{1,0:T(8,128)(2,1)S(1)}, bf16[32,1024]{1,0:T(8,128)(2,1)S(1)}, u32[]{:S(2)}, u32[]{:S(2)}) collective-permute-start(bf16[32,1024]{1,0:T(8,128)(2,1)S(1)} %add_convert_fusion.7), channel_id=1, source_target_pairs={{0,2},{1,3},{2,0},{3,1},{4,6},{5,7},{6,4},{7,5},{8,10},{9,11},{10,... | collective-permute-start | bytes 196616 | tf_op jit(solution)/shard_map/ppermute | solution.py:34
  73.8 1.7 %collective-permute-start.23 = (bf16[32,1024]{1,0:T(8,128)(2,1)S(1)}, bf16[32,1024]{1,0:T(8,128)(2,1)S(1)}, u32[]{:S(2)}, u32[]{:S(2)}) collective-permute-start(bf16[32,1024]{1,0:T(8,128)(2,1)S(1)} %add_convert_fusion.8), channel_id=1, source_target_pairs={{0,3},{1,2},{2,1},{3,0},{4,7},{5,6},{6,5},{7,4},{8,11},{9,10},{10,... | collective-permute-start | bytes 196616 | tf_op jit(solution)/shard_map/ppermute | solution.py:34
  75.5 3.1 %collective-permute-done.26 = bf16[32,1024]{1,0:T(8,128)(2,1)S(1)} collective-permute-done((bf16[32,1024]{1,0:T(8,128)(2,1)S(1)}, bf16[32,1024]{1,0:T(8,128)(2,1)S(1)}, u32[]{:S(2)}, u32[]{:S(2)}) %collective-permute-start.26) | collective-permute-done | bytes 65568 | tf_op jit(solution)/shard_map/ppermute | solution.py:34
  78.6 1.4 %collective-permute-done.23 = bf16[32,1024]{1,0:T(8,128)(2,1)S(1)} collective-permute-done((bf16[32,1024]{1,0:T(8,128)(2,1)S(1)}, bf16[32,1024]{1,0:T(8,128)(2,1)S(1)}, u32[]{:S(2)}, u32[]{:S(2)}) %collective-permute-start.23) | collective-permute-done | bytes 65568 | tf_op jit(solution)/shard_map/ppermute | solution.py:34
  80.1 1.0 %collective-permute-start.32 = (bf16[16,1024]{1,0:T(8,128)(2,1)S(1)}, bf16[16,1024]{1,0:T(8,128)(2,1)S(1)}, u32[]{:S(2)}, u32[]{:S(2)}) collective-permute-start(bf16[16,1024]{1,0:T(8,128)(2,1)S(1)} %get-tuple-element.60), channel_id=1, source_target_pairs={{0,4},{4,0},{1,5},{5,1},{2,6},{6,2},{3,7},{7,3},{8,12},{12,8},{9,1... | collective-permute-start | bytes 98312 | tf_op jit(solution)/shard_map/ppermute | solution.py:34
  81.1 3.0 %collective-permute-done.32 = bf16[16,1024]{1,0:T(8,128)(2,1)S(1)} collective-permute-done((bf16[16,1024]{1,0:T(8,128)(2,1)S(1)}, bf16[16,1024]{1,0:T(8,128)(2,1)S(1)}, u32[]{:S(2)}, u32[]{:S(2)}) %collective-permute-start.32) | collective-permute-done | bytes 32800 | tf_op jit(solution)/shard_map/ppermute | solution.py:34
  84.1 1.3 %collective-permute-start.34 = (bf16[32,1024]{1,0:T(8,128)(2,1)S(1)}, bf16[32,1024]{1,0:T(8,128)(2,1)S(1)}, u32[]{:S(2)}, u32[]{:S(2)}) collective-permute-start(bf16[32,1024]{1,0:T(8,128)(2,1)S(1)} %pad_maximum_fusion.1.refs_0_), channel_id=1, source_target_pairs={{0,16},{8,24},{16,0},{24,8},{1,17},{9,25},{17,1},{25,9},{2,18},{10... | collective-permute-start | bytes 196616 | tf_op jit(solution)/shard_map/ppermute | solution.py:34
  85.4 0.5 collective-permute-start.33
  85.9 0.7 combine.1.combine_ref
  86.7 1.8 %collective-permute-done.35.refs_3_ = bf16[32,1024]{1,0:T(8,128)(2,1)S(1)} collective-permute-done((bf16[32,1024]{1,0:T(8,128)(2,1)S(1)}, bf16[32,1024]{1,0:T(8,128)(2,1)S(1)}, u32[]{:S(2)}, u32[]{:S(2)}) %collective-permute-start.35) | collective-permute-done | bytes 65568 | tf_op jit(solution)/shard_map/ppermute | solution.py:34
  88.5 1.1 %collective-permute-done.34.refs_2_ = bf16[32,1024]{1,0:T(8,128)(2,1)S(1)} collective-permute-done((bf16[32,1024]{1,0:T(8,128)(2,1)S(1)}, bf16[32,1024]{1,0:T(8,128)(2,1)S(1)}, u32[]{:S(2)}, u32[]{:S(2)}) %collective-permute-start.34) | collective-permute-done | bytes 65568 | tf_op jit(solution)/shard_map/ppermute | solution.py:34
  89.6 1.1 %shard_map.73 = bf16[256,1024]{1,0:T(8,128)(2,1)} custom-call(bf16[256,128]{1,0:T(8,128)(2,1)S(1)} %combine.1.combine_ref, bf16[32,1024]{1,0:T(8,128)(2,1)S(1)} %pad_maximum_fusion.1.refs_0_, bf16[32,1024]{1,0:T(8,128)(2,1)S(1)} %collective-permute-done.33.refs_1_, bf16[32,1024]{1,0:T(8,128)(2,1)S(1)} %collective-permute-done.34.refs_2_, ...), custom_call_target="tpu_custom_call" | custom-call | flops 1073741824 | bytes 4194304 | tf_op jit(solution)/shard_map/pallas_call | solution.py:18
  (44 shorter events, 0.4 us)
Async XLA Ops:
  1.5 9.8 %collective-permute-start.2 = (f32[136,256]{1,0:T(8,128)S(1)}, f32[136,256]{1,0:T(8,128)S(1)}, u32[]{:S(2)}, u32[]{:S(2)}) collective-permute-start(f32[136,256]{1,0:T(8,128)S(1)} %get-tuple-element.32.refs_0_), channel_id=1, source_target_pairs={{0,3},{1,2},{2,1},{3,0},{4,7},{5,6},{6,5},{7,4},{8,11},{9,10},{10,... | collective-permute-start | bytes 417800 | tf_op jit(solution)/shard_map/ppermute | solution.py:34
  6.7 11.8 %collective-permute-start.1 = (f32[136,256]{1,0:T(8,128)S(1)}, f32[136,256]{1,0:T(8,128)S(1)}, u32[]{:S(2)}, u32[]{:S(2)}) collective-permute-start(f32[136,256]{1,0:T(8,128)S(1)} %get-tuple-element.32.refs_0_), channel_id=1, source_target_pairs={{0,2},{1,3},{2,0},{3,1},{4,6},{5,7},{6,4},{7,5},{8,10},{9,11},{10,... | collective-permute-start | bytes 417800 | tf_op jit(solution)/shard_map/ppermute | solution.py:34
  6.7 11.8 %collective-permute-start = (f32[136,256]{1,0:T(8,128)S(1)}, f32[136,256]{1,0:T(8,128)S(1)}, u32[]{:S(2)}, u32[]{:S(2)}) collective-permute-start(f32[136,256]{1,0:T(8,128)S(1)} %get-tuple-element.32.refs_0_), channel_id=1, source_target_pairs={{0,1},{1,0},{2,3},{3,2},{4,5},{5,4},{6,7},{7,6},{8,9},{9,8},{10,11... | collective-permute-start | bytes 417800 | tf_op jit(solution)/shard_map/ppermute | solution.py:34
  19.4 3.6 %collective-permute-start.3 = (bf16[16,1152]{1,0:T(8,128)(2,1)S(1)}, bf16[16,1152]{1,0:T(8,128)(2,1)S(1)}, u32[]{:S(2)}, u32[]{:S(2)}) collective-permute-start(bf16[16,1152]{1,0:T(8,128)(2,1)S(1)} %get-tuple-element.35), channel_id=1, source_target_pairs={{0,8},{4,12},{8,0},{12,4},{16,24},{20,28},{24,16},{28,20},{1,9},{5... | collective-permute-start | bytes 110600 | tf_op jit(solution)/shard_map/ppermute | solution.py:34
  19.5 6.0 %collective-permute-start.4 = (bf16[16,1152]{1,0:T(8,128)(2,1)S(1)}, bf16[16,1152]{1,0:T(8,128)(2,1)S(1)}, u32[]{:S(2)}, u32[]{:S(2)}) collective-permute-start(bf16[16,1152]{1,0:T(8,128)(2,1)S(1)} %get-tuple-element.36), channel_id=1, source_target_pairs={{0,16},{4,20},{8,24},{12,28},{16,0},{20,4},{24,8},{28,12},{1,17},{... | collective-permute-start | bytes 110600 | tf_op jit(solution)/shard_map/ppermute | solution.py:34
  21.1 4.7 %collective-permute-start.5 = (bf16[16,1152]{1,0:T(8,128)(2,1)S(1)}, bf16[16,1152]{1,0:T(8,128)(2,1)S(1)}, u32[]{:S(2)}, u32[]{:S(2)}) collective-permute-start(bf16[16,1152]{1,0:T(8,128)(2,1)S(1)} %get-tuple-element.37), channel_id=1, source_target_pairs={{0,24},{4,28},{8,16},{12,20},{16,8},{20,12},{24,0},{28,4},{1,25},{... | collective-permute-start | bytes 110600 | tf_op jit(solution)/shard_map/ppermute | solution.py:34
  21.4 4.4 %collective-permute-start.6 = (bf16[16,1152]{1,0:T(8,128)(2,1)S(1)}, bf16[16,1152]{1,0:T(8,128)(2,1)S(1)}, u32[]{:S(2)}, u32[]{:S(2)}) collective-permute-start(bf16[16,1152]{1,0:T(8,128)(2,1)S(1)} %get-tuple-element.38), channel_id=1, source_target_pairs={{0,4},{4,0},{8,12},{12,8},{16,20},{20,16},{24,28},{28,24},{1,5},{5... | collective-permute-start | bytes 110600 | tf_op jit(solution)/shard_map/ppermute | solution.py:34
  22.9 3.5 %collective-permute-start.7 = (bf16[16,1152]{1,0:T(8,128)(2,1)S(1)}, bf16[16,1152]{1,0:T(8,128)(2,1)S(1)}, u32[]{:S(2)}, u32[]{:S(2)}) collective-permute-start(bf16[16,1152]{1,0:T(8,128)(2,1)S(1)} %get-tuple-element.39), channel_id=1, source_target_pairs={{0,12},{4,8},{8,4},{12,0},{16,28},{20,24},{24,20},{28,16},{1,13},{... | collective-permute-start | bytes 110600 | tf_op jit(solution)/shard_map/ppermute | solution.py:34
  23.1 5.3 %collective-permute-start.8 = (bf16[16,1152]{1,0:T(8,128)(2,1)S(1)}, bf16[16,1152]{1,0:T(8,128)(2,1)S(1)}, u32[]{:S(2)}, u32[]{:S(2)}) collective-permute-start(bf16[16,1152]{1,0:T(8,128)(2,1)S(1)} %get-tuple-element.40), channel_id=1, source_target_pairs={{0,20},{4,16},{8,28},{12,24},{16,4},{20,0},{24,12},{28,8},{1,21},{... | collective-permute-start | bytes 110600 | tf_op jit(solution)/shard_map/ppermute | solution.py:34
  25.5 4.3 %collective-permute-start.9 = (bf16[16,1152]{1,0:T(8,128)(2,1)S(1)}, bf16[16,1152]{1,0:T(8,128)(2,1)S(1)}, u32[]{:S(2)}, u32[]{:S(2)}) collective-permute-start(bf16[16,1152]{1,0:T(8,128)(2,1)S(1)} %get-tuple-element.41), channel_id=1, source_target_pairs={{0,28},{4,24},{8,20},{12,16},{16,12},{20,8},{24,4},{28,0},{1,29},{... | collective-permute-start | bytes 110600 | tf_op jit(solution)/shard_map/ppermute | solution.py:34
  30.1 12.3 %collective-permute-start.19 = (bf16[32,1024]{1,0:T(8,128)(2,1)S(1)}, bf16[32,1024]{1,0:T(8,128)(2,1)S(1)}, u32[]{:S(2)}, u32[]{:S(2)}) collective-permute-start(bf16[32,1024]{1,0:T(8,128)(2,1)S(1)} %shard_map.64), channel_id=1, source_target_pairs={{0,16},{8,24},{16,0},{24,8},{1,17},{9,25},{17,1},{25,9},{2,18},{10... | collective-permute-start | bytes 196616 | tf_op jit(solution)/shard_map/ppermute | solution.py:34
  38.0 10.1 %collective-permute-start.16 = (bf16[32,1024]{1,0:T(8,128)(2,1)S(1)}, bf16[32,1024]{1,0:T(8,128)(2,1)S(1)}, u32[]{:S(2)}, u32[]{:S(2)}) collective-permute-start(bf16[32,1024]{1,0:T(8,128)(2,1)S(1)} %shard_map.64), channel_id=1, source_target_pairs={{0,3},{1,2},{2,1},{3,0},{4,7},{5,6},{6,5},{7,4},{8,11},{9,10},{10,... | collective-permute-start | bytes 196616 | tf_op jit(solution)/shard_map/ppermute | solution.py:34
  40.5 6.4 %collective-permute-start.13 = (bf16[32,1024]{1,0:T(8,128)(2,1)S(1)}, bf16[32,1024]{1,0:T(8,128)(2,1)S(1)}, u32[]{:S(2)}, u32[]{:S(2)}) collective-permute-start(bf16[32,1024]{1,0:T(8,128)(2,1)S(1)} %shard_map.64), channel_id=1, source_target_pairs={{0,2},{1,3},{2,0},{3,1},{4,6},{5,7},{6,4},{7,5},{8,10},{9,11},{10,... | collective-permute-start | bytes 196616 | tf_op jit(solution)/shard_map/ppermute | solution.py:34
  40.5 4.9 %collective-permute-start.10 = (bf16[32,1024]{1,0:T(8,128)(2,1)S(1)}, bf16[32,1024]{1,0:T(8,128)(2,1)S(1)}, u32[]{:S(2)}, u32[]{:S(2)}) collective-permute-start(bf16[32,1024]{1,0:T(8,128)(2,1)S(1)} %shard_map.64), channel_id=1, source_target_pairs={{0,1},{1,0},{2,3},{3,2},{4,5},{5,4},{6,7},{7,6},{8,9},{9,8},{10,11... | collective-permute-start | bytes 196616 | tf_op jit(solution)/shard_map/ppermute | solution.py:34
  42.4 10.8 %collective-permute-start.20 = (bf16[64,1024]{1,0:T(8,128)(2,1)S(1)}, bf16[64,1024]{1,0:T(8,128)(2,1)S(1)}, u32[]{:S(2)}, u32[]{:S(2)}) collective-permute-start(bf16[64,1024]{1,0:T(8,128)(2,1)S(1)} %pad_maximum_fusion.refs_0_), channel_id=1, source_target_pairs={{0,8},{8,0},{16,24},{24,16},{1,9},{9,1},{17,25},{25,17},{2,10},{10... | collective-permute-start | bytes 393224 | tf_op jit(solution)/shard_map/ppermute | solution.py:34
  45.4 7.7 %collective-permute-start.11 = (bf16[32,1024]{1,0:T(8,128)(2,1)S(1)}, bf16[32,1024]{1,0:T(8,128)(2,1)S(1)}, u32[]{:S(2)}, u32[]{:S(2)}) collective-permute-start(bf16[32,1024]{1,0:T(8,128)(2,1)S(1)} %collective-permute-done.10), channel_id=1, source_target_pairs={{0,16},{8,24},{16,0},{24,8},{1,17},{9,25},{17,1},{25,9},{2,18},{10... | collective-permute-start | bytes 196616 | tf_op jit(solution)/shard_map/ppermute | solution.py:34
  46.9 5.6 %collective-permute-start.14 = (bf16[32,1024]{1,0:T(8,128)(2,1)S(1)}, bf16[32,1024]{1,0:T(8,128)(2,1)S(1)}, u32[]{:S(2)}, u32[]{:S(2)}) collective-permute-start(bf16[32,1024]{1,0:T(8,128)(2,1)S(1)} %collective-permute-done.13), channel_id=1, source_target_pairs={{0,16},{8,24},{16,0},{24,8},{1,17},{9,25},{17,1},{25,9},{2,18},{10... | collective-permute-start | bytes 196616 | tf_op jit(solution)/shard_map/ppermute | solution.py:34
  48.0 4.5 %collective-permute-start.17 = (bf16[32,1024]{1,0:T(8,128)(2,1)S(1)}, bf16[32,1024]{1,0:T(8,128)(2,1)S(1)}, u32[]{:S(2)}, u32[]{:S(2)}) collective-permute-start(bf16[32,1024]{1,0:T(8,128)(2,1)S(1)} %collective-permute-done.16), channel_id=1, source_target_pairs={{0,16},{8,24},{16,0},{24,8},{1,17},{9,25},{17,1},{25,9},{2,18},{10... | collective-permute-start | bytes 196616 | tf_op jit(solution)/shard_map/ppermute | solution.py:34
  52.6 2.0 %collective-permute-start.18 = (bf16[64,1024]{1,0:T(8,128)(2,1)S(1)}, bf16[64,1024]{1,0:T(8,128)(2,1)S(1)}, u32[]{:S(2)}, u32[]{:S(2)}) collective-permute-start(bf16[64,1024]{1,0:T(8,128)(2,1)S(1)} %constant_dynamic-update-slice_fusion.4.refs_0_), channel_id=1, source_target_pairs={{0,8},{8,0},{16,24},{24,16},{1,9},{9,1},{17,25},{25,17},{2,10},{10... | collective-permute-start | bytes 393224 | tf_op jit(solution)/shard_map/ppermute | solution.py:34
  52.6 3.2 %collective-permute-start.15 = (bf16[64,1024]{1,0:T(8,128)(2,1)S(1)}, bf16[64,1024]{1,0:T(8,128)(2,1)S(1)}, u32[]{:S(2)}, u32[]{:S(2)}) collective-permute-start(bf16[64,1024]{1,0:T(8,128)(2,1)S(1)} %constant_dynamic-update-slice_fusion.2.refs_0_), channel_id=1, source_target_pairs={{0,8},{8,0},{16,24},{24,16},{1,9},{9,1},{17,25},{25,17},{2,10},{10... | collective-permute-start | bytes 393224 | tf_op jit(solution)/shard_map/ppermute | solution.py:34
  53.2 4.0 %collective-permute-start.12 = (bf16[64,1024]{1,0:T(8,128)(2,1)S(1)}, bf16[64,1024]{1,0:T(8,128)(2,1)S(1)}, u32[]{:S(2)}, u32[]{:S(2)}) collective-permute-start(bf16[64,1024]{1,0:T(8,128)(2,1)S(1)} %constant_dynamic-update-slice_fusion.refs_0_), channel_id=1, source_target_pairs={{0,8},{8,0},{16,24},{24,16},{1,9},{9,1},{17,25},{25,17},{2,10},{10... | collective-permute-start | bytes 393224 | tf_op jit(solution)/shard_map/ppermute | solution.py:34
  59.4 4.3 %collective-permute-start.30 = (bf16[64,1024]{1,0:T(8,128)(2,1)S(1)}, bf16[64,1024]{1,0:T(8,128)(2,1)S(1)}, u32[]{:S(2)}, u32[]{:S(2)}) collective-permute-start(bf16[64,1024]{1,0:T(8,128)(2,1)S(1)} %get-tuple-element.58), channel_id=1, source_target_pairs={{0,8},{8,0},{16,24},{24,16},{1,9},{9,1},{17,25},{25,17},{2,10},{10... | collective-permute-start | bytes 393224 | tf_op jit(solution)/shard_map/ppermute | solution.py:34
  61.0 4.3 %collective-permute-start.27 = (bf16[64,1024]{1,0:T(8,128)(2,1)S(1)}, bf16[64,1024]{1,0:T(8,128)(2,1)S(1)}, u32[]{:S(2)}, u32[]{:S(2)}) collective-permute-start(bf16[64,1024]{1,0:T(8,128)(2,1)S(1)} %get-tuple-element.56), channel_id=1, source_target_pairs={{0,8},{8,0},{16,24},{24,16},{1,9},{9,1},{17,25},{25,17},{2,10},{10... | collective-permute-start | bytes 393224 | tf_op jit(solution)/shard_map/ppermute | solution.py:34
  62.1 3.9 %collective-permute-start.24 = (bf16[64,1024]{1,0:T(8,128)(2,1)S(1)}, bf16[64,1024]{1,0:T(8,128)(2,1)S(1)}, u32[]{:S(2)}, u32[]{:S(2)}) collective-permute-start(bf16[64,1024]{1,0:T(8,128)(2,1)S(1)} %get-tuple-element.54), channel_id=1, source_target_pairs={{0,8},{8,0},{16,24},{24,16},{1,9},{9,1},{17,25},{25,17},{2,10},{10... | collective-permute-start | bytes 393224 | tf_op jit(solution)/shard_map/ppermute | solution.py:34
  63.6 4.0 %collective-permute-start.21 = (bf16[64,1024]{1,0:T(8,128)(2,1)S(1)}, bf16[64,1024]{1,0:T(8,128)(2,1)S(1)}, u32[]{:S(2)}, u32[]{:S(2)}) collective-permute-start(bf16[64,1024]{1,0:T(8,128)(2,1)S(1)} %get-tuple-element.52), channel_id=1, source_target_pairs={{0,8},{8,0},{16,24},{24,16},{1,9},{9,1},{17,25},{25,17},{2,10},{10... | collective-permute-start | bytes 393224 | tf_op jit(solution)/shard_map/ppermute | solution.py:34
  63.8 11.7 %collective-permute-start.31 = (bf16[32,1024]{1,0:T(8,128)(2,1)S(1)}, bf16[32,1024]{1,0:T(8,128)(2,1)S(1)}, u32[]{:S(2)}, u32[]{:S(2)}) collective-permute-start(bf16[32,1024]{1,0:T(8,128)(2,1)S(1)} %slice.47), channel_id=1, source_target_pairs={{0,16},{8,24},{16,0},{24,8},{1,17},{9,25},{17,1},{25,9},{2,18},{10... | collective-permute-start | bytes 196616 | tf_op jit(solution)/shard_map/ppermute | solution.py:34
  65.4 5.0 %collective-permute-start.28 = (bf16[32,1024]{1,0:T(8,128)(2,1)S(1)}, bf16[32,1024]{1,0:T(8,128)(2,1)S(1)}, u32[]{:S(2)}, u32[]{:S(2)}) collective-permute-start(bf16[32,1024]{1,0:T(8,128)(2,1)S(1)} %slice.45), channel_id=1, source_target_pairs={{0,16},{8,24},{16,0},{24,8},{1,17},{9,25},{17,1},{25,9},{2,18},{10... | collective-permute-start | bytes 196616 | tf_op jit(solution)/shard_map/ppermute | solution.py:34
  66.0 5.8 %collective-permute-start.25 = (bf16[32,1024]{1,0:T(8,128)(2,1)S(1)}, bf16[32,1024]{1,0:T(8,128)(2,1)S(1)}, u32[]{:S(2)}, u32[]{:S(2)}) collective-permute-start(bf16[32,1024]{1,0:T(8,128)(2,1)S(1)} %slice.43), channel_id=1, source_target_pairs={{0,16},{8,24},{16,0},{24,8},{1,17},{9,25},{17,1},{25,9},{2,18},{10... | collective-permute-start | bytes 196616 | tf_op jit(solution)/shard_map/ppermute | solution.py:34
  67.6 6.1 %collective-permute-start.22 = (bf16[32,1024]{1,0:T(8,128)(2,1)S(1)}, bf16[32,1024]{1,0:T(8,128)(2,1)S(1)}, u32[]{:S(2)}, u32[]{:S(2)}) collective-permute-start(bf16[32,1024]{1,0:T(8,128)(2,1)S(1)} %slice.41), channel_id=1, source_target_pairs={{0,16},{8,24},{16,0},{24,8},{1,17},{9,25},{17,1},{25,9},{2,18},{10... | collective-permute-start | bytes 196616 | tf_op jit(solution)/shard_map/ppermute | solution.py:34
  70.4 5.1 %collective-permute-start.29 = (bf16[32,1024]{1,0:T(8,128)(2,1)S(1)}, bf16[32,1024]{1,0:T(8,128)(2,1)S(1)}, u32[]{:S(2)}, u32[]{:S(2)}) collective-permute-start(bf16[32,1024]{1,0:T(8,128)(2,1)S(1)} %add_convert_fusion.6), channel_id=1, source_target_pairs={{0,1},{1,0},{2,3},{3,2},{4,5},{5,4},{6,7},{7,6},{8,9},{9,8},{10,11... | collective-permute-start | bytes 196616 | tf_op jit(solution)/shard_map/ppermute | solution.py:34
  71.8 6.8 %collective-permute-start.26 = (bf16[32,1024]{1,0:T(8,128)(2,1)S(1)}, bf16[32,1024]{1,0:T(8,128)(2,1)S(1)}, u32[]{:S(2)}, u32[]{:S(2)}) collective-permute-start(bf16[32,1024]{1,0:T(8,128)(2,1)S(1)} %add_convert_fusion.7), channel_id=1, source_target_pairs={{0,2},{1,3},{2,0},{3,1},{4,6},{5,7},{6,4},{7,5},{8,10},{9,11},{10,... | collective-permute-start | bytes 196616 | tf_op jit(solution)/shard_map/ppermute | solution.py:34
  73.8 6.2 %collective-permute-start.23 = (bf16[32,1024]{1,0:T(8,128)(2,1)S(1)}, bf16[32,1024]{1,0:T(8,128)(2,1)S(1)}, u32[]{:S(2)}, u32[]{:S(2)}) collective-permute-start(bf16[32,1024]{1,0:T(8,128)(2,1)S(1)} %add_convert_fusion.8), channel_id=1, source_target_pairs={{0,3},{1,2},{2,1},{3,0},{4,7},{5,6},{6,5},{7,4},{8,11},{9,10},{10,... | collective-permute-start | bytes 196616 | tf_op jit(solution)/shard_map/ppermute | solution.py:34
  80.1 4.0 %collective-permute-start.32 = (bf16[16,1024]{1,0:T(8,128)(2,1)S(1)}, bf16[16,1024]{1,0:T(8,128)(2,1)S(1)}, u32[]{:S(2)}, u32[]{:S(2)}) collective-permute-start(bf16[16,1024]{1,0:T(8,128)(2,1)S(1)} %get-tuple-element.60), channel_id=1, source_target_pairs={{0,4},{4,0},{1,5},{5,1},{2,6},{6,2},{3,7},{7,3},{8,12},{12,8},{9,1... | collective-permute-start | bytes 98312 | tf_op jit(solution)/shard_map/ppermute | solution.py:34
  84.1 4.4 %collective-permute-start.35 = (bf16[32,1024]{1,0:T(8,128)(2,1)S(1)}, bf16[32,1024]{1,0:T(8,128)(2,1)S(1)}, u32[]{:S(2)}, u32[]{:S(2)}) collective-permute-start(bf16[32,1024]{1,0:T(8,128)(2,1)S(1)} %pad_maximum_fusion.1.refs_0_), channel_id=1, source_target_pairs={{0,24},{8,16},{16,8},{24,0},{1,25},{9,17},{17,9},{25,1},{2,26},{10... | collective-permute-start | bytes 196616 | tf_op jit(solution)/shard_map/ppermute | solution.py:34
  84.1 5.5 %collective-permute-start.34 = (bf16[32,1024]{1,0:T(8,128)(2,1)S(1)}, bf16[32,1024]{1,0:T(8,128)(2,1)S(1)}, u32[]{:S(2)}, u32[]{:S(2)}) collective-permute-start(bf16[32,1024]{1,0:T(8,128)(2,1)S(1)} %pad_maximum_fusion.1.refs_0_), channel_id=1, source_target_pairs={{0,16},{8,24},{16,0},{24,8},{1,17},{9,25},{17,1},{25,9},{2,18},{10... | collective-permute-start | bytes 196616 | tf_op jit(solution)/shard_map/ppermute | solution.py:34
  85.4 4.1 %collective-permute-start.33 = (bf16[32,1024]{1,0:T(8,128)(2,1)S(1)}, bf16[32,1024]{1,0:T(8,128)(2,1)S(1)}, u32[]{:S(2)}, u32[]{:S(2)}) collective-permute-start(bf16[32,1024]{1,0:T(8,128)(2,1)S(1)} %pad_maximum_fusion.1.refs_0_), channel_id=1, source_target_pairs={{0,8},{8,0},{16,24},{24,16},{1,9},{9,1},{17,25},{25,17},{2,10},{10... | collective-permute-start | bytes 196616 | tf_op jit(solution)/shard_map/ppermute | solution.py:34

commit v3 on v2

--- a/solution.py
+++ b/solution.py
@@ -9,6 +9,7 @@
 
 
 BF16, F32 = jnp.bfloat16, jnp.float32
+HEAD = 53
 VMEM = pl.BlockSpec(memory_space=pltpu.VMEM)
 SMEM = pl.BlockSpec(memory_space=pltpu.SMEM)
 
@@ -34,7 +35,7 @@
     return lax.ppermute(x, axes, [(i, i ^ bit) for i in range(count)])
 
 
-def logits_body(tok_hbm, gain_hbm, phi_hbm, scaled_ref, part_ref, tok_ref, gain_ref, phi_ref, sems):
+def logits_body(tok_hbm, gain_hbm, phi_hbm, scaled_ref, part_ref, head_ref, tok_ref, gain_ref, phi_ref, sems):
     copies = [
         pltpu.make_async_copy(tok_hbm, tok_ref, sems.at[0]),
         pltpu.make_async_copy(phi_hbm, phi_ref, sems.at[1]),
@@ -47,25 +48,28 @@
     tok = tok_ref[0].astype(F32)
     scaled = (tok * gain_ref[...].astype(F32)).astype(BF16)
     scaled_ref[...] = scaled
-    slots = phi_ref.shape[1]
-    part = jnp.dot(scaled, phi_ref[...], preferred_element_type=F32)
-    part_ref[:slots] = part.T
+    part = jnp.dot(scaled, phi_ref[...], preferred_element_type=F32).T
     squares = jnp.sum(tok * tok, axis=1, keepdims=True)
-    part_ref[slots:] = jnp.broadcast_to(squares, (tok.shape[0], 128)).T[:8]
-
-
-def logits_of(part_refs, width):
-    total = part_refs[0][...]
-    for ref in part_refs[1:]:
+    part_ref[:8] = jnp.broadcast_to(squares, (tok.shape[0], 128)).T[:8]
+    part_ref[8:] = part
+    head = head_ref.shape[0]
+    head_ref[:8] = part_ref[:8]
+    head_ref[8:] = part[: head - 8]
+
+
+def logits_of(own_ref, near_ref, tail_ref, more_refs, width):
+    head = more_refs[0].shape[0] if more_refs else own_ref.shape[0]
+    total = own_ref[:head] + near_ref[:head]
+    for ref in more_refs:
         total = total + ref[...]
-    slots = total.shape[0] - 8
-    inv_rms = lax.rsqrt(total[slots : slots + 1] / width + 1e-06)
-    return total[:slots] * inv_rms, inv_rms
+    inv_rms = lax.rsqrt(total[:1] / width + 1e-06)
+    logits = jnp.concatenate([total[8:], tail_ref[...]], axis=0) if more_refs else total[8:]
+    return logits * inv_rms, inv_rms
 
 
 def slots_body(width, n, experts, batches, where_ref, *refs):
     part_refs, scaled_ref, message_refs, held = refs[:n], refs[n], refs[n + 1 : -1], refs[-1]
-    logits, inv_rms = logits_of(part_refs, width)
+    logits, inv_rms = logits_of(*part_refs[:3], part_refs[3:], width)
     top = jnp.max(logits, axis=1, keepdims=True)
     raised = jnp.exp(logits - top)
     total = jnp.sum(raised, axis=1, keepdims=True)
@@ -89,17 +93,21 @@
             message_refs[h * batches + r][...] = held[pl.ds(pl.multiple_of(at, rows), rows)]
 
 
+def slot_order(batches, experts):
+    near = [(r, 0) for r in range(batches)]
+    return near + [(r, h) for r in range(batches) for h in range(1, experts)]
+
+
 def combine_body(width, n, experts, batches, where_ref, *refs):
     part_refs, out_ref, held = refs[:n], refs[n], refs[n + 1]
-    logits, _ = logits_of(part_refs, width)
+    logits, _ = logits_of(*part_refs[:3], part_refs[3:], width)
     raised = jnp.exp(logits - jnp.max(logits, axis=0, keepdims=True))
     held[...] = raised / jnp.sum(raised, axis=0, keepdims=True)
     rows = logits.shape[0] // (experts * batches)
     blocks = []
-    for r in range(batches):
-        for h in range(experts):
-            at = ((where_ref[1] ^ h) * batches + (where_ref[0] ^ r)) * rows
-            blocks.append(held[pl.ds(pl.multiple_of(at, rows), rows)])
+    for r, h in slot_order(batches, experts):
+        at = ((where_ref[1] ^ h) * batches + (where_ref[0] ^ r)) * rows
+        blocks.append(held[pl.ds(pl.multiple_of(at, rows), rows)])
     out_ref[...] = jnp.concatenate(blocks, axis=0).T.astype(BF16)
 
 
@@ -189,11 +197,16 @@
     slots = phi.shape[1]
     rows = slots // (experts * batches)
 
-    scaled, part = pl.pallas_call(
+    head = 8 * max(1, (slots + 8) * HEAD // 800)
+    scaled, part, first = pl.pallas_call(
         logits_body,
-        out_shape=[shape((count, share), BF16), shape((slots + 8, count), F32)],
+        out_shape=[
+            shape((count, share), BF16),
+            shape((slots + 8, count), F32),
+            shape((head, count), F32),
+        ],
         in_specs=[pl.BlockSpec(memory_space=pltpu.HBM)] * 3,
-        out_specs=[VMEM, VMEM],
+        out_specs=[VMEM] * 3,
         scratch_shapes=[
             pltpu.VMEM(tokens.shape, BF16),
             pltpu.VMEM(gain.shape, BF16),
@@ -204,11 +217,18 @@
         compiler_params=pltpu.CompilerParams(vmem_limit_bytes=6 << 20),
         name="logits",
     )(*(pltpu.with_memory_space_constraint(x, pltpu.HBM) for x in (tokens, gain, phi)))
-    parts = [part] + [swap(part, "tensor", s) for s in range(1, tensors)]
+    near = swap(part, "tensor", 1)
+    tail = part[head:] + near[head:]
+    bit = 2
+    while bit < tensors:
+        tail = tail + swap(tail, "tensor", bit)
+        bit <<= 1
+    parts = [part, near, tail] + [swap(first, "tensor", s) for s in range(2, tensors)]
+    parts_count = len(parts)
     messages = pl.pallas_call(
-        functools.partial(slots_body, width, tensors, experts, batches),
+        functools.partial(slots_body, width, parts_count, experts, batches),
         out_shape=[shape((rows, share + 128), BF16)] * (experts * batches),
-        in_specs=[SMEM] + [VMEM] * (tensors + 1),
+        in_specs=[SMEM] + [VMEM] * (parts_count + 1),
         out_specs=[VMEM] * (experts * batches),
         scratch_shapes=[pltpu.VMEM((slots, share + 128), BF16)],
         cost_estimate=pl.CostEstimate(flops=1 << 30, bytes_accessed=1 << 22, transcendentals=0),
@@ -216,9 +236,9 @@
         name="slots",
     )(where, *parts, scaled)
     combine = pl.pallas_call(
-        functools.partial(combine_body, width, tensors, experts, batches),
+        functools.partial(combine_body, width, parts_count, experts, batches),
         out_shape=shape((count, slots), BF16),
-        in_specs=[SMEM] + [VMEM] * tensors,
+        in_specs=[SMEM] + [VMEM] * parts_count,
         out_specs=VMEM,
         scratch_shapes=[pltpu.VMEM((slots, count), F32)],
         cost_estimate=pl.CostEstimate(flops=1 << 30, bytes_accessed=1 << 22, transcendentals=0),
@@ -234,17 +254,23 @@
         shape((experts * rows, share), BF16),
         *arrived,
     )
-    w_gate, w_up, w_down = fetch(w_gate, w_up, w_down)
+    (w_gate,) = fetch(w_gate)
+    (w_up,) = fetch(w_up)
+    (w_down,) = fetch(w_down)
     hidden_share = w_gate.shape[2]
     all_rows = batches * experts * rows
     carry = []
-    for s in [0, *range(tensors - 1, 0, -1)]:
+    for s in [0, 1, *range(tensors - 1, 1, -1)][:tensors]:
         piece = own if s == 0 else swap(own, "tensor", s)
         bit = batches >> 1
         while bit > 1:
-            piece = jnp.concatenate([piece, swap(piece, "batch", bit)], axis=0)
+            if direct(batches, s):
+                other = swap(own, ("batch", "tensor"), bit * tensors + s)
+            else:
+                other = swap(piece, "batch", bit)
+            piece = jnp.concatenate([piece, other], axis=0)
             bit >>= 1
-        last = s == min(1, tensors - 1)
+        last = s == min(2, tensors - 1)
         carry = call(
             functools.partial(gate_up_body, s, last),
             shape((all_rows, hidden_share), BF16)
@@ -277,11 +303,18 @@
             bit <<= 1
         arrived.append(swap(total, "tensor", s) if s else total)
     total = add(*arrived)
-    pieces = [total[h * rows : (h + 1) * rows] for h in range(experts)]
-    pieces = [p if h == 0 else swap(p, "expert", h) for h, p in enumerate(pieces)]
-    out = jnp.concatenate(pieces, axis=0)
-    gathered = [out] + [swap(out, "batch", r) for r in range(1, batches)]
+    groups = [total[:rows]]
+    if experts > 1:
+        pieces = [swap(total[h * rows : (h + 1) * rows], "expert", h) for h in range(1, experts)]
+        groups.append(jnp.concatenate(pieces, axis=0))
+    gathered = []
+    for group in groups:
+        gathered += [group] + [swap(group, "batch", r) for r in range(1, batches)]
     return call(output_body, shape((count, share), BF16), combine, *gathered)[None]
+
+
+def direct(batches, s):
+    return s == 1 and batches == 4
 
 
 def solution(mesh):

time: 90.8 us -> 86.4 us (0.952)
  waiting for transfers between devices: 34.3 us -> 24.7 us
  starting transfers between devices: 34.8 us -> 37.8 us
  Pallas kernels: 20.9 us -> 22.9 us
    ppermute x36 -> x40, waiting for transfers between devices: 34.3 us -> 24.7 us  [swap(): return lax.ppermute(x, axes, [(i, i ^ bit) for i in range(count)])]
    ppermute x36 -> x40, starting transfers between devices: 34.8 us -> 37.8 us  [swap(): return lax.ppermute(x, axes, [(i, i ^ bit) for i in range(count)])]
    pallas_call x1 -> x3, Pallas kernels: 7.28 us -> 9.27 us  [fetch(): pl.pallas_call(fetch_body, out_shape=[pltpu.VMEM(a.shape, a.dtype) for a...]
  transfers between devices with their start and end apart: 36 -> 40, of which waited for: 14 -> 14; matrix products, arithmetic and copies ran while one was open for 0% -> 0% of each run, Pallas kernels for 16% -> 19%
where the time goes in v3:
time: 86.4 us; the launch traced here: 86.2 us
  starting transfers between devices  37.8 us (44%)
  waiting for transfers between devices  24.7 us (29%)
  Pallas kernels  22.9 us (27%)
    ppermute x40, starting transfers between devices, swap(): return lax.ppermute(x, axes, [(i, i ^ bit) for i in range(count)])  37.8 us
    ppermute x40, waiting for transfers between devices, swap(): return lax.ppermute(x, axes, [(i, i ^ bit) for i in range(count)])  24.7 us
    pallas_call x10, Pallas kernels, call(): pl.pallas_call(body, out_shape=shapes, in_specs=specs, out_specs=jax.tree...  10.4 us
    pallas_call x3, Pallas kernels, fetch(): pl.pallas_call(fetch_body, out_shape=[pltpu.VMEM(a.shape, a.dtype) for a...  9.27 us
  transfers between devices with their start and end apart: 40, of which 14 were waited for; matrix products, arithmetic and copies ran while one was open for 0% of the time, Pallas kernels for 19%

profile of v3, /device:TPU:0, one launch (start us, length us, event | category | flops | bytes accessed | tf_op | source)
XLA Modules:
  0.0 86.2 jit_solution(16146489700246405227)
XLA Ops:
  0.0 1.5 %logits.1 = (bf16[256,1024]{1,0:T(8,128)(2,1)S(1)}, f32[136,256]{1,0:T(8,128)S(1)}, f32[72,256]{1,0:T(8,128)S(1)}) custom-call(bf16[1,256,1024]{2,1,0:T(8,128)(2,1)} %tok_hbm.1, bf16[1024]{0:T(1024)(128)(2,1)} %gain_hbm.1, bf16[1024,128]{1,0:T(8,128)(2,1)} %phi_hbm.1), custom_call_target="tpu_custom_call" | custom-call | flops 1073741824 | bytes 4194304 | tf_op jit(solution)/shard_map/logits/pallas_call | solution.py:201
  1.5 3.1 %collective-permute-start = (f32[136,256]{1,0:T(8,128)S(1)}, f32[136,256]{1,0:T(8,128)S(1)}, u32[]{:S(2)}, u32[]{:S(2)}) collective-permute-start(f32[136,256]{1,0:T(8,128)S(1)} %get-tuple-element.30.refs_0_), channel_id=1, source_target_pairs={{0,1},{1,0},{2,3},{3,2},{4,5},{5,4},{6,7},{7,6},{8,9},{9,8},{10,11... | collective-permute-start | bytes 417800 | tf_op jit(solution)/shard_map/ppermute | solution.py:35
  4.6 2.6 %collective-permute-start.2 = (f32[72,256]{1,0:T(8,128)S(1)}, f32[72,256]{1,0:T(8,128)S(1)}, u32[]{:S(2)}, u32[]{:S(2)}) collective-permute-start(f32[72,256]{1,0:T(8,128)S(1)} %get-tuple-element.31), channel_id=1, source_target_pairs={{0,2},{1,3},{2,0},{3,1},{4,6},{5,7},{6,4},{7,5},{8,10},{9,11},{10,... | collective-permute-start | bytes 221192 | tf_op jit(solution)/shard_map/ppermute | solution.py:35
  7.2 1.9 %collective-permute-done.refs_1_ = f32[136,256]{1,0:T(8,128)S(1)} collective-permute-done((f32[136,256]{1,0:T(8,128)S(1)}, f32[136,256]{1,0:T(8,128)S(1)}, u32[]{:S(2)}, u32[]{:S(2)}) %collective-permute-start) | collective-permute-done | bytes 139296 | tf_op jit(solution)/shard_map/ppermute | solution.py:35
  9.1 3.2 %collective-permute-start.1 = (f32[64,256]{1,0:T(8,128)S(1)}, f32[64,256]{1,0:T(8,128)S(1)}, u32[]{:S(2)}, u32[]{:S(2)}) collective-permute-start(f32[64,256]{1,0:T(8,128)S(1)} %slice_add_fusion), channel_id=1, source_target_pairs={{0,2},{1,3},{2,0},{3,1},{4,6},{5,7},{6,4},{7,5},{8,10},{9,11},{10,... | collective-permute-start | bytes 196616 | tf_op jit(solution)/shard_map/ppermute | solution.py:35
  12.3 0.1 pad_add_fusion.where_ref
  12.4 5.0 %collective-permute-done.1 = f32[64,256]{1,0:T(8,128)S(1)} collective-permute-done((f32[64,256]{1,0:T(8,128)S(1)}, f32[64,256]{1,0:T(8,128)S(1)}, u32[]{:S(2)}, u32[]{:S(2)}) %collective-permute-start.1) | collective-permute-done | bytes 65568 | tf_op jit(solution)/shard_map/ppermute | solution.py:35
  17.4 1.0 %slots.1 = (bf16[16,1152]{1,0:T(8,128)(2,1)S(1)}, bf16[16,1152]{1,0:T(8,128)(2,1)S(1)}, bf16[16,1152]{1,0:T(8,128)(2,1)S(1)}, bf16[16,1152]{1,0:T(8,128)(2,1)S(1...) custom-call(s32[3]{0:T(128)S(1)} %pad_add_fusion.where_ref, ...), custom_call_target="tpu_custom_call" | custom-call | flops 1073741824 | bytes 4194304 | tf_op jit(solution)/shard_map/slots/pallas_call | solution.py:228
  18.3 1.0 %collective-permute-start.10 = (bf16[16,1152]{1,0:T(8,128)(2,1)S(1)}, bf16[16,1152]{1,0:T(8,128)(2,1)S(1)}, u32[]{:S(2)}, u32[]{:S(2)}) collective-permute-start(bf16[16,1152]{1,0:T(8,128)(2,1)S(1)} %get-tuple-element.40), channel_id=1, source_target_pairs={{0,28},{4,24},{8,20},{12,16},{16,12},{20,8},{24,4},{28,0},{1,29},{... | collective-permute-start | bytes 110600 | tf_op jit(solution)/shard_map/ppermute | solution.py:35
  19.4 1.6 %collective-permute-start.4 = (bf16[16,1152]{1,0:T(8,128)(2,1)S(1)}, bf16[16,1152]{1,0:T(8,128)(2,1)S(1)}, u32[]{:S(2)}, u32[]{:S(2)}) collective-permute-start(bf16[16,1152]{1,0:T(8,128)(2,1)S(1)} %get-tuple-element.34), channel_id=1, source_target_pairs={{0,8},{4,12},{8,0},{12,4},{16,24},{20,28},{24,16},{28,20},{1,9},{5... | collective-permute-start | bytes 110600 | tf_op jit(solution)/shard_map/ppermute | solution.py:35
  21.0 3.1 %fetch.3.refs_2_ = bf16[1,4096,896]{2,1,0:T(8,128)(2,1)S(1)} custom-call(bf16[1,4096,896]{2,1,0:T(8,128)(2,1)} %refs_0_.3), custom_call_target="tpu_custom_call" | custom-call | flops 1073741824 | bytes 33554432 | tf_op jit(solution)/shard_map/fetch/pallas_call | solution.py:173
  24.1 0.6 collective-permute-start.5
  24.6 0.8 collective-permute-start.6
  25.5 0.5 collective-permute-start.7
  26.0 1.6 %collective-permute-start.8 = (bf16[16,1152]{1,0:T(8,128)(2,1)S(1)}, bf16[16,1152]{1,0:T(8,128)(2,1)S(1)}, u32[]{:S(2)}, u32[]{:S(2)}) collective-permute-start(bf16[16,1152]{1,0:T(8,128)(2,1)S(1)} %get-tuple-element.38), channel_id=1, source_target_pairs={{0,12},{4,8},{8,4},{12,0},{16,28},{20,24},{24,20},{28,16},{1,13},{... | collective-permute-start | bytes 110600 | tf_op jit(solution)/shard_map/ppermute | solution.py:35
  27.6 0.5 collective-permute-start.9
  28.1 3.1 %fetch.4.refs_3_ = bf16[1,4096,896]{2,1,0:T(8,128)(2,1)S(1)} custom-call(bf16[1,4096,896]{2,1,0:T(8,128)(2,1)} %refs_0_.4), custom_call_target="tpu_custom_call" | custom-call | flops 1073741824 | bytes 33554432 | tf_op jit(solution)/shard_map/fetch/pallas_call | solution.py:173
  31.3 1.2 %collective-permute-done.9.refs_6_ = bf16[16,1152]{1,0:T(8,128)(2,1)S(1)} collective-permute-done((bf16[16,1152]{1,0:T(8,128)(2,1)S(1)}, bf16[16,1152]{1,0:T(8,128)(2,1)S(1)}, u32[]{:S(2)}, u32[]{:S(2)}) %collective-permute-start.9) | collective-permute-done | bytes 36896 | tf_op jit(solution)/shard_map/ppermute | solution.py:35
  32.5 0.2 shard_map.64
  32.7 0.6 collective-permute-start.20
  33.3 3.1 %fetch.5.down_ref = bf16[1,896,4096]{2,1,0:T(8,128)(2,1)S(1)} custom-call(bf16[1,896,4096]{2,1,0:T(8,128)(2,1)} %refs_0_.5), custom_call_target="tpu_custom_call" | custom-call | flops 1073741824 | bytes 33554432 | tf_op jit(solution)/shard_map/fetch/pallas_call | solution.py:173
  36.4 0.1 collective-permute-start.17
  36.5 3.0 %collective-permute-start.18 = (bf16[32,1024]{1,0:T(8,128)(2,1)S(1)}, bf16[32,1024]{1,0:T(8,128)(2,1)S(1)}, u32[]{:S(2)}, u32[]{:S(2)}) collective-permute-start(bf16[32,1024]{1,0:T(8,128)(2,1)S(1)} %shard_map.64), channel_id=1, source_target_pairs={{0,17},{1,16},{2,19},{3,18},{8,25},{9,24},{10,27},{11,26},{16,1},{... | collective-permute-start | bytes 196616 | tf_op jit(solution)/shard_map/ppermute | solution.py:35
  39.4 2.0 %collective-permute-start.14 = (bf16[32,1024]{1,0:T(8,128)(2,1)S(1)}, bf16[32,1024]{1,0:T(8,128)(2,1)S(1)}, u32[]{:S(2)}, u32[]{:S(2)}) collective-permute-start(bf16[32,1024]{1,0:T(8,128)(2,1)S(1)} %shard_map.64), channel_id=1, source_target_pairs={{0,3},{1,2},{2,1},{3,0},{4,7},{5,6},{6,5},{7,4},{8,11},{9,10},{10,... | collective-permute-start | bytes 196616 | tf_op jit(solution)/shard_map/ppermute | solution.py:35
  41.4 0.1 collective-permute-start.21
  41.5 0.8 collective-permute-done.18
  42.4 3.1 %collective-permute-done.14 = bf16[32,1024]{1,0:T(8,128)(2,1)S(1)} collective-permute-done((bf16[32,1024]{1,0:T(8,128)(2,1)S(1)}, bf16[32,1024]{1,0:T(8,128)(2,1)S(1)}, u32[]{:S(2)}, u32[]{:S(2)}) %collective-permute-start.14) | collective-permute-done | bytes 65568 | tf_op jit(solution)/shard_map/ppermute | solution.py:35
  45.5 0.5 collective-permute-start.15
  46.0 0.9 %collective-permute-done.11 = bf16[32,1024]{1,0:T(8,128)(2,1)S(1)} collective-permute-done((bf16[32,1024]{1,0:T(8,128)(2,1)S(1)}, bf16[32,1024]{1,0:T(8,128)(2,1)S(1)}, u32[]{:S(2)}, u32[]{:S(2)}) %collective-permute-start.11) | collective-permute-done | bytes 65568 | tf_op jit(solution)/shard_map/ppermute | solution.py:35
  46.9 1.0 %collective-permute-start.12 = (bf16[32,1024]{1,0:T(8,128)(2,1)S(1)}, bf16[32,1024]{1,0:T(8,128)(2,1)S(1)}, u32[]{:S(2)}, u32[]{:S(2)}) collective-permute-start(bf16[32,1024]{1,0:T(8,128)(2,1)S(1)} %collective-permute-done.11), channel_id=1, source_target_pairs={{0,16},{8,24},{16,0},{24,8},{1,17},{9,25},{17,1},{25,9},{2,18},{10... | collective-permute-start | bytes 196616 | tf_op jit(solution)/shard_map/ppermute | solution.py:35
  47.9 1.8 %collective-permute-done.15 = bf16[32,1024]{1,0:T(8,128)(2,1)S(1)} collective-permute-done((bf16[32,1024]{1,0:T(8,128)(2,1)S(1)}, bf16[32,1024]{1,0:T(8,128)(2,1)S(1)}, u32[]{:S(2)}, u32[]{:S(2)}) %collective-permute-start.15) | collective-permute-done | bytes 65568 | tf_op jit(solution)/shard_map/ppermute | solution.py:35
  49.8 1.4 %collective-permute-done.12 = bf16[32,1024]{1,0:T(8,128)(2,1)S(1)} collective-permute-done((bf16[32,1024]{1,0:T(8,128)(2,1)S(1)}, bf16[32,1024]{1,0:T(8,128)(2,1)S(1)}, u32[]{:S(2)}, u32[]{:S(2)}) %collective-permute-start.12) | collective-permute-done | bytes 65568 | tf_op jit(solution)/shard_map/ppermute | solution.py:35
  51.2 1.3 %shard_map.65 = (f32[128,896]{1,0:T(8,128)S(1)}, f32[128,896]{1,0:T(8,128)S(1)}) custom-call(s32[3]{0:T(128)S(1)} %pad_add_fusion.where_ref, bf16[64,1024]{1,0:T(8,128)(2,1)S(1)} %pad_maximum_fusion.refs_0_, bf16[64,1024]{1,0:T(8,128)(2,1)S(1)} %collective-permute-done.21.refs_1_, bf16[1,4096,896]{2,1,0:T(8,128)(2,1)S(1)} %fetch.3.refs_2_, ...), custom_call_target="tpu_custom_call" | custom-call | flops 469762048 | bytes 16777216 | tf_op jit(solution)/shard_map/pallas_call | solution.py:19
  52.5 1.3 %shard_map.66 = (f32[128,896]{1,0:T(8,128)S(1)}, f32[128,896]{1,0:T(8,128)S(1)}) custom-call(s32[3]{0:T(128)S(1)} %pad_add_fusion.where_ref, bf16[64,1024]{1,0:T(8,128)(2,1)S(1)} %constant_dynamic-update-slice_fusion.4.refs_0_, bf16[64,1024]{1,0:T(8,128)(2,1)S(1)} %collective-permute-done.19.refs_1_, bf16[1,4096,896]{2,1,0:T(8,128)(2,1)S(1)} %fetch.3.refs_2_, ...), custom_call_target="tpu_custom_call" | custom-call | flops 469762048 | bytes 16777216 | tf_op jit(solution)/shard_map/pallas_call | solution.py:19
  53.8 1.3 %shard_map.67 = (f32[128,896]{1,0:T(8,128)S(1)}, f32[128,896]{1,0:T(8,128)S(1)}) custom-call(s32[3]{0:T(128)S(1)} %pad_add_fusion.where_ref, bf16[64,1024]{1,0:T(8,128)(2,1)S(1)} %constant_dynamic-update-slice_fusion.2.refs_0_, bf16[64,1024]{1,0:T(8,128)(2,1)S(1)} %collective-permute-done.16.refs_1_, bf16[1,4096,896]{2,1,0:T(8,128)(2,1)S(1)} %fetch.3.refs_2_, ...), custom_call_target="tpu_custom_call" | custom-call | flops 469762048 | bytes 16777216 | tf_op jit(solution)/shard_map/pallas_call | solution.py:19
  55.1 1.3 %shard_map.68.hidden_ref = bf16[128,896]{1,0:T(8,128)(2,1)S(1)} custom-call(s32[3]{0:T(128)S(1)} %pad_add_fusion.where_ref, bf16[64,1024]{1,0:T(8,128)(2,1)S(1)} %constant_dynamic-update-slice_fusion.refs_0_, bf16[64,1024]{1,0:T(8,128)(2,1)S(1)} %collective-permute-done.13.refs_1_, bf16[1,4096,896]{2,1,0:T(8,128)(2,1)S(1)} %fetch.3.refs_2_, ...), custom_call_target="tpu_custom_call" | custom-call | flops 469762048 | bytes 16777216 | tf_op jit(solution)/shard_map/pallas_call | solution.py:19
  56.4 1.0 %shard_map.72 = (bf16[64,1024]{1,0:T(8,128)(2,1)S(1)}, bf16[64,1024]{1,0:T(8,128)(2,1)S(1)}) custom-call(s32[3]{0:T(128)S(1)} %pad_add_fusion.where_ref, bf16[128,896]{1,0:T(8,128)(2,1)S(1)} %shard_map.68.hidden_ref, bf16[1,896,4096]{2,1,0:T(8,128)(2,1)S(1)} %fetch.5.down_ref), custom_call_target="tpu_custom_call" | custom-call | flops 234881024 | bytes 8388608 | tf_op jit(solution)/shard_map/pallas_call | solution.py:19
  57.4 0.6 collective-permute-start.31
  58.0 1.0 %shard_map.69 = (bf16[64,1024]{1,0:T(8,128)(2,1)S(1)}, bf16[64,1024]{1,0:T(8,128)(2,1)S(1)}) custom-call(s32[3]{0:T(128)S(1)} %pad_add_fusion.where_ref, bf16[128,896]{1,0:T(8,128)(2,1)S(1)} %shard_map.68.hidden_ref, bf16[1,896,4096]{2,1,0:T(8,128)(2,1)S(1)} %fetch.5.down_ref), custom_call_target="tpu_custom_call" | custom-call | flops 234881024 | bytes 8388608 | tf_op jit(solution)/shard_map/pallas_call | solution.py:19
  59.0 0.1 collective-permute-start.22
  59.0 1.0 %shard_map.70 = (bf16[64,1024]{1,0:T(8,128)(2,1)S(1)}, bf16[64,1024]{1,0:T(8,128)(2,1)S(1)}) custom-call(s32[3]{0:T(128)S(1)} %pad_add_fusion.where_ref, bf16[128,896]{1,0:T(8,128)(2,1)S(1)} %shard_map.68.hidden_ref, bf16[1,896,4096]{2,1,0:T(8,128)(2,1)S(1)} %fetch.5.down_ref), custom_call_target="tpu_custom_call" | custom-call | flops 234881024 | bytes 8388608 | tf_op jit(solution)/shard_map/pallas_call | solution.py:19
  60.0 0.5 collective-permute-start.25
  60.6 1.0 %shard_map.71 = (bf16[64,1024]{1,0:T(8,128)(2,1)S(1)}, bf16[64,1024]{1,0:T(8,128)(2,1)S(1)}) custom-call(s32[3]{0:T(128)S(1)} %pad_add_fusion.where_ref, bf16[128,896]{1,0:T(8,128)(2,1)S(1)} %shard_map.68.hidden_ref, bf16[1,896,4096]{2,1,0:T(8,128)(2,1)S(1)} %fetch.5.down_ref), custom_call_target="tpu_custom_call" | custom-call | flops 234881024 | bytes 8388608 | tf_op jit(solution)/shard_map/pallas_call | solution.py:19
  61.6 0.1 collective-permute-start.28
  61.7 1.1 %collective-permute-start.32 = (bf16[32,1024]{1,0:T(8,128)(2,1)S(1)}, bf16[32,1024]{1,0:T(8,128)(2,1)S(1)}, u32[]{:S(2)}, u32[]{:S(2)}) collective-permute-start(bf16[32,1024]{1,0:T(8,128)(2,1)S(1)} %slice.56), channel_id=1, source_target_pairs={{0,16},{8,24},{16,0},{24,8},{1,17},{9,25},{17,1},{25,9},{2,18},{10... | collective-permute-start | bytes 196616 | tf_op jit(solution)/shard_map/ppermute | solution.py:35
  62.9 1.1 %collective-permute-start.23 = (bf16[32,1024]{1,0:T(8,128)(2,1)S(1)}, bf16[32,1024]{1,0:T(8,128)(2,1)S(1)}, u32[]{:S(2)}, u32[]{:S(2)}) collective-permute-start(bf16[32,1024]{1,0:T(8,128)(2,1)S(1)} %slice.50), channel_id=1, source_target_pairs={{0,16},{8,24},{16,0},{24,8},{1,17},{9,25},{17,1},{25,9},{2,18},{10... | collective-permute-start | bytes 196616 | tf_op jit(solution)/shard_map/ppermute | solution.py:35
  64.0 1.1 %collective-permute-start.26 = (bf16[32,1024]{1,0:T(8,128)(2,1)S(1)}, bf16[32,1024]{1,0:T(8,128)(2,1)S(1)}, u32[]{:S(2)}, u32[]{:S(2)}) collective-permute-start(bf16[32,1024]{1,0:T(8,128)(2,1)S(1)} %slice.52), channel_id=1, source_target_pairs={{0,16},{8,24},{16,0},{24,8},{1,17},{9,25},{17,1},{25,9},{2,18},{10... | collective-permute-start | bytes 196616 | tf_op jit(solution)/shard_map/ppermute | solution.py:35
  65.2 1.1 %collective-permute-start.29 = (bf16[32,1024]{1,0:T(8,128)(2,1)S(1)}, bf16[32,1024]{1,0:T(8,128)(2,1)S(1)}, u32[]{:S(2)}, u32[]{:S(2)}) collective-permute-start(bf16[32,1024]{1,0:T(8,128)(2,1)S(1)} %slice.54), channel_id=1, source_target_pairs={{0,16},{8,24},{16,0},{24,8},{1,17},{9,25},{17,1},{25,9},{2,18},{10... | collective-permute-start | bytes 196616 | tf_op jit(solution)/shard_map/ppermute | solution.py:35
  66.2 2.0 %collective-permute-done.23 = bf16[32,1024]{1,0:T(8,128)(2,1)S(1)} collective-permute-done((bf16[32,1024]{1,0:T(8,128)(2,1)S(1)}, bf16[32,1024]{1,0:T(8,128)(2,1)S(1)}, u32[]{:S(2)}, u32[]{:S(2)}) %collective-permute-start.23) | collective-permute-done | bytes 65568 | tf_op jit(solution)/shard_map/ppermute | solution.py:35
  68.2 2.0 %collective-permute-start.24 = (bf16[32,1024]{1,0:T(8,128)(2,1)S(1)}, bf16[32,1024]{1,0:T(8,128)(2,1)S(1)}, u32[]{:S(2)}, u32[]{:S(2)}) collective-permute-start(bf16[32,1024]{1,0:T(8,128)(2,1)S(1)} %add_convert_fusion.8), channel_id=1, source_target_pairs={{0,3},{1,2},{2,1},{3,0},{4,7},{5,6},{6,5},{7,4},{8,11},{9,10},{10,... | collective-permute-start | bytes 196616 | tf_op jit(solution)/shard_map/ppermute | solution.py:35
  70.3 0.7 collective-permute-start.27
  71.0 1.8 %collective-permute-start.30 = (bf16[32,1024]{1,0:T(8,128)(2,1)S(1)}, bf16[32,1024]{1,0:T(8,128)(2,1)S(1)}, u32[]{:S(2)}, u32[]{:S(2)}) collective-permute-start(bf16[32,1024]{1,0:T(8,128)(2,1)S(1)} %add_convert_fusion.6), channel_id=1, source_target_pairs={{0,1},{1,0},{2,3},{3,2},{4,5},{5,4},{6,7},{7,6},{8,9},{9,8},{10,11... | collective-permute-start | bytes 196616 | tf_op jit(solution)/shard_map/ppermute | solution.py:35
  72.8 1.9 %collective-permute-done.24 = bf16[32,1024]{1,0:T(8,128)(2,1)S(1)} collective-permute-done((bf16[32,1024]{1,0:T(8,128)(2,1)S(1)}, bf16[32,1024]{1,0:T(8,128)(2,1)S(1)}, u32[]{:S(2)}, u32[]{:S(2)}) %collective-permute-start.24) | collective-permute-done | bytes 65568 | tf_op jit(solution)/shard_map/ppermute | solution.py:35
  74.7 2.0 %collective-permute-done.27 = bf16[32,1024]{1,0:T(8,128)(2,1)S(1)} collective-permute-done((bf16[32,1024]{1,0:T(8,128)(2,1)S(1)}, bf16[32,1024]{1,0:T(8,128)(2,1)S(1)}, u32[]{:S(2)}, u32[]{:S(2)}) %collective-permute-start.27) | collective-permute-done | bytes 65568 | tf_op jit(solution)/shard_map/ppermute | solution.py:35
  76.8 1.2 %collective-permute-start.36 = (bf16[16,1024]{1,0:T(8,128)(2,1)S(1)}, bf16[16,1024]{1,0:T(8,128)(2,1)S(1)}, u32[]{:S(2)}, u32[]{:S(2)}) collective-permute-start(bf16[16,1024]{1,0:T(8,128)(2,1)S(1)} %get-tuple-element.55), channel_id=1, source_target_pairs={{0,4},{4,0},{1,5},{5,1},{2,6},{6,2},{3,7},{7,3},{8,12},{12,8},{9,1... | collective-permute-start | bytes 98312 | tf_op jit(solution)/shard_map/ppermute | solution.py:35
  78.0 1.1 %collective-permute-start.34 = (bf16[16,1024]{1,0:T(8,128)(2,1)S(1)}, bf16[16,1024]{1,0:T(8,128)(2,1)S(1)}, u32[]{:S(2)}, u32[]{:S(2)}) collective-permute-start(bf16[16,1024]{1,0:T(8,128)(2,1)S(1)} %get-tuple-element.56.refs_0_), channel_id=1, source_target_pairs={{0,16},{8,24},{16,0},{24,8},{1,17},{9,25},{17,1},{25,9},{2,18},{10... | collective-permute-start | bytes 98312 | tf_op jit(solution)/shard_map/ppermute | solution.py:35
  79.0 0.8 collective-permute-start.35
  79.8 0.9 %collective-permute-done.36.refs_4_ = bf16[16,1024]{1,0:T(8,128)(2,1)S(1)} collective-permute-done((bf16[16,1024]{1,0:T(8,128)(2,1)S(1)}, bf16[16,1024]{1,0:T(8,128)(2,1)S(1)}, u32[]{:S(2)}, u32[]{:S(2)}) %collective-permute-start.36) | collective-permute-done | bytes 32800 | tf_op jit(solution)/shard_map/ppermute | solution.py:35
  80.8 1.0 %collective-permute-start.38 = (bf16[16,1024]{1,0:T(8,128)(2,1)S(1)}, bf16[16,1024]{1,0:T(8,128)(2,1)S(1)}, u32[]{:S(2)}, u32[]{:S(2)}) collective-permute-start(bf16[16,1024]{1,0:T(8,128)(2,1)S(1)} %collective-permute-done.36.refs_4_), channel_id=1, source_target_pairs={{0,16},{8,24},{16,0},{24,8},{1,17},{9,25},{17,1},{25,9},{2,18},{10... | collective-permute-start | bytes 98312 | tf_op jit(solution)/shard_map/ppermute | solution.py:35
  81.8 0.9 collective-permute-start.39
  82.6 0.7 combine.1.combine_ref
  83.4 1.3 %collective-permute-done.38.refs_6_ = bf16[16,1024]{1,0:T(8,128)(2,1)S(1)} collective-permute-done((bf16[16,1024]{1,0:T(8,128)(2,1)S(1)}, bf16[16,1024]{1,0:T(8,128)(2,1)S(1)}, u32[]{:S(2)}, u32[]{:S(2)}) %collective-permute-start.38) | collective-permute-done | bytes 32800 | tf_op jit(solution)/shard_map/ppermute | solution.py:35
  84.7 0.4 collective-permute-done.39.refs_7_
  85.1 1.1 %shard_map.73 = bf16[256,1024]{1,0:T(8,128)(2,1)} custom-call(bf16[256,128]{1,0:T(8,128)(2,1)S(1)} %combine.1.combine_ref, bf16[16,1024]{1,0:T(8,128)(2,1)S(1)} %get-tuple-element.56.refs_0_, bf16[16,1024]{1,0:T(8,128)(2,1)S(1)} %collective-permute-done.33.refs_1_, bf16[16,1024]{1,0:T(8,128)(2,1)S(1)} %collective-permute-done.34.refs_2_, ...), custom_call_target="tpu_custom_call" | custom-call | flops 1073741824 | bytes 4194304 | tf_op jit(solution)/shard_map/pallas_call | solution.py:19
  (55 shorter events, 0.4 us)
Async XLA Ops:
  1.5 7.6 %collective-permute-start = (f32[136,256]{1,0:T(8,128)S(1)}, f32[136,256]{1,0:T(8,128)S(1)}, u32[]{:S(2)}, u32[]{:S(2)}) collective-permute-start(f32[136,256]{1,0:T(8,128)S(1)} %get-tuple-element.30.refs_0_), channel_id=1, source_target_pairs={{0,1},{1,0},{2,3},{3,2},{4,5},{5,4},{6,7},{7,6},{8,9},{9,8},{10,11... | collective-permute-start | bytes 417800 | tf_op jit(solution)/shard_map/ppermute | solution.py:35
  4.6 12.7 %collective-permute-start.2 = (f32[72,256]{1,0:T(8,128)S(1)}, f32[72,256]{1,0:T(8,128)S(1)}, u32[]{:S(2)}, u32[]{:S(2)}) collective-permute-start(f32[72,256]{1,0:T(8,128)S(1)} %get-tuple-element.31), channel_id=1, source_target_pairs={{0,2},{1,3},{2,0},{3,1},{4,6},{5,7},{6,4},{7,5},{8,10},{9,11},{10,... | collective-permute-start | bytes 221192 | tf_op jit(solution)/shard_map/ppermute | solution.py:35
  7.2 10.1 %collective-permute-start.3 = (f32[72,256]{1,0:T(8,128)S(1)}, f32[72,256]{1,0:T(8,128)S(1)}, u32[]{:S(2)}, u32[]{:S(2)}) collective-permute-start(f32[72,256]{1,0:T(8,128)S(1)} %get-tuple-element.31), channel_id=1, source_target_pairs={{0,3},{1,2},{2,1},{3,0},{4,7},{5,6},{6,5},{7,4},{8,11},{9,10},{10,... | collective-permute-start | bytes 221192 | tf_op jit(solution)/shard_map/ppermute | solution.py:35
  9.1 8.2 %collective-permute-start.1 = (f32[64,256]{1,0:T(8,128)S(1)}, f32[64,256]{1,0:T(8,128)S(1)}, u32[]{:S(2)}, u32[]{:S(2)}) collective-permute-start(f32[64,256]{1,0:T(8,128)S(1)} %slice_add_fusion), channel_id=1, source_target_pairs={{0,2},{1,3},{2,0},{3,1},{4,6},{5,7},{6,4},{7,5},{8,10},{9,11},{10,... | collective-permute-start | bytes 196616 | tf_op jit(solution)/shard_map/ppermute | solution.py:35
  18.3 7.7 %collective-permute-start.10 = (bf16[16,1152]{1,0:T(8,128)(2,1)S(1)}, bf16[16,1152]{1,0:T(8,128)(2,1)S(1)}, u32[]{:S(2)}, u32[]{:S(2)}) collective-permute-start(bf16[16,1152]{1,0:T(8,128)(2,1)S(1)} %get-tuple-element.40), channel_id=1, source_target_pairs={{0,28},{4,24},{8,20},{12,16},{16,12},{20,8},{24,4},{28,0},{1,29},{... | collective-permute-start | bytes 110600 | tf_op jit(solution)/shard_map/ppermute | solution.py:35
  19.4 8.3 %collective-permute-start.4 = (bf16[16,1152]{1,0:T(8,128)(2,1)S(1)}, bf16[16,1152]{1,0:T(8,128)(2,1)S(1)}, u32[]{:S(2)}, u32[]{:S(2)}) collective-permute-start(bf16[16,1152]{1,0:T(8,128)(2,1)S(1)} %get-tuple-element.34), channel_id=1, source_target_pairs={{0,8},{4,12},{8,0},{12,4},{16,24},{20,28},{24,16},{28,20},{1,9},{5... | collective-permute-start | bytes 110600 | tf_op jit(solution)/shard_map/ppermute | solution.py:35
  24.1 7.1 %collective-permute-start.5 = (bf16[16,1152]{1,0:T(8,128)(2,1)S(1)}, bf16[16,1152]{1,0:T(8,128)(2,1)S(1)}, u32[]{:S(2)}, u32[]{:S(2)}) collective-permute-start(bf16[16,1152]{1,0:T(8,128)(2,1)S(1)} %get-tuple-element.35), channel_id=1, source_target_pairs={{0,16},{4,20},{8,24},{12,28},{16,0},{20,4},{24,8},{28,12},{1,17},{... | collective-permute-start | bytes 110600 | tf_op jit(solution)/shard_map/ppermute | solution.py:35
  24.6 6.6 %collective-permute-start.6 = (bf16[16,1152]{1,0:T(8,128)(2,1)S(1)}, bf16[16,1152]{1,0:T(8,128)(2,1)S(1)}, u32[]{:S(2)}, u32[]{:S(2)}) collective-permute-start(bf16[16,1152]{1,0:T(8,128)(2,1)S(1)} %get-tuple-element.36), channel_id=1, source_target_pairs={{0,24},{4,28},{8,16},{12,20},{16,8},{20,12},{24,0},{28,4},{1,25},{... | collective-permute-start | bytes 110600 | tf_op jit(solution)/shard_map/ppermute | solution.py:35
  25.5 5.7 %collective-permute-start.7 = (bf16[16,1152]{1,0:T(8,128)(2,1)S(1)}, bf16[16,1152]{1,0:T(8,128)(2,1)S(1)}, u32[]{:S(2)}, u32[]{:S(2)}) collective-permute-start(bf16[16,1152]{1,0:T(8,128)(2,1)S(1)} %get-tuple-element.37), channel_id=1, source_target_pairs={{0,4},{4,0},{8,12},{12,8},{16,20},{20,16},{24,28},{28,24},{1,5},{5... | collective-permute-start | bytes 110600 | tf_op jit(solution)/shard_map/ppermute | solution.py:35
  26.0 5.2 %collective-permute-start.8 = (bf16[16,1152]{1,0:T(8,128)(2,1)S(1)}, bf16[16,1152]{1,0:T(8,128)(2,1)S(1)}, u32[]{:S(2)}, u32[]{:S(2)}) collective-permute-start(bf16[16,1152]{1,0:T(8,128)(2,1)S(1)} %get-tuple-element.38), channel_id=1, source_target_pairs={{0,12},{4,8},{8,4},{12,0},{16,28},{20,24},{24,20},{28,16},{1,13},{... | collective-permute-start | bytes 110600 | tf_op jit(solution)/shard_map/ppermute | solution.py:35
  27.6 4.9 %collective-permute-start.9 = (bf16[16,1152]{1,0:T(8,128)(2,1)S(1)}, bf16[16,1152]{1,0:T(8,128)(2,1)S(1)}, u32[]{:S(2)}, u32[]{:S(2)}) collective-permute-start(bf16[16,1152]{1,0:T(8,128)(2,1)S(1)} %get-tuple-element.39), channel_id=1, source_target_pairs={{0,20},{4,16},{8,28},{12,24},{16,4},{20,0},{24,12},{28,8},{1,21},{... | collective-permute-start | bytes 110600 | tf_op jit(solution)/shard_map/ppermute | solution.py:35
  32.7 8.7 %collective-permute-start.20 = (bf16[32,1024]{1,0:T(8,128)(2,1)S(1)}, bf16[32,1024]{1,0:T(8,128)(2,1)S(1)}, u32[]{:S(2)}, u32[]{:S(2)}) collective-permute-start(bf16[32,1024]{1,0:T(8,128)(2,1)S(1)} %shard_map.64), channel_id=1, source_target_pairs={{0,16},{8,24},{16,0},{24,8},{1,17},{9,25},{17,1},{25,9},{2,18},{10... | collective-permute-start | bytes 196616 | tf_op jit(solution)/shard_map/ppermute | solution.py:35
  36.4 5.1 %collective-permute-start.17 = (bf16[32,1024]{1,0:T(8,128)(2,1)S(1)}, bf16[32,1024]{1,0:T(8,128)(2,1)S(1)}, u32[]{:S(2)}, u32[]{:S(2)}) collective-permute-start(bf16[32,1024]{1,0:T(8,128)(2,1)S(1)} %shard_map.64), channel_id=1, source_target_pairs={{0,1},{1,0},{2,3},{3,2},{4,5},{5,4},{6,7},{7,6},{8,9},{9,8},{10,11... | collective-permute-start | bytes 196616 | tf_op jit(solution)/shard_map/ppermute | solution.py:35
  36.5 5.9 %collective-permute-start.18 = (bf16[32,1024]{1,0:T(8,128)(2,1)S(1)}, bf16[32,1024]{1,0:T(8,128)(2,1)S(1)}, u32[]{:S(2)}, u32[]{:S(2)}) collective-permute-start(bf16[32,1024]{1,0:T(8,128)(2,1)S(1)} %shard_map.64), channel_id=1, source_target_pairs={{0,17},{1,16},{2,19},{3,18},{8,25},{9,24},{10,27},{11,26},{16,1},{... | collective-permute-start | bytes 196616 | tf_op jit(solution)/shard_map/ppermute | solution.py:35
  39.4 6.1 %collective-permute-start.14 = (bf16[32,1024]{1,0:T(8,128)(2,1)S(1)}, bf16[32,1024]{1,0:T(8,128)(2,1)S(1)}, u32[]{:S(2)}, u32[]{:S(2)}) collective-permute-start(bf16[32,1024]{1,0:T(8,128)(2,1)S(1)} %shard_map.64), channel_id=1, source_target_pairs={{0,3},{1,2},{2,1},{3,0},{4,7},{5,6},{6,5},{7,4},{8,11},{9,10},{10,... | collective-permute-start | bytes 196616 | tf_op jit(solution)/shard_map/ppermute | solution.py:35
  41.4 5.5 %collective-permute-start.11 = (bf16[32,1024]{1,0:T(8,128)(2,1)S(1)}, bf16[32,1024]{1,0:T(8,128)(2,1)S(1)}, u32[]{:S(2)}, u32[]{:S(2)}) collective-permute-start(bf16[32,1024]{1,0:T(8,128)(2,1)S(1)} %shard_map.64), channel_id=1, source_target_pairs={{0,2},{1,3},{2,0},{3,1},{4,6},{5,7},{6,4},{7,5},{8,10},{9,11},{10,... | collective-permute-start | bytes 196616 | tf_op jit(solution)/shard_map/ppermute | solution.py:35
  41.4 9.8 %collective-permute-start.21 = (bf16[64,1024]{1,0:T(8,128)(2,1)S(1)}, bf16[64,1024]{1,0:T(8,128)(2,1)S(1)}, u32[]{:S(2)}, u32[]{:S(2)}) collective-permute-start(bf16[64,1024]{1,0:T(8,128)(2,1)S(1)} %pad_maximum_fusion.refs_0_), channel_id=1, source_target_pairs={{0,8},{8,0},{16,24},{24,16},{1,9},{9,1},{17,25},{25,17},{2,10},{10... | collective-permute-start | bytes 393224 | tf_op jit(solution)/shard_map/ppermute | solution.py:35
  42.4 10.1 %collective-permute-start.19 = (bf16[64,1024]{1,0:T(8,128)(2,1)S(1)}, bf16[64,1024]{1,0:T(8,128)(2,1)S(1)}, u32[]{:S(2)}, u32[]{:S(2)}) collective-permute-start(bf16[64,1024]{1,0:T(8,128)(2,1)S(1)} %constant_dynamic-update-slice_fusion.4.refs_0_), channel_id=1, source_target_pairs={{0,8},{8,0},{16,24},{24,16},{1,9},{9,1},{17,25},{25,17},{2,10},{10... | collective-permute-start | bytes 393224 | tf_op jit(solution)/shard_map/ppermute | solution.py:35
  45.5 4.3 %collective-permute-start.15 = (bf16[32,1024]{1,0:T(8,128)(2,1)S(1)}, bf16[32,1024]{1,0:T(8,128)(2,1)S(1)}, u32[]{:S(2)}, u32[]{:S(2)}) collective-permute-start(bf16[32,1024]{1,0:T(8,128)(2,1)S(1)} %collective-permute-done.14), channel_id=1, source_target_pairs={{0,16},{8,24},{16,0},{24,8},{1,17},{9,25},{17,1},{25,9},{2,18},{10... | collective-permute-start | bytes 196616 | tf_op jit(solution)/shard_map/ppermute | solution.py:35
  46.9 4.3 %collective-permute-start.12 = (bf16[32,1024]{1,0:T(8,128)(2,1)S(1)}, bf16[32,1024]{1,0:T(8,128)(2,1)S(1)}, u32[]{:S(2)}, u32[]{:S(2)}) collective-permute-start(bf16[32,1024]{1,0:T(8,128)(2,1)S(1)} %collective-permute-done.11), channel_id=1, source_target_pairs={{0,16},{8,24},{16,0},{24,8},{1,17},{9,25},{17,1},{25,9},{2,18},{10... | collective-permute-start | bytes 196616 | tf_op jit(solution)/shard_map/ppermute | solution.py:35
  49.8 4.0 %collective-permute-start.16 = (bf16[64,1024]{1,0:T(8,128)(2,1)S(1)}, bf16[64,1024]{1,0:T(8,128)(2,1)S(1)}, u32[]{:S(2)}, u32[]{:S(2)}) collective-permute-start(bf16[64,1024]{1,0:T(8,128)(2,1)S(1)} %constant_dynamic-update-slice_fusion.2.refs_0_), channel_id=1, source_target_pairs={{0,8},{8,0},{16,24},{24,16},{1,9},{9,1},{17,25},{25,17},{2,10},{10... | collective-permute-start | bytes 393224 | tf_op jit(solution)/shard_map/ppermute | solution.py:35
  51.2 3.9 %collective-permute-start.13 = (bf16[64,1024]{1,0:T(8,128)(2,1)S(1)}, bf16[64,1024]{1,0:T(8,128)(2,1)S(1)}, u32[]{:S(2)}, u32[]{:S(2)}) collective-permute-start(bf16[64,1024]{1,0:T(8,128)(2,1)S(1)} %constant_dynamic-update-slice_fusion.refs_0_), channel_id=1, source_target_pairs={{0,8},{8,0},{16,24},{24,16},{1,9},{9,1},{17,25},{25,17},{2,10},{10... | collective-permute-start | bytes 393224 | tf_op jit(solution)/shard_map/ppermute | solution.py:35
  57.4 4.3 %collective-permute-start.31 = (bf16[64,1024]{1,0:T(8,128)(2,1)S(1)}, bf16[64,1024]{1,0:T(8,128)(2,1)S(1)}, u32[]{:S(2)}, u32[]{:S(2)}) collective-permute-start(bf16[64,1024]{1,0:T(8,128)(2,1)S(1)} %get-tuple-element.54), channel_id=1, source_target_pairs={{0,8},{8,0},{16,24},{24,16},{1,9},{9,1},{17,25},{25,17},{2,10},{10... | collective-permute-start | bytes 393224 | tf_op jit(solution)/shard_map/ppermute | solution.py:35
  59.0 3.9 %collective-permute-start.22 = (bf16[64,1024]{1,0:T(8,128)(2,1)S(1)}, bf16[64,1024]{1,0:T(8,128)(2,1)S(1)}, u32[]{:S(2)}, u32[]{:S(2)}) collective-permute-start(bf16[64,1024]{1,0:T(8,128)(2,1)S(1)} %get-tuple-element.48), channel_id=1, source_target_pairs={{0,8},{8,0},{16,24},{24,16},{1,9},{9,1},{17,25},{25,17},{2,10},{10... | collective-permute-start | bytes 393224 | tf_op jit(solution)/shard_map/ppermute | solution.py:35
  60.0 3.9 %collective-permute-start.25 = (bf16[64,1024]{1,0:T(8,128)(2,1)S(1)}, bf16[64,1024]{1,0:T(8,128)(2,1)S(1)}, u32[]{:S(2)}, u32[]{:S(2)}) collective-permute-start(bf16[64,1024]{1,0:T(8,128)(2,1)S(1)} %get-tuple-element.50), channel_id=1, source_target_pairs={{0,8},{8,0},{16,24},{24,16},{1,9},{9,1},{17,25},{25,17},{2,10},{10... | collective-permute-start | bytes 393224 | tf_op jit(solution)/shard_map/ppermute | solution.py:35
  61.6 3.5 %collective-permute-start.28 = (bf16[64,1024]{1,0:T(8,128)(2,1)S(1)}, bf16[64,1024]{1,0:T(8,128)(2,1)S(1)}, u32[]{:S(2)}, u32[]{:S(2)}) collective-permute-start(bf16[64,1024]{1,0:T(8,128)(2,1)S(1)} %get-tuple-element.52), channel_id=1, source_target_pairs={{0,8},{8,0},{16,24},{24,16},{1,9},{9,1},{17,25},{25,17},{2,10},{10... | collective-permute-start | bytes 393224 | tf_op jit(solution)/shard_map/ppermute | solution.py:35
  61.7 11.1 %collective-permute-start.32 = (bf16[32,1024]{1,0:T(8,128)(2,1)S(1)}, bf16[32,1024]{1,0:T(8,128)(2,1)S(1)}, u32[]{:S(2)}, u32[]{:S(2)}) collective-permute-start(bf16[32,1024]{1,0:T(8,128)(2,1)S(1)} %slice.56), channel_id=1, source_target_pairs={{0,16},{8,24},{16,0},{24,8},{1,17},{9,25},{17,1},{25,9},{2,18},{10... | collective-permute-start | bytes 196616 | tf_op jit(solution)/shard_map/ppermute | solution.py:35
  62.9 5.3 %collective-permute-start.23 = (bf16[32,1024]{1,0:T(8,128)(2,1)S(1)}, bf16[32,1024]{1,0:T(8,128)(2,1)S(1)}, u32[]{:S(2)}, u32[]{:S(2)}) collective-permute-start(bf16[32,1024]{1,0:T(8,128)(2,1)S(1)} %slice.50), channel_id=1, source_target_pairs={{0,16},{8,24},{16,0},{24,8},{1,17},{9,25},{17,1},{25,9},{2,18},{10... | collective-permute-start | bytes 196616 | tf_op jit(solution)/shard_map/ppermute | solution.py:35
  64.0 6.2 %collective-permute-start.26 = (bf16[32,1024]{1,0:T(8,128)(2,1)S(1)}, bf16[32,1024]{1,0:T(8,128)(2,1)S(1)}, u32[]{:S(2)}, u32[]{:S(2)}) collective-permute-start(bf16[32,1024]{1,0:T(8,128)(2,1)S(1)} %slice.52), channel_id=1, source_target_pairs={{0,16},{8,24},{16,0},{24,8},{1,17},{9,25},{17,1},{25,9},{2,18},{10... | collective-permute-start | bytes 196616 | tf_op jit(solution)/shard_map/ppermute | solution.py:35
  65.2 5.8 %collective-permute-start.29 = (bf16[32,1024]{1,0:T(8,128)(2,1)S(1)}, bf16[32,1024]{1,0:T(8,128)(2,1)S(1)}, u32[]{:S(2)}, u32[]{:S(2)}) collective-permute-start(bf16[32,1024]{1,0:T(8,128)(2,1)S(1)} %slice.54), channel_id=1, source_target_pairs={{0,16},{8,24},{16,0},{24,8},{1,17},{9,25},{17,1},{25,9},{2,18},{10... | collective-permute-start | bytes 196616 | tf_op jit(solution)/shard_map/ppermute | solution.py:35
  68.2 6.5 %collective-permute-start.24 = (bf16[32,1024]{1,0:T(8,128)(2,1)S(1)}, bf16[32,1024]{1,0:T(8,128)(2,1)S(1)}, u32[]{:S(2)}, u32[]{:S(2)}) collective-permute-start(bf16[32,1024]{1,0:T(8,128)(2,1)S(1)} %add_convert_fusion.8), channel_id=1, source_target_pairs={{0,3},{1,2},{2,1},{3,0},{4,7},{5,6},{6,5},{7,4},{8,11},{9,10},{10,... | collective-permute-start | bytes 196616 | tf_op jit(solution)/shard_map/ppermute | solution.py:35
  70.3 6.4 %collective-permute-start.27 = (bf16[32,1024]{1,0:T(8,128)(2,1)S(1)}, bf16[32,1024]{1,0:T(8,128)(2,1)S(1)}, u32[]{:S(2)}, u32[]{:S(2)}) collective-permute-start(bf16[32,1024]{1,0:T(8,128)(2,1)S(1)} %add_convert_fusion.7), channel_id=1, source_target_pairs={{0,2},{1,3},{2,0},{3,1},{4,6},{5,7},{6,4},{7,5},{8,10},{9,11},{10,... | collective-permute-start | bytes 196616 | tf_op jit(solution)/shard_map/ppermute | solution.py:35
  71.0 5.7 %collective-permute-start.30 = (bf16[32,1024]{1,0:T(8,128)(2,1)S(1)}, bf16[32,1024]{1,0:T(8,128)(2,1)S(1)}, u32[]{:S(2)}, u32[]{:S(2)}) collective-permute-start(bf16[32,1024]{1,0:T(8,128)(2,1)S(1)} %add_convert_fusion.6), channel_id=1, source_target_pairs={{0,1},{1,0},{2,3},{3,2},{4,5},{5,4},{6,7},{7,6},{8,9},{9,8},{10,11... | collective-permute-start | bytes 196616 | tf_op jit(solution)/shard_map/ppermute | solution.py:35
  76.8 4.0 %collective-permute-start.36 = (bf16[16,1024]{1,0:T(8,128)(2,1)S(1)}, bf16[16,1024]{1,0:T(8,128)(2,1)S(1)}, u32[]{:S(2)}, u32[]{:S(2)}) collective-permute-start(bf16[16,1024]{1,0:T(8,128)(2,1)S(1)} %get-tuple-element.55), channel_id=1, source_target_pairs={{0,4},{4,0},{1,5},{5,1},{2,6},{6,2},{3,7},{7,3},{8,12},{12,8},{9,1... | collective-permute-start | bytes 98312 | tf_op jit(solution)/shard_map/ppermute | solution.py:35
  77.9 3.8 %collective-permute-start.33 = (bf16[16,1024]{1,0:T(8,128)(2,1)S(1)}, bf16[16,1024]{1,0:T(8,128)(2,1)S(1)}, u32[]{:S(2)}, u32[]{:S(2)}) collective-permute-start(bf16[16,1024]{1,0:T(8,128)(2,1)S(1)} %get-tuple-element.56.refs_0_), channel_id=1, source_target_pairs={{0,8},{8,0},{16,24},{24,16},{1,9},{9,1},{17,25},{25,17},{2,10},{10... | collective-permute-start | bytes 98312 | tf_op jit(solution)/shard_map/ppermute | solution.py:35
  78.0 5.4 %collective-permute-start.34 = (bf16[16,1024]{1,0:T(8,128)(2,1)S(1)}, bf16[16,1024]{1,0:T(8,128)(2,1)S(1)}, u32[]{:S(2)}, u32[]{:S(2)}) collective-permute-start(bf16[16,1024]{1,0:T(8,128)(2,1)S(1)} %get-tuple-element.56.refs_0_), channel_id=1, source_target_pairs={{0,16},{8,24},{16,0},{24,8},{1,17},{9,25},{17,1},{25,9},{2,18},{10... | collective-permute-start | bytes 98312 | tf_op jit(solution)/shard_map/ppermute | solution.py:35
  79.0 4.3 %collective-permute-start.35 = (bf16[16,1024]{1,0:T(8,128)(2,1)S(1)}, bf16[16,1024]{1,0:T(8,128)(2,1)S(1)}, u32[]{:S(2)}, u32[]{:S(2)}) collective-permute-start(bf16[16,1024]{1,0:T(8,128)(2,1)S(1)} %get-tuple-element.56.refs_0_), channel_id=1, source_target_pairs={{0,24},{8,16},{16,8},{24,0},{1,25},{9,17},{17,9},{25,1},{2,26},{10... | collective-permute-start | bytes 98312 | tf_op jit(solution)/shard_map/ppermute | solution.py:35
  80.7 2.6 %collective-permute-start.37 = (bf16[16,1024]{1,0:T(8,128)(2,1)S(1)}, bf16[16,1024]{1,0:T(8,128)(2,1)S(1)}, u32[]{:S(2)}, u32[]{:S(2)}) collective-permute-start(bf16[16,1024]{1,0:T(8,128)(2,1)S(1)} %collective-permute-done.36.refs_4_), channel_id=1, source_target_pairs={{0,8},{8,0},{16,24},{24,16},{1,9},{9,1},{17,25},{25,17},{2,10},{10... | collective-permute-start | bytes 98312 | tf_op jit(solution)/shard_map/ppermute | solution.py:35
  80.8 3.9 %collective-permute-start.38 = (bf16[16,1024]{1,0:T(8,128)(2,1)S(1)}, bf16[16,1024]{1,0:T(8,128)(2,1)S(1)}, u32[]{:S(2)}, u32[]{:S(2)}) collective-permute-start(bf16[16,1024]{1,0:T(8,128)(2,1)S(1)} %collective-permute-done.36.refs_4_), channel_id=1, source_target_pairs={{0,16},{8,24},{16,0},{24,8},{1,17},{9,25},{17,1},{25,9},{2,18},{10... | collective-permute-start | bytes 98312 | tf_op jit(solution)/shard_map/ppermute | solution.py:35
  81.8 3.3 %collective-permute-start.39 = (bf16[16,1024]{1,0:T(8,128)(2,1)S(1)}, bf16[16,1024]{1,0:T(8,128)(2,1)S(1)}, u32[]{:S(2)}, u32[]{:S(2)}) collective-permute-start(bf16[16,1024]{1,0:T(8,128)(2,1)S(1)} %collective-permute-done.36.refs_4_), channel_id=1, source_target_pairs={{0,24},{8,16},{16,8},{24,0},{1,25},{9,17},{17,9},{25,1},{2,26},{10... | collective-permute-start | bytes 98312 | tf_op jit(solution)/shard_map/ppermute | solution.py:35

commit v4 on v3

--- a/solution.py
+++ b/solution.py
@@ -67,8 +67,24 @@
     return logits * inv_rms, inv_rms
 
 
+def mass_of(piece, share):
+    lanes = [piece[:, share + i : share + i + 1].astype(F32) for i in range(3)]
+    return lanes[0] + lanes[1] + lanes[2]
+
+
+def mass_lanes(mass, lanes):
+    high = mass.astype(BF16).astype(F32)
+    middle = (mass - high).astype(BF16).astype(F32)
+    low = mass - high - middle
+    lane = lax.broadcasted_iota(jnp.int32, (mass.shape[0], lanes), 1)
+    stats = jnp.where(
+        lane == 0, high, jnp.where(lane == 1, middle, jnp.where(lane == 2, low, 0.0))
+    )
+    return stats.astype(BF16)
+
+
 def slots_body(width, n, experts, batches, where_ref, *refs):
-    part_refs, scaled_ref, message_refs, held = refs[:n], refs[n], refs[n + 1 : -1], refs[-1]
+    part_refs, scaled_ref, keep_ref, send_ref, held = refs[:n], refs[n], *refs[n + 1 :]
     logits, inv_rms = logits_of(*part_refs[:3], part_refs[3:], width)
     top = jnp.max(logits, axis=1, keepdims=True)
     raised = jnp.exp(logits - top)
@@ -78,19 +94,28 @@
     rows = held.shape[0] // (experts * batches)
     slot = jnp.dot(weights, scaled_ref[...], preferred_element_type=F32)
     held[:, :share] = slot.astype(BF16)
-    mass = top + jnp.log(total)
-    high = mass.astype(BF16).astype(F32)
-    middle = (mass - high).astype(BF16).astype(F32)
-    low = mass - high - middle
-    lane = lax.broadcasted_iota(jnp.int32, (held.shape[0], held.shape[1] - share), 1)
-    stats = jnp.where(
-        lane == 0, high, jnp.where(lane == 1, middle, jnp.where(lane == 2, low, 0.0))
-    )
-    held[:, share:] = stats.astype(BF16)
+    held[:, share:] = mass_lanes(top + jnp.log(total), held.shape[1] - share)
     for h in range(experts):
         for r in range(batches):
             at = ((where_ref[1] ^ h) * batches + (where_ref[0] ^ r)) * rows
-            message_refs[h * batches + r][...] = held[pl.ds(pl.multiple_of(at, rows), rows)]
+            to = (h * (batches // 2) + r // 2) * rows
+            target = send_ref if r % 2 else keep_ref
+            target[to : to + rows] = held[pl.ds(pl.multiple_of(at, rows), rows)]
+
+
+def merge_body(share, keep_ref, came_ref, *out_refs):
+    one, two = keep_ref[...], came_ref[...]
+    mass = [mass_of(p, share) for p in (one, two)]
+    top = jnp.maximum(*mass)
+    raised = [jnp.exp(m - top) for m in mass]
+    total = raised[0] + raised[1]
+    both = one[:, :share].astype(F32) * (raised[0] / total)
+    both = (both + two[:, :share].astype(F32) * (raised[1] / total)).astype(BF16)
+    lanes = mass_lanes(top + jnp.log(total), one.shape[1] - share)
+    rows = out_refs[0].shape[0]
+    for i, ref in enumerate(out_refs):
+        ref[:, :share] = both[i * rows : (i + 1) * rows]
+        ref[:, share:] = lanes[i * rows : (i + 1) * rows]
 
 
 def slot_order(batches, experts):
@@ -111,19 +136,16 @@
     out_ref[...] = jnp.concatenate(blocks, axis=0).T.astype(BF16)
 
 
-def gather_body(groups, batches, *refs):
+def gather_body(groups, count, *refs):
     out_ref = refs[-1]
     rows, share = refs[0].shape[0], out_ref.shape[1]
     for h in range(groups):
-        pieces = [refs[h * batches + r][...].astype(F32) for r in range(batches)]
-        mass = [
-            p[:, share : share + 1] + p[:, share + 1 : share + 2] + p[:, share + 2 : share + 3]
-            for p in pieces
-        ]
+        pieces = [refs[h * count + i][...] for i in range(count)]
+        mass = [mass_of(p, share) for p in pieces]
         top = functools.reduce(jnp.maximum, mass)
         raised = [jnp.exp(m - top) for m in mass]
         total = functools.reduce(jnp.add, raised)
-        out = sum(p[:, :share] * (w / total) for p, w in zip(pieces, raised))
+        out = sum(p[:, :share].astype(F32) * (w / total) for p, w in zip(pieces, raised))
         out_ref[h * rows : (h + 1) * rows] = out.astype(BF16)
 
 
@@ -193,7 +215,7 @@
     assert tokens.shape[0] == 1 and w_gate.shape[0] == 1
     where = jnp.stack([lax.axis_index(a) for a in ("batch", "expert", "tensor")]).astype(jnp.int32)
     width = w_gate.shape[1]
-    count, share = tokens.shape[1:]
+    token_count, share = tokens.shape[1:]
     slots = phi.shape[1]
     rows = slots // (experts * batches)
 
@@ -201,9 +223,9 @@
     scaled, part, first = pl.pallas_call(
         logits_body,
         out_shape=[
-            shape((count, share), BF16),
-            shape((slots + 8, count), F32),
-            shape((head, count), F32),
+            shape((token_count, share), BF16),
+            shape((slots + 8, token_count), F32),
+            shape((head, token_count), F32),
         ],
         in_specs=[pl.BlockSpec(memory_space=pltpu.HBM)] * 3,
         out_specs=[VMEM] * 3,
@@ -225,32 +247,40 @@
         bit <<= 1
     parts = [part, near, tail] + [swap(first, "tensor", s) for s in range(2, tensors)]
     parts_count = len(parts)
-    messages = pl.pallas_call(
+    half = experts * batches // 2
+    keep, send = pl.pallas_call(
         functools.partial(slots_body, width, parts_count, experts, batches),
-        out_shape=[shape((rows, share + 128), BF16)] * (experts * batches),
+        out_shape=[shape((half * rows, share + 128), BF16)] * 2,
         in_specs=[SMEM] + [VMEM] * (parts_count + 1),
-        out_specs=[VMEM] * (experts * batches),
+        out_specs=[VMEM] * 2,
         scratch_shapes=[pltpu.VMEM((slots, share + 128), BF16)],
         cost_estimate=pl.CostEstimate(flops=1 << 30, bytes_accessed=1 << 22, transcendentals=0),
         compiler_params=pltpu.CompilerParams(vmem_limit_bytes=6 << 20),
         name="slots",
     )(where, *parts, scaled)
+    messages = call(
+        functools.partial(merge_body, share),
+        [shape((rows, share + 128), BF16)] * half,
+        keep,
+        swap(send, "batch", 1),
+    )
     combine = pl.pallas_call(
         functools.partial(combine_body, width, parts_count, experts, batches),
-        out_shape=shape((count, slots), BF16),
+        out_shape=shape((token_count, slots), BF16),
         in_specs=[SMEM] + [VMEM] * parts_count,
         out_specs=VMEM,
-        scratch_shapes=[pltpu.VMEM((slots, count), F32)],
+        scratch_shapes=[pltpu.VMEM((slots, token_count), F32)],
         cost_estimate=pl.CostEstimate(flops=1 << 30, bytes_accessed=1 << 22, transcendentals=0),
         compiler_params=pltpu.CompilerParams(vmem_limit_bytes=6 << 20),
         name="combine",
     )(where, *parts)
+    count = batches // 2
     arrived = [
-        m if i == 0 else swap(m, ("batch", "expert"), i % batches * experts + i // batches)
+        m if i == 0 else swap(m, ("batch", "expert"), i % count * 2 * experts + i // count)
         for i, m in enumerate(messages)
     ]
     own = call(
-        functools.partial(gather_body, experts, batches),
+        functools.partial(gather_body, experts, count),
         shape((experts * rows, share), BF16),
         *arrived,
     )
@@ -310,7 +340,7 @@
     gathered = []
     for group in groups:
         gathered += [group] + [swap(group, "batch", r) for r in range(1, batches)]
-    return call(output_body, shape((count, share), BF16), combine, *gathered)[None]
+    return call(output_body, shape((token_count, share), BF16), combine, *gathered)[None]
 
 
 def direct(batches, s):

time: 86.4 us -> 83.5 us (0.966)
  starting transfers between devices: 37.8 us -> 34.3 us
    ppermute x40 -> x37, starting transfers between devices: 37.8 us -> 34.3 us  [swap(): return lax.ppermute(x, axes, [(i, i ^ bit) for i in range(count)])]
    ppermute x40 -> x37, waiting for transfers between devices: 24.7 us -> 25.1 us  [swap(): return lax.ppermute(x, axes, [(i, i ^ bit) for i in range(count)])]
    pallas_call x10 -> x11, Pallas kernels: 10.4 us -> 10.6 us  [call(): pl.pallas_call(body, out_shape=shapes, in_specs=specs, out_specs=jax.tree...]
  transfers between devices with their start and end apart: 40 -> 37, of which waited for: 14 -> 14; matrix products, arithmetic and copies ran while one was open for 0% -> 0% of each run, Pallas kernels for 19% -> 20%
where the time goes in v4:
time: 83.5 us; the launch traced here: 83.3 us
  starting transfers between devices  34.3 us (41%)
  waiting for transfers between devices  25.1 us (30%)
  Pallas kernels  23 us (28%)
    ppermute x37, starting transfers between devices, swap(): return lax.ppermute(x, axes, [(i, i ^ bit) for i in range(count)])  34.3 us
    ppermute x37, waiting for transfers between devices, swap(): return lax.ppermute(x, axes, [(i, i ^ bit) for i in range(count)])  25.1 us
    pallas_call x11, Pallas kernels, call(): pl.pallas_call(body, out_shape=shapes, in_specs=specs, out_specs=jax.tree...  10.6 us
    pallas_call x3, Pallas kernels, fetch(): pl.pallas_call(fetch_body, out_shape=[pltpu.VMEM(a.shape, a.dtype) for a...  9.28 us
  transfers between devices with their start and end apart: 37, of which 14 were waited for; matrix products, arithmetic and copies ran while one was open for 0% of the time, Pallas kernels for 20%

profile of v4, /device:TPU:0, one launch (start us, length us, event | category | flops | bytes accessed | tf_op | source)
XLA Modules:
  0.0 83.3 jit_solution(13960261887559422089)
XLA Ops:
  0.0 1.5 %logits.1 = (bf16[256,1024]{1,0:T(8,128)(2,1)S(1)}, f32[136,256]{1,0:T(8,128)S(1)}, f32[72,256]{1,0:T(8,128)S(1)}) custom-call(bf16[1,256,1024]{2,1,0:T(8,128)(2,1)} %tok_hbm.1, bf16[1024]{0:T(1024)(128)(2,1)} %gain_hbm.1, bf16[1024,128]{1,0:T(8,128)(2,1)} %phi_hbm.1), custom_call_target="tpu_custom_call" | custom-call | flops 1073741824 | bytes 4194304 | tf_op jit(solution)/shard_map/logits/pallas_call | solution.py:223
  1.5 3.1 %collective-permute-start = (f32[136,256]{1,0:T(8,128)S(1)}, f32[136,256]{1,0:T(8,128)S(1)}, u32[]{:S(2)}, u32[]{:S(2)}) collective-permute-start(f32[136,256]{1,0:T(8,128)S(1)} %get-tuple-element.28.refs_0_), channel_id=1, source_target_pairs={{0,1},{1,0},{2,3},{3,2},{4,5},{5,4},{6,7},{7,6},{8,9},{9,8},{10,11... | collective-permute-start | bytes 417800 | tf_op jit(solution)/shard_map/ppermute | solution.py:35
  4.6 2.6 %collective-permute-start.2 = (f32[72,256]{1,0:T(8,128)S(1)}, f32[72,256]{1,0:T(8,128)S(1)}, u32[]{:S(2)}, u32[]{:S(2)}) collective-permute-start(f32[72,256]{1,0:T(8,128)S(1)} %get-tuple-element.29), channel_id=1, source_target_pairs={{0,2},{1,3},{2,0},{3,1},{4,6},{5,7},{6,4},{7,5},{8,10},{9,11},{10,... | collective-permute-start | bytes 221192 | tf_op jit(solution)/shard_map/ppermute | solution.py:35
  7.2 0.0 collective-permute-start.3
  7.2 1.9 %collective-permute-done.refs_1_ = f32[136,256]{1,0:T(8,128)S(1)} collective-permute-done((f32[136,256]{1,0:T(8,128)S(1)}, f32[136,256]{1,0:T(8,128)S(1)}, u32[]{:S(2)}, u32[]{:S(2)}) %collective-permute-start) | collective-permute-done | bytes 139296 | tf_op jit(solution)/shard_map/ppermute | solution.py:35
  9.1 3.2 %collective-permute-start.1 = (f32[64,256]{1,0:T(8,128)S(1)}, f32[64,256]{1,0:T(8,128)S(1)}, u32[]{:S(2)}, u32[]{:S(2)}) collective-permute-start(f32[64,256]{1,0:T(8,128)S(1)} %slice_add_fusion), channel_id=1, source_target_pairs={{0,2},{1,3},{2,0},{3,1},{4,6},{5,7},{6,4},{7,5},{8,10},{9,11},{10,... | collective-permute-start | bytes 196616 | tf_op jit(solution)/shard_map/ppermute | solution.py:35
  12.3 0.1 pad_add_fusion.where_ref
  12.4 5.0 %collective-permute-done.1 = f32[64,256]{1,0:T(8,128)S(1)} collective-permute-done((f32[64,256]{1,0:T(8,128)S(1)}, f32[64,256]{1,0:T(8,128)S(1)}, u32[]{:S(2)}, u32[]{:S(2)}) %collective-permute-start.1) | collective-permute-done | bytes 65568 | tf_op jit(solution)/shard_map/ppermute | solution.py:35
  17.3 0.0 collective-permute-done.2.refs_3_
  17.4 1.0 %slots.1 = (bf16[64,1152]{1,0:T(8,128)(2,1)S(1)}, bf16[64,1152]{1,0:T(8,128)(2,1)S(1)}) custom-call(s32[3]{0:T(128)S(1)} %pad_add_fusion.where_ref, f32[136,256]{1,0:T(8,128)S(1)} %get-tuple-element.28.refs_0_, f32[136,256]{1,0:T(8,128)S(1)} %collective-permute-done.refs_1_, f32[64,256]{1,0:T(8,128)S(1)} %add.40.refs_2_, ...), custom_call_target="tpu_custom_call" | custom-call | flops 1073741824 | bytes 4194304 | tf_op jit(solution)/shard_map/slots/pallas_call | solution.py:251
  18.3 0.1 collective-permute-start.4
  18.4 3.1 %fetch.3.refs_2_ = bf16[1,4096,896]{2,1,0:T(8,128)(2,1)S(1)} custom-call(bf16[1,4096,896]{2,1,0:T(8,128)(2,1)} %refs_0_.3), custom_call_target="tpu_custom_call" | custom-call | flops 1073741824 | bytes 33554432 | tf_op jit(solution)/shard_map/fetch/pallas_call | solution.py:195
  21.5 0.2 shard_map.64
  21.8 1.6 %collective-permute-start.5 = (bf16[16,1152]{1,0:T(8,128)(2,1)S(1)}, bf16[16,1152]{1,0:T(8,128)(2,1)S(1)}, u32[]{:S(2)}, u32[]{:S(2)}) collective-permute-start(bf16[16,1152]{1,0:T(8,128)(2,1)S(1)} %get-tuple-element.34), channel_id=1, source_target_pairs={{0,16},{4,20},{8,24},{12,28},{16,0},{20,4},{24,8},{28,12},{1,17},{... | collective-permute-start | bytes 110600 | tf_op jit(solution)/shard_map/ppermute | solution.py:35
  23.4 1.5 %collective-permute-start.6 = (bf16[16,1152]{1,0:T(8,128)(2,1)S(1)}, bf16[16,1152]{1,0:T(8,128)(2,1)S(1)}, u32[]{:S(2)}, u32[]{:S(2)}) collective-permute-start(bf16[16,1152]{1,0:T(8,128)(2,1)S(1)} %get-tuple-element.35), channel_id=1, source_target_pairs={{0,4},{4,0},{8,12},{12,8},{16,20},{20,16},{24,28},{28,24},{1,5},{5... | collective-permute-start | bytes 110600 | tf_op jit(solution)/shard_map/ppermute | solution.py:35
  24.8 0.5 collective-permute-start.7
  25.3 3.1 %fetch.4.refs_3_ = bf16[1,4096,896]{2,1,0:T(8,128)(2,1)S(1)} custom-call(bf16[1,4096,896]{2,1,0:T(8,128)(2,1)} %refs_0_.4), custom_call_target="tpu_custom_call" | custom-call | flops 1073741824 | bytes 33554432 | tf_op jit(solution)/shard_map/fetch/pallas_call | solution.py:195
  28.4 1.3 %collective-permute-done.7.refs_3_ = bf16[16,1152]{1,0:T(8,128)(2,1)S(1)} collective-permute-done((bf16[16,1152]{1,0:T(8,128)(2,1)S(1)}, bf16[16,1152]{1,0:T(8,128)(2,1)S(1)}, u32[]{:S(2)}, u32[]{:S(2)}) %collective-permute-start.7) | collective-permute-done | bytes 36896 | tf_op jit(solution)/shard_map/ppermute | solution.py:35
  29.7 0.2 shard_map.65
  29.9 0.6 collective-permute-start.17
  30.5 3.1 %fetch.5.down_ref = bf16[1,896,4096]{2,1,0:T(8,128)(2,1)S(1)} custom-call(bf16[1,896,4096]{2,1,0:T(8,128)(2,1)} %refs_0_.5), custom_call_target="tpu_custom_call" | custom-call | flops 1073741824 | bytes 33554432 | tf_op jit(solution)/shard_map/fetch/pallas_call | solution.py:195
  33.6 0.1 collective-permute-start.14
  33.6 3.0 %collective-permute-start.15 = (bf16[32,1024]{1,0:T(8,128)(2,1)S(1)}, bf16[32,1024]{1,0:T(8,128)(2,1)S(1)}, u32[]{:S(2)}, u32[]{:S(2)}) collective-permute-start(bf16[32,1024]{1,0:T(8,128)(2,1)S(1)} %shard_map.65), channel_id=1, source_target_pairs={{0,17},{1,16},{2,19},{3,18},{8,25},{9,24},{10,27},{11,26},{16,1},{... | collective-permute-start | bytes 196616 | tf_op jit(solution)/shard_map/ppermute | solution.py:35
  36.6 2.0 %collective-permute-start.11 = (bf16[32,1024]{1,0:T(8,128)(2,1)S(1)}, bf16[32,1024]{1,0:T(8,128)(2,1)S(1)}, u32[]{:S(2)}, u32[]{:S(2)}) collective-permute-start(bf16[32,1024]{1,0:T(8,128)(2,1)S(1)} %shard_map.65), channel_id=1, source_target_pairs={{0,3},{1,2},{2,1},{3,0},{4,7},{5,6},{6,5},{7,4},{8,11},{9,10},{10,... | collective-permute-start | bytes 196616 | tf_op jit(solution)/shard_map/ppermute | solution.py:35
  38.6 0.1 collective-permute-start.18
  38.7 0.9 %collective-permute-done.15 = bf16[32,1024]{1,0:T(8,128)(2,1)S(1)} collective-permute-done((bf16[32,1024]{1,0:T(8,128)(2,1)S(1)}, bf16[32,1024]{1,0:T(8,128)(2,1)S(1)}, u32[]{:S(2)}, u32[]{:S(2)}) %collective-permute-start.15) | collective-permute-done | bytes 65568 | tf_op jit(solution)/shard_map/ppermute | solution.py:35
  39.6 3.1 %collective-permute-done.11 = bf16[32,1024]{1,0:T(8,128)(2,1)S(1)} collective-permute-done((bf16[32,1024]{1,0:T(8,128)(2,1)S(1)}, bf16[32,1024]{1,0:T(8,128)(2,1)S(1)}, u32[]{:S(2)}, u32[]{:S(2)}) %collective-permute-start.11) | collective-permute-done | bytes 65568 | tf_op jit(solution)/shard_map/ppermute | solution.py:35
  42.7 0.5 collective-permute-start.12
  43.2 0.9 %collective-permute-done.8 = bf16[32,1024]{1,0:T(8,128)(2,1)S(1)} collective-permute-done((bf16[32,1024]{1,0:T(8,128)(2,1)S(1)}, bf16[32,1024]{1,0:T(8,128)(2,1)S(1)}, u32[]{:S(2)}, u32[]{:S(2)}) %collective-permute-start.8) | collective-permute-done | bytes 65568 | tf_op jit(solution)/shard_map/ppermute | solution.py:35
  44.1 0.9 %collective-permute-start.9 = (bf16[32,1024]{1,0:T(8,128)(2,1)S(1)}, bf16[32,1024]{1,0:T(8,128)(2,1)S(1)}, u32[]{:S(2)}, u32[]{:S(2)}) collective-permute-start(bf16[32,1024]{1,0:T(8,128)(2,1)S(1)} %collective-permute-done.8), channel_id=1, source_target_pairs={{0,16},{8,24},{16,0},{24,8},{1,17},{9,25},{17,1},{25,9},{2,18},{10... | collective-permute-start | bytes 196616 | tf_op jit(solution)/shard_map/ppermute | solution.py:35
  45.0 1.9 %collective-permute-done.12 = bf16[32,1024]{1,0:T(8,128)(2,1)S(1)} collective-permute-done((bf16[32,1024]{1,0:T(8,128)(2,1)S(1)}, bf16[32,1024]{1,0:T(8,128)(2,1)S(1)}, u32[]{:S(2)}, u32[]{:S(2)}) %collective-permute-start.12) | collective-permute-done | bytes 65568 | tf_op jit(solution)/shard_map/ppermute | solution.py:35
  47.0 1.4 %collective-permute-done.9 = bf16[32,1024]{1,0:T(8,128)(2,1)S(1)} collective-permute-done((bf16[32,1024]{1,0:T(8,128)(2,1)S(1)}, bf16[32,1024]{1,0:T(8,128)(2,1)S(1)}, u32[]{:S(2)}, u32[]{:S(2)}) %collective-permute-start.9) | collective-permute-done | bytes 65568 | tf_op jit(solution)/shard_map/ppermute | solution.py:35
  48.4 1.3 %shard_map.66 = (f32[128,896]{1,0:T(8,128)S(1)}, f32[128,896]{1,0:T(8,128)S(1)}) custom-call(s32[3]{0:T(128)S(1)} %pad_add_fusion.where_ref, bf16[64,1024]{1,0:T(8,128)(2,1)S(1)} %pad_maximum_fusion.refs_0_, bf16[64,1024]{1,0:T(8,128)(2,1)S(1)} %collective-permute-done.18.refs_1_, bf16[1,4096,896]{2,1,0:T(8,128)(2,1)S(1)} %fetch.3.refs_2_, ...), custom_call_target="tpu_custom_call" | custom-call | flops 469762048 | bytes 16777216 | tf_op jit(solution)/shard_map/pallas_call | solution.py:19
  49.7 1.3 %shard_map.67 = (f32[128,896]{1,0:T(8,128)S(1)}, f32[128,896]{1,0:T(8,128)S(1)}) custom-call(s32[3]{0:T(128)S(1)} %pad_add_fusion.where_ref, bf16[64,1024]{1,0:T(8,128)(2,1)S(1)} %constant_dynamic-update-slice_fusion.4.refs_0_, bf16[64,1024]{1,0:T(8,128)(2,1)S(1)} %collective-permute-done.16.refs_1_, bf16[1,4096,896]{2,1,0:T(8,128)(2,1)S(1)} %fetch.3.refs_2_, ...), custom_call_target="tpu_custom_call" | custom-call | flops 469762048 | bytes 16777216 | tf_op jit(solution)/shard_map/pallas_call | solution.py:19
  51.0 1.3 %shard_map.68 = (f32[128,896]{1,0:T(8,128)S(1)}, f32[128,896]{1,0:T(8,128)S(1)}) custom-call(s32[3]{0:T(128)S(1)} %pad_add_fusion.where_ref, bf16[64,1024]{1,0:T(8,128)(2,1)S(1)} %constant_dynamic-update-slice_fusion.2.refs_0_, bf16[64,1024]{1,0:T(8,128)(2,1)S(1)} %collective-permute-done.13.refs_1_, bf16[1,4096,896]{2,1,0:T(8,128)(2,1)S(1)} %fetch.3.refs_2_, ...), custom_call_target="tpu_custom_call" | custom-call | flops 469762048 | bytes 16777216 | tf_op jit(solution)/shard_map/pallas_call | solution.py:19
  52.2 1.3 %shard_map.69.hidden_ref = bf16[128,896]{1,0:T(8,128)(2,1)S(1)} custom-call(s32[3]{0:T(128)S(1)} %pad_add_fusion.where_ref, bf16[64,1024]{1,0:T(8,128)(2,1)S(1)} %constant_dynamic-update-slice_fusion.refs_0_, bf16[64,1024]{1,0:T(8,128)(2,1)S(1)} %collective-permute-done.10.refs_1_, bf16[1,4096,896]{2,1,0:T(8,128)(2,1)S(1)} %fetch.3.refs_2_, ...), custom_call_target="tpu_custom_call" | custom-call | flops 469762048 | bytes 16777216 | tf_op jit(solution)/shard_map/pallas_call | solution.py:19
  53.6 1.0 %shard_map.73 = (bf16[64,1024]{1,0:T(8,128)(2,1)S(1)}, bf16[64,1024]{1,0:T(8,128)(2,1)S(1)}) custom-call(s32[3]{0:T(128)S(1)} %pad_add_fusion.where_ref, bf16[128,896]{1,0:T(8,128)(2,1)S(1)} %shard_map.69.hidden_ref, bf16[1,896,4096]{2,1,0:T(8,128)(2,1)S(1)} %fetch.5.down_ref), custom_call_target="tpu_custom_call" | custom-call | flops 234881024 | bytes 8388608 | tf_op jit(solution)/shard_map/pallas_call | solution.py:19
  54.6 0.6 collective-permute-start.28
  55.1 1.0 %shard_map.70 = (bf16[64,1024]{1,0:T(8,128)(2,1)S(1)}, bf16[64,1024]{1,0:T(8,128)(2,1)S(1)}) custom-call(s32[3]{0:T(128)S(1)} %pad_add_fusion.where_ref, bf16[128,896]{1,0:T(8,128)(2,1)S(1)} %shard_map.69.hidden_ref, bf16[1,896,4096]{2,1,0:T(8,128)(2,1)S(1)} %fetch.5.down_ref), custom_call_target="tpu_custom_call" | custom-call | flops 234881024 | bytes 8388608 | tf_op jit(solution)/shard_map/pallas_call | solution.py:19
  56.1 0.1 collective-permute-start.19
  56.2 1.0 %shard_map.71 = (bf16[64,1024]{1,0:T(8,128)(2,1)S(1)}, bf16[64,1024]{1,0:T(8,128)(2,1)S(1)}) custom-call(s32[3]{0:T(128)S(1)} %pad_add_fusion.where_ref, bf16[128,896]{1,0:T(8,128)(2,1)S(1)} %shard_map.69.hidden_ref, bf16[1,896,4096]{2,1,0:T(8,128)(2,1)S(1)} %fetch.5.down_ref), custom_call_target="tpu_custom_call" | custom-call | flops 234881024 | bytes 8388608 | tf_op jit(solution)/shard_map/pallas_call | solution.py:19
  57.2 0.6 collective-permute-start.22
  57.8 1.0 %shard_map.72 = (bf16[64,1024]{1,0:T(8,128)(2,1)S(1)}, bf16[64,1024]{1,0:T(8,128)(2,1)S(1)}) custom-call(s32[3]{0:T(128)S(1)} %pad_add_fusion.where_ref, bf16[128,896]{1,0:T(8,128)(2,1)S(1)} %shard_map.69.hidden_ref, bf16[1,896,4096]{2,1,0:T(8,128)(2,1)S(1)} %fetch.5.down_ref), custom_call_target="tpu_custom_call" | custom-call | flops 234881024 | bytes 8388608 | tf_op jit(solution)/shard_map/pallas_call | solution.py:19
  58.8 0.1 collective-permute-start.25
  58.9 1.0 %collective-permute-start.29 = (bf16[32,1024]{1,0:T(8,128)(2,1)S(1)}, bf16[32,1024]{1,0:T(8,128)(2,1)S(1)}, u32[]{:S(2)}, u32[]{:S(2)}) collective-permute-start(bf16[32,1024]{1,0:T(8,128)(2,1)S(1)} %slice.56), channel_id=1, source_target_pairs={{0,16},{8,24},{16,0},{24,8},{1,17},{9,25},{17,1},{25,9},{2,18},{10... | collective-permute-start | bytes 196616 | tf_op jit(solution)/shard_map/ppermute | solution.py:35
  59.9 1.2 %collective-permute-start.20 = (bf16[32,1024]{1,0:T(8,128)(2,1)S(1)}, bf16[32,1024]{1,0:T(8,128)(2,1)S(1)}, u32[]{:S(2)}, u32[]{:S(2)}) collective-permute-start(bf16[32,1024]{1,0:T(8,128)(2,1)S(1)} %slice.50), channel_id=1, source_target_pairs={{0,16},{8,24},{16,0},{24,8},{1,17},{9,25},{17,1},{25,9},{2,18},{10... | collective-permute-start | bytes 196616 | tf_op jit(solution)/shard_map/ppermute | solution.py:35
  61.2 1.0 %collective-permute-start.23 = (bf16[32,1024]{1,0:T(8,128)(2,1)S(1)}, bf16[32,1024]{1,0:T(8,128)(2,1)S(1)}, u32[]{:S(2)}, u32[]{:S(2)}) collective-permute-start(bf16[32,1024]{1,0:T(8,128)(2,1)S(1)} %slice.52), channel_id=1, source_target_pairs={{0,16},{8,24},{16,0},{24,8},{1,17},{9,25},{17,1},{25,9},{2,18},{10... | collective-permute-start | bytes 196616 | tf_op jit(solution)/shard_map/ppermute | solution.py:35
  62.2 1.2 %collective-permute-start.26 = (bf16[32,1024]{1,0:T(8,128)(2,1)S(1)}, bf16[32,1024]{1,0:T(8,128)(2,1)S(1)}, u32[]{:S(2)}, u32[]{:S(2)}) collective-permute-start(bf16[32,1024]{1,0:T(8,128)(2,1)S(1)} %slice.54), channel_id=1, source_target_pairs={{0,16},{8,24},{16,0},{24,8},{1,17},{9,25},{17,1},{25,9},{2,18},{10... | collective-permute-start | bytes 196616 | tf_op jit(solution)/shard_map/ppermute | solution.py:35
  63.4 2.0 %collective-permute-done.20 = bf16[32,1024]{1,0:T(8,128)(2,1)S(1)} collective-permute-done((bf16[32,1024]{1,0:T(8,128)(2,1)S(1)}, bf16[32,1024]{1,0:T(8,128)(2,1)S(1)}, u32[]{:S(2)}, u32[]{:S(2)}) %collective-permute-start.20) | collective-permute-done | bytes 65568 | tf_op jit(solution)/shard_map/ppermute | solution.py:35
  65.4 2.0 %collective-permute-start.21 = (bf16[32,1024]{1,0:T(8,128)(2,1)S(1)}, bf16[32,1024]{1,0:T(8,128)(2,1)S(1)}, u32[]{:S(2)}, u32[]{:S(2)}) collective-permute-start(bf16[32,1024]{1,0:T(8,128)(2,1)S(1)} %add_convert_fusion.8), channel_id=1, source_target_pairs={{0,3},{1,2},{2,1},{3,0},{4,7},{5,6},{6,5},{7,4},{8,11},{9,10},{10,... | collective-permute-start | bytes 196616 | tf_op jit(solution)/shard_map/ppermute | solution.py:35
  67.4 0.7 collective-permute-start.24
  68.1 1.9 %collective-permute-start.27 = (bf16[32,1024]{1,0:T(8,128)(2,1)S(1)}, bf16[32,1024]{1,0:T(8,128)(2,1)S(1)}, u32[]{:S(2)}, u32[]{:S(2)}) collective-permute-start(bf16[32,1024]{1,0:T(8,128)(2,1)S(1)} %add_convert_fusion.6), channel_id=1, source_target_pairs={{0,1},{1,0},{2,3},{3,2},{4,5},{5,4},{6,7},{7,6},{8,9},{9,8},{10,11... | collective-permute-start | bytes 196616 | tf_op jit(solution)/shard_map/ppermute | solution.py:35
  70.0 1.9 %collective-permute-done.21 = bf16[32,1024]{1,0:T(8,128)(2,1)S(1)} collective-permute-done((bf16[32,1024]{1,0:T(8,128)(2,1)S(1)}, bf16[32,1024]{1,0:T(8,128)(2,1)S(1)}, u32[]{:S(2)}, u32[]{:S(2)}) %collective-permute-start.21) | collective-permute-done | bytes 65568 | tf_op jit(solution)/shard_map/ppermute | solution.py:35
  71.8 2.0 %collective-permute-done.24 = bf16[32,1024]{1,0:T(8,128)(2,1)S(1)} collective-permute-done((bf16[32,1024]{1,0:T(8,128)(2,1)S(1)}, bf16[32,1024]{1,0:T(8,128)(2,1)S(1)}, u32[]{:S(2)}, u32[]{:S(2)}) %collective-permute-start.24) | collective-permute-done | bytes 65568 | tf_op jit(solution)/shard_map/ppermute | solution.py:35
  73.9 0.8 %collective-permute-start.33 = (bf16[16,1024]{1,0:T(8,128)(2,1)S(1)}, bf16[16,1024]{1,0:T(8,128)(2,1)S(1)}, u32[]{:S(2)}, u32[]{:S(2)}) collective-permute-start(bf16[16,1024]{1,0:T(8,128)(2,1)S(1)} %get-tuple-element.51), channel_id=1, source_target_pairs={{0,4},{4,0},{1,5},{5,1},{2,6},{6,2},{3,7},{7,3},{8,12},{12,8},{9,1... | collective-permute-start | bytes 98312 | tf_op jit(solution)/shard_map/ppermute | solution.py:35
  74.8 1.4 %collective-permute-start.31 = (bf16[16,1024]{1,0:T(8,128)(2,1)S(1)}, bf16[16,1024]{1,0:T(8,128)(2,1)S(1)}, u32[]{:S(2)}, u32[]{:S(2)}) collective-permute-start(bf16[16,1024]{1,0:T(8,128)(2,1)S(1)} %get-tuple-element.52.refs_0_), channel_id=1, source_target_pairs={{0,16},{8,24},{16,0},{24,8},{1,17},{9,25},{17,1},{25,9},{2,18},{10... | collective-permute-start | bytes 98312 | tf_op jit(solution)/shard_map/ppermute | solution.py:35
  76.2 0.4 collective-permute-start.32
  76.6 1.3 %collective-permute-done.33.refs_4_ = bf16[16,1024]{1,0:T(8,128)(2,1)S(1)} collective-permute-done((bf16[16,1024]{1,0:T(8,128)(2,1)S(1)}, bf16[16,1024]{1,0:T(8,128)(2,1)S(1)}, u32[]{:S(2)}, u32[]{:S(2)}) %collective-permute-start.33) | collective-permute-done | bytes 32800 | tf_op jit(solution)/shard_map/ppermute | solution.py:35
  77.9 0.9 %collective-permute-start.35 = (bf16[16,1024]{1,0:T(8,128)(2,1)S(1)}, bf16[16,1024]{1,0:T(8,128)(2,1)S(1)}, u32[]{:S(2)}, u32[]{:S(2)}) collective-permute-start(bf16[16,1024]{1,0:T(8,128)(2,1)S(1)} %collective-permute-done.33.refs_4_), channel_id=1, source_target_pairs={{0,16},{8,24},{16,0},{24,8},{1,17},{9,25},{17,1},{25,9},{2,18},{10... | collective-permute-start | bytes 98312 | tf_op jit(solution)/shard_map/ppermute | solution.py:35
  78.9 0.9 %collective-permute-start.36 = (bf16[16,1024]{1,0:T(8,128)(2,1)S(1)}, bf16[16,1024]{1,0:T(8,128)(2,1)S(1)}, u32[]{:S(2)}, u32[]{:S(2)}) collective-permute-start(bf16[16,1024]{1,0:T(8,128)(2,1)S(1)} %collective-permute-done.33.refs_4_), channel_id=1, source_target_pairs={{0,24},{8,16},{16,8},{24,0},{1,25},{9,17},{17,9},{25,1},{2,26},{10... | collective-permute-start | bytes 98312 | tf_op jit(solution)/shard_map/ppermute | solution.py:35
  79.8 0.7 combine.1.combine_ref
  80.5 1.3 %collective-permute-done.35.refs_6_ = bf16[16,1024]{1,0:T(8,128)(2,1)S(1)} collective-permute-done((bf16[16,1024]{1,0:T(8,128)(2,1)S(1)}, bf16[16,1024]{1,0:T(8,128)(2,1)S(1)}, u32[]{:S(2)}, u32[]{:S(2)}) %collective-permute-start.35) | collective-permute-done | bytes 32800 | tf_op jit(solution)/shard_map/ppermute | solution.py:35
  81.8 0.4 collective-permute-done.36.refs_7_
  82.2 1.1 %shard_map.74 = bf16[256,1024]{1,0:T(8,128)(2,1)} custom-call(bf16[256,128]{1,0:T(8,128)(2,1)S(1)} %combine.1.combine_ref, bf16[16,1024]{1,0:T(8,128)(2,1)S(1)} %get-tuple-element.52.refs_0_, bf16[16,1024]{1,0:T(8,128)(2,1)S(1)} %collective-permute-done.30.refs_1_, bf16[16,1024]{1,0:T(8,128)(2,1)S(1)} %collective-permute-done.31.refs_2_, ...), custom_call_target="tpu_custom_call" | custom-call | flops 1073741824 | bytes 4194304 | tf_op jit(solution)/shard_map/pallas_call | solution.py:19
  (50 shorter events, 0.4 us)
Async XLA Ops:
  1.5 7.6 %collective-permute-start = (f32[136,256]{1,0:T(8,128)S(1)}, f32[136,256]{1,0:T(8,128)S(1)}, u32[]{:S(2)}, u32[]{:S(2)}) collective-permute-start(f32[136,256]{1,0:T(8,128)S(1)} %get-tuple-element.28.refs_0_), channel_id=1, source_target_pairs={{0,1},{1,0},{2,3},{3,2},{4,5},{5,4},{6,7},{7,6},{8,9},{9,8},{10,11... | collective-permute-start | bytes 417800 | tf_op jit(solution)/shard_map/ppermute | solution.py:35
  4.6 12.7 %collective-permute-start.2 = (f32[72,256]{1,0:T(8,128)S(1)}, f32[72,256]{1,0:T(8,128)S(1)}, u32[]{:S(2)}, u32[]{:S(2)}) collective-permute-start(f32[72,256]{1,0:T(8,128)S(1)} %get-tuple-element.29), channel_id=1, source_target_pairs={{0,2},{1,3},{2,0},{3,1},{4,6},{5,7},{6,4},{7,5},{8,10},{9,11},{10,... | collective-permute-start | bytes 221192 | tf_op jit(solution)/shard_map/ppermute | solution.py:35
  7.2 10.1 %collective-permute-start.3 = (f32[72,256]{1,0:T(8,128)S(1)}, f32[72,256]{1,0:T(8,128)S(1)}, u32[]{:S(2)}, u32[]{:S(2)}) collective-permute-start(f32[72,256]{1,0:T(8,128)S(1)} %get-tuple-element.29), channel_id=1, source_target_pairs={{0,3},{1,2},{2,1},{3,0},{4,7},{5,6},{6,5},{7,4},{8,11},{9,10},{10,... | collective-permute-start | bytes 221192 | tf_op jit(solution)/shard_map/ppermute | solution.py:35
  9.1 8.2 %collective-permute-start.1 = (f32[64,256]{1,0:T(8,128)S(1)}, f32[64,256]{1,0:T(8,128)S(1)}, u32[]{:S(2)}, u32[]{:S(2)}) collective-permute-start(f32[64,256]{1,0:T(8,128)S(1)} %slice_add_fusion), channel_id=1, source_target_pairs={{0,2},{1,3},{2,0},{3,1},{4,6},{5,7},{6,4},{7,5},{8,10},{9,11},{10,... | collective-permute-start | bytes 196616 | tf_op jit(solution)/shard_map/ppermute | solution.py:35
  18.3 3.2 %collective-permute-start.4 = (bf16[64,1152]{1,0:T(8,128)(2,1)S(1)}, bf16[64,1152]{1,0:T(8,128)(2,1)S(1)}, u32[]{:S(2)}, u32[]{:S(2)}) collective-permute-start(bf16[64,1152]{1,0:T(8,128)(2,1)S(1)} %get-tuple-element.32), channel_id=1, source_target_pairs={{0,8},{8,0},{16,24},{24,16},{1,9},{9,1},{17,25},{25,17},{2,10},{10... | collective-permute-start | bytes 442376 | tf_op jit(solution)/shard_map/ppermute | solution.py:35
  21.8 6.7 %collective-permute-start.5 = (bf16[16,1152]{1,0:T(8,128)(2,1)S(1)}, bf16[16,1152]{1,0:T(8,128)(2,1)S(1)}, u32[]{:S(2)}, u32[]{:S(2)}) collective-permute-start(bf16[16,1152]{1,0:T(8,128)(2,1)S(1)} %get-tuple-element.34), channel_id=1, source_target_pairs={{0,16},{4,20},{8,24},{12,28},{16,0},{20,4},{24,8},{28,12},{1,17},{... | collective-permute-start | bytes 110600 | tf_op jit(solution)/shard_map/ppermute | solution.py:35
  23.4 5.1 %collective-permute-start.6 = (bf16[16,1152]{1,0:T(8,128)(2,1)S(1)}, bf16[16,1152]{1,0:T(8,128)(2,1)S(1)}, u32[]{:S(2)}, u32[]{:S(2)}) collective-permute-start(bf16[16,1152]{1,0:T(8,128)(2,1)S(1)} %get-tuple-element.35), channel_id=1, source_target_pairs={{0,4},{4,0},{8,12},{12,8},{16,20},{20,16},{24,28},{28,24},{1,5},{5... | collective-permute-start | bytes 110600 | tf_op jit(solution)/shard_map/ppermute | solution.py:35
  24.8 4.9 %collective-permute-start.7 = (bf16[16,1152]{1,0:T(8,128)(2,1)S(1)}, bf16[16,1152]{1,0:T(8,128)(2,1)S(1)}, u32[]{:S(2)}, u32[]{:S(2)}) collective-permute-start(bf16[16,1152]{1,0:T(8,128)(2,1)S(1)} %get-tuple-element.36), channel_id=1, source_target_pairs={{0,20},{4,16},{8,28},{12,24},{16,4},{20,0},{24,12},{28,8},{1,21},{... | collective-permute-start | bytes 110600 | tf_op jit(solution)/shard_map/ppermute | solution.py:35
  29.9 8.7 %collective-permute-start.17 = (bf16[32,1024]{1,0:T(8,128)(2,1)S(1)}, bf16[32,1024]{1,0:T(8,128)(2,1)S(1)}, u32[]{:S(2)}, u32[]{:S(2)}) collective-permute-start(bf16[32,1024]{1,0:T(8,128)(2,1)S(1)} %shard_map.65), channel_id=1, source_target_pairs={{0,16},{8,24},{16,0},{24,8},{1,17},{9,25},{17,1},{25,9},{2,18},{10... | collective-permute-start | bytes 196616 | tf_op jit(solution)/shard_map/ppermute | solution.py:35
  33.6 5.1 %collective-permute-start.14 = (bf16[32,1024]{1,0:T(8,128)(2,1)S(1)}, bf16[32,1024]{1,0:T(8,128)(2,1)S(1)}, u32[]{:S(2)}, u32[]{:S(2)}) collective-permute-start(bf16[32,1024]{1,0:T(8,128)(2,1)S(1)} %shard_map.65), channel_id=1, source_target_pairs={{0,1},{1,0},{2,3},{3,2},{4,5},{5,4},{6,7},{7,6},{8,9},{9,8},{10,11... | collective-permute-start | bytes 196616 | tf_op jit(solution)/shard_map/ppermute | solution.py:35
  33.6 5.9 %collective-permute-start.15 = (bf16[32,1024]{1,0:T(8,128)(2,1)S(1)}, bf16[32,1024]{1,0:T(8,128)(2,1)S(1)}, u32[]{:S(2)}, u32[]{:S(2)}) collective-permute-start(bf16[32,1024]{1,0:T(8,128)(2,1)S(1)} %shard_map.65), channel_id=1, source_target_pairs={{0,17},{1,16},{2,19},{3,18},{8,25},{9,24},{10,27},{11,26},{16,1},{... | collective-permute-start | bytes 196616 | tf_op jit(solution)/shard_map/ppermute | solution.py:35
  36.6 6.1 %collective-permute-start.11 = (bf16[32,1024]{1,0:T(8,128)(2,1)S(1)}, bf16[32,1024]{1,0:T(8,128)(2,1)S(1)}, u32[]{:S(2)}, u32[]{:S(2)}) collective-permute-start(bf16[32,1024]{1,0:T(8,128)(2,1)S(1)} %shard_map.65), channel_id=1, source_target_pairs={{0,3},{1,2},{2,1},{3,0},{4,7},{5,6},{6,5},{7,4},{8,11},{9,10},{10,... | collective-permute-start | bytes 196616 | tf_op jit(solution)/shard_map/ppermute | solution.py:35
  38.6 5.5 %collective-permute-start.8 = (bf16[32,1024]{1,0:T(8,128)(2,1)S(1)}, bf16[32,1024]{1,0:T(8,128)(2,1)S(1)}, u32[]{:S(2)}, u32[]{:S(2)}) collective-permute-start(bf16[32,1024]{1,0:T(8,128)(2,1)S(1)} %shard_map.65), channel_id=1, source_target_pairs={{0,2},{1,3},{2,0},{3,1},{4,6},{5,7},{6,4},{7,5},{8,10},{9,11},{10,... | collective-permute-start | bytes 196616 | tf_op jit(solution)/shard_map/ppermute | solution.py:35
  38.6 9.8 %collective-permute-start.18 = (bf16[64,1024]{1,0:T(8,128)(2,1)S(1)}, bf16[64,1024]{1,0:T(8,128)(2,1)S(1)}, u32[]{:S(2)}, u32[]{:S(2)}) collective-permute-start(bf16[64,1024]{1,0:T(8,128)(2,1)S(1)} %pad_maximum_fusion.refs_0_), channel_id=1, source_target_pairs={{0,8},{8,0},{16,24},{24,16},{1,9},{9,1},{17,25},{25,17},{2,10},{10... | collective-permute-start | bytes 393224 | tf_op jit(solution)/shard_map/ppermute | solution.py:35
  39.6 10.1 %collective-permute-start.16 = (bf16[64,1024]{1,0:T(8,128)(2,1)S(1)}, bf16[64,1024]{1,0:T(8,128)(2,1)S(1)}, u32[]{:S(2)}, u32[]{:S(2)}) collective-permute-start(bf16[64,1024]{1,0:T(8,128)(2,1)S(1)} %constant_dynamic-update-slice_fusion.4.refs_0_), channel_id=1, source_target_pairs={{0,8},{8,0},{16,24},{24,16},{1,9},{9,1},{17,25},{25,17},{2,10},{10... | collective-permute-start | bytes 393224 | tf_op jit(solution)/shard_map/ppermute | solution.py:35
  42.7 4.3 %collective-permute-start.12 = (bf16[32,1024]{1,0:T(8,128)(2,1)S(1)}, bf16[32,1024]{1,0:T(8,128)(2,1)S(1)}, u32[]{:S(2)}, u32[]{:S(2)}) collective-permute-start(bf16[32,1024]{1,0:T(8,128)(2,1)S(1)} %collective-permute-done.11), channel_id=1, source_target_pairs={{0,16},{8,24},{16,0},{24,8},{1,17},{9,25},{17,1},{25,9},{2,18},{10... | collective-permute-start | bytes 196616 | tf_op jit(solution)/shard_map/ppermute | solution.py:35
  44.1 4.3 %collective-permute-start.9 = (bf16[32,1024]{1,0:T(8,128)(2,1)S(1)}, bf16[32,1024]{1,0:T(8,128)(2,1)S(1)}, u32[]{:S(2)}, u32[]{:S(2)}) collective-permute-start(bf16[32,1024]{1,0:T(8,128)(2,1)S(1)} %collective-permute-done.8), channel_id=1, source_target_pairs={{0,16},{8,24},{16,0},{24,8},{1,17},{9,25},{17,1},{25,9},{2,18},{10... | collective-permute-start | bytes 196616 | tf_op jit(solution)/shard_map/ppermute | solution.py:35
  46.9 4.0 %collective-permute-start.13 = (bf16[64,1024]{1,0:T(8,128)(2,1)S(1)}, bf16[64,1024]{1,0:T(8,128)(2,1)S(1)}, u32[]{:S(2)}, u32[]{:S(2)}) collective-permute-start(bf16[64,1024]{1,0:T(8,128)(2,1)S(1)} %constant_dynamic-update-slice_fusion.2.refs_0_), channel_id=1, source_target_pairs={{0,8},{8,0},{16,24},{24,16},{1,9},{9,1},{17,25},{25,17},{2,10},{10... | collective-permute-start | bytes 393224 | tf_op jit(solution)/shard_map/ppermute | solution.py:35
  48.4 3.9 %collective-permute-start.10 = (bf16[64,1024]{1,0:T(8,128)(2,1)S(1)}, bf16[64,1024]{1,0:T(8,128)(2,1)S(1)}, u32[]{:S(2)}, u32[]{:S(2)}) collective-permute-start(bf16[64,1024]{1,0:T(8,128)(2,1)S(1)} %constant_dynamic-update-slice_fusion.refs_0_), channel_id=1, source_target_pairs={{0,8},{8,0},{16,24},{24,16},{1,9},{9,1},{17,25},{25,17},{2,10},{10... | collective-permute-start | bytes 393224 | tf_op jit(solution)/shard_map/ppermute | solution.py:35
  54.6 4.3 %collective-permute-start.28 = (bf16[64,1024]{1,0:T(8,128)(2,1)S(1)}, bf16[64,1024]{1,0:T(8,128)(2,1)S(1)}, u32[]{:S(2)}, u32[]{:S(2)}) collective-permute-start(bf16[64,1024]{1,0:T(8,128)(2,1)S(1)} %get-tuple-element.50), channel_id=1, source_target_pairs={{0,8},{8,0},{16,24},{24,16},{1,9},{9,1},{17,25},{25,17},{2,10},{10... | collective-permute-start | bytes 393224 | tf_op jit(solution)/shard_map/ppermute | solution.py:35
  56.1 3.8 %collective-permute-start.19 = (bf16[64,1024]{1,0:T(8,128)(2,1)S(1)}, bf16[64,1024]{1,0:T(8,128)(2,1)S(1)}, u32[]{:S(2)}, u32[]{:S(2)}) collective-permute-start(bf16[64,1024]{1,0:T(8,128)(2,1)S(1)} %get-tuple-element.44), channel_id=1, source_target_pairs={{0,8},{8,0},{16,24},{24,16},{1,9},{9,1},{17,25},{25,17},{2,10},{10... | collective-permute-start | bytes 393224 | tf_op jit(solution)/shard_map/ppermute | solution.py:35
  57.2 3.9 %collective-permute-start.22 = (bf16[64,1024]{1,0:T(8,128)(2,1)S(1)}, bf16[64,1024]{1,0:T(8,128)(2,1)S(1)}, u32[]{:S(2)}, u32[]{:S(2)}) collective-permute-start(bf16[64,1024]{1,0:T(8,128)(2,1)S(1)} %get-tuple-element.46), channel_id=1, source_target_pairs={{0,8},{8,0},{16,24},{24,16},{1,9},{9,1},{17,25},{25,17},{2,10},{10... | collective-permute-start | bytes 393224 | tf_op jit(solution)/shard_map/ppermute | solution.py:35
  58.8 3.4 %collective-permute-start.25 = (bf16[64,1024]{1,0:T(8,128)(2,1)S(1)}, bf16[64,1024]{1,0:T(8,128)(2,1)S(1)}, u32[]{:S(2)}, u32[]{:S(2)}) collective-permute-start(bf16[64,1024]{1,0:T(8,128)(2,1)S(1)} %get-tuple-element.48), channel_id=1, source_target_pairs={{0,8},{8,0},{16,24},{24,16},{1,9},{9,1},{17,25},{25,17},{2,10},{10... | collective-permute-start | bytes 393224 | tf_op jit(solution)/shard_map/ppermute | solution.py:35
  58.9 11.1 %collective-permute-start.29 = (bf16[32,1024]{1,0:T(8,128)(2,1)S(1)}, bf16[32,1024]{1,0:T(8,128)(2,1)S(1)}, u32[]{:S(2)}, u32[]{:S(2)}) collective-permute-start(bf16[32,1024]{1,0:T(8,128)(2,1)S(1)} %slice.56), channel_id=1, source_target_pairs={{0,16},{8,24},{16,0},{24,8},{1,17},{9,25},{17,1},{25,9},{2,18},{10... | collective-permute-start | bytes 196616 | tf_op jit(solution)/shard_map/ppermute | solution.py:35
  59.9 5.4 %collective-permute-start.20 = (bf16[32,1024]{1,0:T(8,128)(2,1)S(1)}, bf16[32,1024]{1,0:T(8,128)(2,1)S(1)}, u32[]{:S(2)}, u32[]{:S(2)}) collective-permute-start(bf16[32,1024]{1,0:T(8,128)(2,1)S(1)} %slice.50), channel_id=1, source_target_pairs={{0,16},{8,24},{16,0},{24,8},{1,17},{9,25},{17,1},{25,9},{2,18},{10... | collective-permute-start | bytes 196616 | tf_op jit(solution)/shard_map/ppermute | solution.py:35
  61.2 6.2 %collective-permute-start.23 = (bf16[32,1024]{1,0:T(8,128)(2,1)S(1)}, bf16[32,1024]{1,0:T(8,128)(2,1)S(1)}, u32[]{:S(2)}, u32[]{:S(2)}) collective-permute-start(bf16[32,1024]{1,0:T(8,128)(2,1)S(1)} %slice.52), channel_id=1, source_target_pairs={{0,16},{8,24},{16,0},{24,8},{1,17},{9,25},{17,1},{25,9},{2,18},{10... | collective-permute-start | bytes 196616 | tf_op jit(solution)/shard_map/ppermute | solution.py:35
  62.2 5.9 %collective-permute-start.26 = (bf16[32,1024]{1,0:T(8,128)(2,1)S(1)}, bf16[32,1024]{1,0:T(8,128)(2,1)S(1)}, u32[]{:S(2)}, u32[]{:S(2)}) collective-permute-start(bf16[32,1024]{1,0:T(8,128)(2,1)S(1)} %slice.54), channel_id=1, source_target_pairs={{0,16},{8,24},{16,0},{24,8},{1,17},{9,25},{17,1},{25,9},{2,18},{10... | collective-permute-start | bytes 196616 | tf_op jit(solution)/shard_map/ppermute | solution.py:35
  65.4 6.5 %collective-permute-start.21 = (bf16[32,1024]{1,0:T(8,128)(2,1)S(1)}, bf16[32,1024]{1,0:T(8,128)(2,1)S(1)}, u32[]{:S(2)}, u32[]{:S(2)}) collective-permute-start(bf16[32,1024]{1,0:T(8,128)(2,1)S(1)} %add_convert_fusion.8), channel_id=1, source_target_pairs={{0,3},{1,2},{2,1},{3,0},{4,7},{5,6},{6,5},{7,4},{8,11},{9,10},{10,... | collective-permute-start | bytes 196616 | tf_op jit(solution)/shard_map/ppermute | solution.py:35
  67.4 6.4 %collective-permute-start.24 = (bf16[32,1024]{1,0:T(8,128)(2,1)S(1)}, bf16[32,1024]{1,0:T(8,128)(2,1)S(1)}, u32[]{:S(2)}, u32[]{:S(2)}) collective-permute-start(bf16[32,1024]{1,0:T(8,128)(2,1)S(1)} %add_convert_fusion.7), channel_id=1, source_target_pairs={{0,2},{1,3},{2,0},{3,1},{4,6},{5,7},{6,4},{7,5},{8,10},{9,11},{10,... | collective-permute-start | bytes 196616 | tf_op jit(solution)/shard_map/ppermute | solution.py:35
  68.1 5.8 %collective-permute-start.27 = (bf16[32,1024]{1,0:T(8,128)(2,1)S(1)}, bf16[32,1024]{1,0:T(8,128)(2,1)S(1)}, u32[]{:S(2)}, u32[]{:S(2)}) collective-permute-start(bf16[32,1024]{1,0:T(8,128)(2,1)S(1)} %add_convert_fusion.6), channel_id=1, source_target_pairs={{0,1},{1,0},{2,3},{3,2},{4,5},{5,4},{6,7},{7,6},{8,9},{9,8},{10,11... | collective-permute-start | bytes 196616 | tf_op jit(solution)/shard_map/ppermute | solution.py:35
  73.9 4.0 %collective-permute-start.33 = (bf16[16,1024]{1,0:T(8,128)(2,1)S(1)}, bf16[16,1024]{1,0:T(8,128)(2,1)S(1)}, u32[]{:S(2)}, u32[]{:S(2)}) collective-permute-start(bf16[16,1024]{1,0:T(8,128)(2,1)S(1)} %get-tuple-element.51), channel_id=1, source_target_pairs={{0,4},{4,0},{1,5},{5,1},{2,6},{6,2},{3,7},{7,3},{8,12},{12,8},{9,1... | collective-permute-start | bytes 98312 | tf_op jit(solution)/shard_map/ppermute | solution.py:35
  74.8 4.1 %collective-permute-start.30 = (bf16[16,1024]{1,0:T(8,128)(2,1)S(1)}, bf16[16,1024]{1,0:T(8,128)(2,1)S(1)}, u32[]{:S(2)}, u32[]{:S(2)}) collective-permute-start(bf16[16,1024]{1,0:T(8,128)(2,1)S(1)} %get-tuple-element.52.refs_0_), channel_id=1, source_target_pairs={{0,8},{8,0},{16,24},{24,16},{1,9},{9,1},{17,25},{25,17},{2,10},{10... | collective-permute-start | bytes 98312 | tf_op jit(solution)/shard_map/ppermute | solution.py:35
  74.8 5.7 %collective-permute-start.31 = (bf16[16,1024]{1,0:T(8,128)(2,1)S(1)}, bf16[16,1024]{1,0:T(8,128)(2,1)S(1)}, u32[]{:S(2)}, u32[]{:S(2)}) collective-permute-start(bf16[16,1024]{1,0:T(8,128)(2,1)S(1)} %get-tuple-element.52.refs_0_), channel_id=1, source_target_pairs={{0,16},{8,24},{16,0},{24,8},{1,17},{9,25},{17,1},{25,9},{2,18},{10... | collective-permute-start | bytes 98312 | tf_op jit(solution)/shard_map/ppermute | solution.py:35
  76.2 4.3 %collective-permute-start.32 = (bf16[16,1024]{1,0:T(8,128)(2,1)S(1)}, bf16[16,1024]{1,0:T(8,128)(2,1)S(1)}, u32[]{:S(2)}, u32[]{:S(2)}) collective-permute-start(bf16[16,1024]{1,0:T(8,128)(2,1)S(1)} %get-tuple-element.52.refs_0_), channel_id=1, source_target_pairs={{0,24},{8,16},{16,8},{24,0},{1,25},{9,17},{17,9},{25,1},{2,26},{10... | collective-permute-start | bytes 98312 | tf_op jit(solution)/shard_map/ppermute | solution.py:35
  77.9 2.6 %collective-permute-start.34 = (bf16[16,1024]{1,0:T(8,128)(2,1)S(1)}, bf16[16,1024]{1,0:T(8,128)(2,1)S(1)}, u32[]{:S(2)}, u32[]{:S(2)}) collective-permute-start(bf16[16,1024]{1,0:T(8,128)(2,1)S(1)} %collective-permute-done.33.refs_4_), channel_id=1, source_target_pairs={{0,8},{8,0},{16,24},{24,16},{1,9},{9,1},{17,25},{25,17},{2,10},{10... | collective-permute-start | bytes 98312 | tf_op jit(solution)/shard_map/ppermute | solution.py:35
  77.9 3.9 %collective-permute-start.35 = (bf16[16,1024]{1,0:T(8,128)(2,1)S(1)}, bf16[16,1024]{1,0:T(8,128)(2,1)S(1)}, u32[]{:S(2)}, u32[]{:S(2)}) collective-permute-start(bf16[16,1024]{1,0:T(8,128)(2,1)S(1)} %collective-permute-done.33.refs_4_), channel_id=1, source_target_pairs={{0,16},{8,24},{16,0},{24,8},{1,17},{9,25},{17,1},{25,9},{2,18},{10... | collective-permute-start | bytes 98312 | tf_op jit(solution)/shard_map/ppermute | solution.py:35
  78.9 3.3 %collective-permute-start.36 = (bf16[16,1024]{1,0:T(8,128)(2,1)S(1)}, bf16[16,1024]{1,0:T(8,128)(2,1)S(1)}, u32[]{:S(2)}, u32[]{:S(2)}) collective-permute-start(bf16[16,1024]{1,0:T(8,128)(2,1)S(1)} %collective-permute-done.33.refs_4_), channel_id=1, source_target_pairs={{0,24},{8,16},{16,8},{24,0},{1,25},{9,17},{17,9},{25,1},{2,26},{10... | collective-permute-start | bytes 98312 | tf_op jit(solution)/shard_map/ppermute | solution.py:35

commit v5 on v4

--- a/solution.py
+++ b/solution.py
@@ -11,15 +11,13 @@
 BF16, F32 = jnp.bfloat16, jnp.float32
 HEAD = 53
 VMEM = pl.BlockSpec(memory_space=pltpu.VMEM)
-SMEM = pl.BlockSpec(memory_space=pltpu.SMEM)
 
 
 def call(body, shapes, *args, cost=(1 << 30, 1 << 22)):
-    specs = [SMEM if a.dtype == jnp.int32 else VMEM for a in args]
     return pl.pallas_call(
         body,
         out_shape=shapes,
-        in_specs=specs,
+        in_specs=[VMEM] * len(args),
         out_specs=jax.tree.map(lambda _: VMEM, shapes),
         cost_estimate=pl.CostEstimate(flops=cost[0], bytes_accessed=cost[1], transcendentals=0),
         compiler_params=pltpu.CompilerParams(vmem_limit_bytes=6 << 20),
@@ -83,7 +81,7 @@
     return stats.astype(BF16)
 
 
-def slots_body(width, n, experts, batches, where_ref, *refs):
+def slots_body(width, n, experts, batches, *refs):
     part_refs, scaled_ref, keep_ref, send_ref, held = refs[:n], refs[n], *refs[n + 1 :]
     logits, inv_rms = logits_of(*part_refs[:3], part_refs[3:], width)
     top = jnp.max(logits, axis=1, keepdims=True)
@@ -97,7 +95,7 @@
     held[:, share:] = mass_lanes(top + jnp.log(total), held.shape[1] - share)
     for h in range(experts):
         for r in range(batches):
-            at = ((where_ref[1] ^ h) * batches + (where_ref[0] ^ r)) * rows
+            at = ((lax.axis_index("expert") ^ h) * batches + (lax.axis_index("batch") ^ r)) * rows
             to = (h * (batches // 2) + r // 2) * rows
             target = send_ref if r % 2 else keep_ref
             target[to : to + rows] = held[pl.ds(pl.multiple_of(at, rows), rows)]
@@ -123,7 +121,7 @@
     return near + [(r, h) for r in range(batches) for h in range(1, experts)]
 
 
-def combine_body(width, n, experts, batches, where_ref, *refs):
+def combine_body(width, n, experts, batches, *refs):
     part_refs, out_ref, held = refs[:n], refs[n], refs[n + 1]
     logits, _ = logits_of(*part_refs[:3], part_refs[3:], width)
     raised = jnp.exp(logits - jnp.max(logits, axis=0, keepdims=True))
@@ -131,7 +129,7 @@
     rows = logits.shape[0] // (experts * batches)
     blocks = []
     for r, h in slot_order(batches, experts):
-        at = ((where_ref[1] ^ h) * batches + (where_ref[0] ^ r)) * rows
+        at = ((lax.axis_index("expert") ^ h) * batches + (lax.axis_index("batch") ^ r)) * rows
         blocks.append(held[pl.ds(pl.multiple_of(at, rows), rows)])
     out_ref[...] = jnp.concatenate(blocks, axis=0).T.astype(BF16)
 
@@ -149,10 +147,10 @@
         out_ref[h * rows : (h + 1) * rows] = out.astype(BF16)
 
 
-def gate_up_body(s, last, where_ref, *refs):
+def gate_up_body(s, last, *refs):
     low_ref, high_ref, gate_ref, up_ref = refs[:4]
     share = low_ref.shape[1]
-    at = pl.ds(pl.multiple_of((where_ref[2] ^ s) * share, share), share)
+    at = pl.ds(pl.multiple_of((lax.axis_index("tensor") ^ s) * share, share), share)
     x = jnp.concatenate([low_ref[...], high_ref[...]], axis=0)
     g = jnp.dot(x, gate_ref[0, at], preferred_element_type=F32)
     u = jnp.dot(x, up_ref[0, at], preferred_element_type=F32)
@@ -165,9 +163,9 @@
         refs[-1][...] = u
 
 
-def down_body(s, where_ref, hidden_ref, down_ref, keep_ref, send_ref):
+def down_body(s, hidden_ref, down_ref, keep_ref, send_ref):
     share = keep_ref.shape[1]
-    at = pl.ds(pl.multiple_of((where_ref[2] ^ s) * share, share), share)
+    at = pl.ds(pl.multiple_of((lax.axis_index("tensor") ^ s) * share, share), share)
     out = jnp.dot(hidden_ref[...], down_ref[0, :, at], preferred_element_type=F32).astype(BF16)
     half = out.shape[0] // 2
     keep_ref[...] = out[:half]
@@ -213,7 +211,6 @@
     for n in (batches, experts, tensors):
         assert n & (n - 1) == 0
     assert tokens.shape[0] == 1 and w_gate.shape[0] == 1
-    where = jnp.stack([lax.axis_index(a) for a in ("batch", "expert", "tensor")]).astype(jnp.int32)
     width = w_gate.shape[1]
     token_count, share = tokens.shape[1:]
     slots = phi.shape[1]
@@ -251,13 +248,13 @@
     keep, send = pl.pallas_call(
         functools.partial(slots_body, width, parts_count, experts, batches),
         out_shape=[shape((half * rows, share + 128), BF16)] * 2,
-        in_specs=[SMEM] + [VMEM] * (parts_count + 1),
+        in_specs=[VMEM] * (parts_count + 1),
         out_specs=[VMEM] * 2,
         scratch_shapes=[pltpu.VMEM((slots, share + 128), BF16)],
         cost_estimate=pl.CostEstimate(flops=1 << 30, bytes_accessed=1 << 22, transcendentals=0),
         compiler_params=pltpu.CompilerParams(vmem_limit_bytes=6 << 20),
         name="slots",
-    )(where, *parts, scaled)
+    )(*parts, scaled)
     messages = call(
         functools.partial(merge_body, share),
         [shape((rows, share + 128), BF16)] * half,
@@ -267,13 +264,13 @@
     combine = pl.pallas_call(
         functools.partial(combine_body, width, parts_count, experts, batches),
         out_shape=shape((token_count, slots), BF16),
-        in_specs=[SMEM] + [VMEM] * parts_count,
+        in_specs=[VMEM] * parts_count,
         out_specs=VMEM,
         scratch_shapes=[pltpu.VMEM((slots, token_count), F32)],
         cost_estimate=pl.CostEstimate(flops=1 << 30, bytes_accessed=1 << 22, transcendentals=0),
         compiler_params=pltpu.CompilerParams(vmem_limit_bytes=6 << 20),
         name="combine",
-    )(where, *parts)
+    )(*parts)
     count = batches // 2
     arrived = [
         m if i == 0 else swap(m, ("batch", "expert"), i % count * 2 * experts + i // count)
@@ -306,7 +303,6 @@
             shape((all_rows, hidden_share), BF16)
             if last
             else [shape((all_rows, hidden_share), F32)] * 2,
-            where,
             piece,
             swap(piece, "batch", 1),
             w_gate,
@@ -319,8 +315,7 @@
         keep, send = call(
             functools.partial(down_body, s),
             [shape((all_rows // 2, share), BF16)] * 2,
-            where,
-            carry,
+                carry,
             w_down,
             cost=(2 * all_rows * hidden_share * share, 1 << 23),
         )

time: 83.5 us -> 78.6 us (0.941)
  Pallas kernels: 23 us -> 17.6 us
    pallas_call x11, Pallas kernels: 10.6 us -> 6.22 us  [call(): pl.pallas_call(body, out_shape=shapes, in_specs=[VMEM] * len(args), out_s...]
  transfers between devices with their start and end apart: 37 -> 37, of which waited for: 14 -> 14; matrix products, arithmetic and copies ran while one was open for 0% -> 0% of each run, Pallas kernels for 20% -> 17%
where the time goes in v5:
time: 78.6 us; the launch traced here: 78.4 us
  starting transfers between devices  34.3 us (44%)
  waiting for transfers between devices  25.7 us (33%)
  Pallas kernels  17.6 us (22%)
    ppermute x37, starting transfers between devices, swap(): return lax.ppermute(x, axes, [(i, i ^ bit) for i in range(count)])  34.3 us
    ppermute x37, waiting for transfers between devices, swap(): return lax.ppermute(x, axes, [(i, i ^ bit) for i in range(count)])  25.7 us
    pallas_call x3, Pallas kernels, fetch(): pl.pallas_call(fetch_body, out_shape=[pltpu.VMEM(a.shape, a.dtype) for a...  9.28 us
    pallas_call x11, Pallas kernels, call(): pl.pallas_call(body, out_shape=shapes, in_specs=[VMEM] * len(args), out_s...  6.22 us
  transfers between devices with their start and end apart: 37, of which 14 were waited for; matrix products, arithmetic and copies ran while one was open for 0% of the time, Pallas kernels for 17%

profile of v5, /device:TPU:0, one launch (start us, length us, event | category | flops | bytes accessed | tf_op | source)
XLA Modules:
  0.0 78.4 jit_solution(2885394952214001695)
XLA Ops:
  0.0 1.5 %logits.1 = (bf16[256,1024]{1,0:T(8,128)(2,1)S(1)}, f32[136,256]{1,0:T(8,128)S(1)}, f32[72,256]{1,0:T(8,128)S(1)}) custom-call(bf16[1,256,1024]{2,1,0:T(8,128)(2,1)} %tok_hbm.1, bf16[1024]{0:T(1024)(128)(2,1)} %gain_hbm.1, bf16[1024,128]{1,0:T(8,128)(2,1)} %phi_hbm.1), custom_call_target="tpu_custom_call" | custom-call | flops 1073741824 | bytes 4194304 | tf_op jit(solution)/shard_map/logits/pallas_call | solution.py:220
  1.5 3.1 %collective-permute-start = (f32[136,256]{1,0:T(8,128)S(1)}, f32[136,256]{1,0:T(8,128)S(1)}, u32[]{:S(2)}, u32[]{:S(2)}) collective-permute-start(f32[136,256]{1,0:T(8,128)S(1)} %get-tuple-element.28.refs_0_), channel_id=1, source_target_pairs={{0,1},{1,0},{2,3},{3,2},{4,5},{5,4},{6,7},{7,6},{8,9},{9,8},{10,11... | collective-permute-start | bytes 417800 | tf_op jit(solution)/shard_map/ppermute | solution.py:33
  4.6 2.6 %collective-permute-start.2 = (f32[72,256]{1,0:T(8,128)S(1)}, f32[72,256]{1,0:T(8,128)S(1)}, u32[]{:S(2)}, u32[]{:S(2)}) collective-permute-start(f32[72,256]{1,0:T(8,128)S(1)} %get-tuple-element.29), channel_id=1, source_target_pairs={{0,2},{1,3},{2,0},{3,1},{4,6},{5,7},{6,4},{7,5},{8,10},{9,11},{10,... | collective-permute-start | bytes 221192 | tf_op jit(solution)/shard_map/ppermute | solution.py:33
  7.2 0.0 collective-permute-start.3
  7.2 1.9 %collective-permute-done.refs_1_ = f32[136,256]{1,0:T(8,128)S(1)} collective-permute-done((f32[136,256]{1,0:T(8,128)S(1)}, f32[136,256]{1,0:T(8,128)S(1)}, u32[]{:S(2)}, u32[]{:S(2)}) %collective-permute-start) | collective-permute-done | bytes 139296 | tf_op jit(solution)/shard_map/ppermute | solution.py:33
  9.1 3.2 %collective-permute-start.1 = (f32[64,256]{1,0:T(8,128)S(1)}, f32[64,256]{1,0:T(8,128)S(1)}, u32[]{:S(2)}, u32[]{:S(2)}) collective-permute-start(f32[64,256]{1,0:T(8,128)S(1)} %slice_add_fusion), channel_id=1, source_target_pairs={{0,2},{1,3},{2,0},{3,1},{4,6},{5,7},{6,4},{7,5},{8,10},{9,11},{10,... | collective-permute-start | bytes 196616 | tf_op jit(solution)/shard_map/ppermute | solution.py:33
  12.3 5.0 %collective-permute-done.1 = f32[64,256]{1,0:T(8,128)S(1)} collective-permute-done((f32[64,256]{1,0:T(8,128)S(1)}, f32[64,256]{1,0:T(8,128)S(1)}, u32[]{:S(2)}, u32[]{:S(2)}) %collective-permute-start.1) | collective-permute-done | bytes 65568 | tf_op jit(solution)/shard_map/ppermute | solution.py:33
  17.3 0.0 collective-permute-done.2.refs_3_
  17.4 0.4 slots.1
  17.8 0.1 collective-permute-start.4
  17.9 3.1 %fetch.3.refs_2_ = bf16[1,4096,896]{2,1,0:T(8,128)(2,1)S(1)} custom-call(bf16[1,4096,896]{2,1,0:T(8,128)(2,1)} %refs_0_.3), custom_call_target="tpu_custom_call" | custom-call | flops 1073741824 | bytes 33554432 | tf_op jit(solution)/shard_map/fetch/pallas_call | solution.py:193
  21.0 0.0 collective-permute-done.4.came_ref
  21.0 0.2 shard_map.64
  21.2 1.6 %collective-permute-start.5 = (bf16[16,1152]{1,0:T(8,128)(2,1)S(1)}, bf16[16,1152]{1,0:T(8,128)(2,1)S(1)}, u32[]{:S(2)}, u32[]{:S(2)}) collective-permute-start(bf16[16,1152]{1,0:T(8,128)(2,1)S(1)} %get-tuple-element.34), channel_id=1, source_target_pairs={{0,16},{4,20},{8,24},{12,28},{16,0},{20,4},{24,8},{28,12},{1,17},{... | collective-permute-start | bytes 110600 | tf_op jit(solution)/shard_map/ppermute | solution.py:33
  22.8 1.5 %collective-permute-start.6 = (bf16[16,1152]{1,0:T(8,128)(2,1)S(1)}, bf16[16,1152]{1,0:T(8,128)(2,1)S(1)}, u32[]{:S(2)}, u32[]{:S(2)}) collective-permute-start(bf16[16,1152]{1,0:T(8,128)(2,1)S(1)} %get-tuple-element.35), channel_id=1, source_target_pairs={{0,4},{4,0},{8,12},{12,8},{16,20},{20,16},{24,28},{28,24},{1,5},{5... | collective-permute-start | bytes 110600 | tf_op jit(solution)/shard_map/ppermute | solution.py:33
  24.3 0.5 collective-permute-start.7
  24.8 3.1 %fetch.4.refs_3_ = bf16[1,4096,896]{2,1,0:T(8,128)(2,1)S(1)} custom-call(bf16[1,4096,896]{2,1,0:T(8,128)(2,1)} %refs_0_.4), custom_call_target="tpu_custom_call" | custom-call | flops 1073741824 | bytes 33554432 | tf_op jit(solution)/shard_map/fetch/pallas_call | solution.py:193
  27.9 1.3 %collective-permute-done.7.refs_3_ = bf16[16,1152]{1,0:T(8,128)(2,1)S(1)} collective-permute-done((bf16[16,1152]{1,0:T(8,128)(2,1)S(1)}, bf16[16,1152]{1,0:T(8,128)(2,1)S(1)}, u32[]{:S(2)}, u32[]{:S(2)}) %collective-permute-start.7) | collective-permute-done | bytes 36896 | tf_op jit(solution)/shard_map/ppermute | solution.py:33
  29.2 0.2 shard_map.65
  29.4 0.6 collective-permute-start.17
  29.9 3.1 %fetch.5.down_ref = bf16[1,896,4096]{2,1,0:T(8,128)(2,1)S(1)} custom-call(bf16[1,896,4096]{2,1,0:T(8,128)(2,1)} %refs_0_.5), custom_call_target="tpu_custom_call" | custom-call | flops 1073741824 | bytes 33554432 | tf_op jit(solution)/shard_map/fetch/pallas_call | solution.py:193
  33.0 0.1 collective-permute-start.14
  33.1 3.0 %collective-permute-start.15 = (bf16[32,1024]{1,0:T(8,128)(2,1)S(1)}, bf16[32,1024]{1,0:T(8,128)(2,1)S(1)}, u32[]{:S(2)}, u32[]{:S(2)}) collective-permute-start(bf16[32,1024]{1,0:T(8,128)(2,1)S(1)} %shard_map.65), channel_id=1, source_target_pairs={{0,17},{1,16},{2,19},{3,18},{8,25},{9,24},{10,27},{11,26},{16,1},{... | collective-permute-start | bytes 196616 | tf_op jit(solution)/shard_map/ppermute | solution.py:33
  36.1 2.0 %collective-permute-start.11 = (bf16[32,1024]{1,0:T(8,128)(2,1)S(1)}, bf16[32,1024]{1,0:T(8,128)(2,1)S(1)}, u32[]{:S(2)}, u32[]{:S(2)}) collective-permute-start(bf16[32,1024]{1,0:T(8,128)(2,1)S(1)} %shard_map.65), channel_id=1, source_target_pairs={{0,3},{1,2},{2,1},{3,0},{4,7},{5,6},{6,5},{7,4},{8,11},{9,10},{10,... | collective-permute-start | bytes 196616 | tf_op jit(solution)/shard_map/ppermute | solution.py:33
  38.1 0.1 collective-permute-start.18
  38.2 0.9 %collective-permute-done.15 = bf16[32,1024]{1,0:T(8,128)(2,1)S(1)} collective-permute-done((bf16[32,1024]{1,0:T(8,128)(2,1)S(1)}, bf16[32,1024]{1,0:T(8,128)(2,1)S(1)}, u32[]{:S(2)}, u32[]{:S(2)}) %collective-permute-start.15) | collective-permute-done | bytes 65568 | tf_op jit(solution)/shard_map/ppermute | solution.py:33
  39.0 3.1 %collective-permute-done.11 = bf16[32,1024]{1,0:T(8,128)(2,1)S(1)} collective-permute-done((bf16[32,1024]{1,0:T(8,128)(2,1)S(1)}, bf16[32,1024]{1,0:T(8,128)(2,1)S(1)}, u32[]{:S(2)}, u32[]{:S(2)}) %collective-permute-start.11) | collective-permute-done | bytes 65568 | tf_op jit(solution)/shard_map/ppermute | solution.py:33
  42.1 0.5 collective-permute-start.12
  42.6 0.9 %collective-permute-done.8 = bf16[32,1024]{1,0:T(8,128)(2,1)S(1)} collective-permute-done((bf16[32,1024]{1,0:T(8,128)(2,1)S(1)}, bf16[32,1024]{1,0:T(8,128)(2,1)S(1)}, u32[]{:S(2)}, u32[]{:S(2)}) %collective-permute-start.8) | collective-permute-done | bytes 65568 | tf_op jit(solution)/shard_map/ppermute | solution.py:33
  43.5 0.9 %collective-permute-start.9 = (bf16[32,1024]{1,0:T(8,128)(2,1)S(1)}, bf16[32,1024]{1,0:T(8,128)(2,1)S(1)}, u32[]{:S(2)}, u32[]{:S(2)}) collective-permute-start(bf16[32,1024]{1,0:T(8,128)(2,1)S(1)} %collective-permute-done.8), channel_id=1, source_target_pairs={{0,16},{8,24},{16,0},{24,8},{1,17},{9,25},{17,1},{25,9},{2,18},{10... | collective-permute-start | bytes 196616 | tf_op jit(solution)/shard_map/ppermute | solution.py:33
  44.5 1.9 %collective-permute-done.12 = bf16[32,1024]{1,0:T(8,128)(2,1)S(1)} collective-permute-done((bf16[32,1024]{1,0:T(8,128)(2,1)S(1)}, bf16[32,1024]{1,0:T(8,128)(2,1)S(1)}, u32[]{:S(2)}, u32[]{:S(2)}) %collective-permute-start.12) | collective-permute-done | bytes 65568 | tf_op jit(solution)/shard_map/ppermute | solution.py:33
  46.4 1.4 %collective-permute-done.9 = bf16[32,1024]{1,0:T(8,128)(2,1)S(1)} collective-permute-done((bf16[32,1024]{1,0:T(8,128)(2,1)S(1)}, bf16[32,1024]{1,0:T(8,128)(2,1)S(1)}, u32[]{:S(2)}, u32[]{:S(2)}) %collective-permute-start.9) | collective-permute-done | bytes 65568 | tf_op jit(solution)/shard_map/ppermute | solution.py:33
  47.8 0.7 shard_map.66
  48.6 0.7 shard_map.67
  49.3 0.7 shard_map.68
  50.1 0.7 shard_map.69.hidden_ref
  50.8 0.5 shard_map.73
  51.3 0.6 collective-permute-start.28
  51.8 0.4 shard_map.70
  52.3 0.1 collective-permute-start.19
  52.4 0.5 shard_map.71
  52.9 0.5 collective-permute-start.22
  53.4 0.4 shard_map.72
  53.8 0.1 collective-permute-start.25
  54.0 1.0 %collective-permute-start.29 = (bf16[32,1024]{1,0:T(8,128)(2,1)S(1)}, bf16[32,1024]{1,0:T(8,128)(2,1)S(1)}, u32[]{:S(2)}, u32[]{:S(2)}) collective-permute-start(bf16[32,1024]{1,0:T(8,128)(2,1)S(1)} %slice.56), channel_id=1, source_target_pairs={{0,16},{8,24},{16,0},{24,8},{1,17},{9,25},{17,1},{25,9},{2,18},{10... | collective-permute-start | bytes 196616 | tf_op jit(solution)/shard_map/ppermute | solution.py:33
  55.0 1.2 %collective-permute-start.20 = (bf16[32,1024]{1,0:T(8,128)(2,1)S(1)}, bf16[32,1024]{1,0:T(8,128)(2,1)S(1)}, u32[]{:S(2)}, u32[]{:S(2)}) collective-permute-start(bf16[32,1024]{1,0:T(8,128)(2,1)S(1)} %slice.50), channel_id=1, source_target_pairs={{0,16},{8,24},{16,0},{24,8},{1,17},{9,25},{17,1},{25,9},{2,18},{10... | collective-permute-start | bytes 196616 | tf_op jit(solution)/shard_map/ppermute | solution.py:33
  56.3 1.0 %collective-permute-start.23 = (bf16[32,1024]{1,0:T(8,128)(2,1)S(1)}, bf16[32,1024]{1,0:T(8,128)(2,1)S(1)}, u32[]{:S(2)}, u32[]{:S(2)}) collective-permute-start(bf16[32,1024]{1,0:T(8,128)(2,1)S(1)} %slice.52), channel_id=1, source_target_pairs={{0,16},{8,24},{16,0},{24,8},{1,17},{9,25},{17,1},{25,9},{2,18},{10... | collective-permute-start | bytes 196616 | tf_op jit(solution)/shard_map/ppermute | solution.py:33
  57.3 1.2 %collective-permute-start.26 = (bf16[32,1024]{1,0:T(8,128)(2,1)S(1)}, bf16[32,1024]{1,0:T(8,128)(2,1)S(1)}, u32[]{:S(2)}, u32[]{:S(2)}) collective-permute-start(bf16[32,1024]{1,0:T(8,128)(2,1)S(1)} %slice.54), channel_id=1, source_target_pairs={{0,16},{8,24},{16,0},{24,8},{1,17},{9,25},{17,1},{25,9},{2,18},{10... | collective-permute-start | bytes 196616 | tf_op jit(solution)/shard_map/ppermute | solution.py:33
  58.5 1.9 %collective-permute-done.20 = bf16[32,1024]{1,0:T(8,128)(2,1)S(1)} collective-permute-done((bf16[32,1024]{1,0:T(8,128)(2,1)S(1)}, bf16[32,1024]{1,0:T(8,128)(2,1)S(1)}, u32[]{:S(2)}, u32[]{:S(2)}) %collective-permute-start.20) | collective-permute-done | bytes 65568 | tf_op jit(solution)/shard_map/ppermute | solution.py:33
  60.5 2.0 %collective-permute-start.21 = (bf16[32,1024]{1,0:T(8,128)(2,1)S(1)}, bf16[32,1024]{1,0:T(8,128)(2,1)S(1)}, u32[]{:S(2)}, u32[]{:S(2)}) collective-permute-start(bf16[32,1024]{1,0:T(8,128)(2,1)S(1)} %add_convert_fusion.8), channel_id=1, source_target_pairs={{0,3},{1,2},{2,1},{3,0},{4,7},{5,6},{6,5},{7,4},{8,11},{9,10},{10,... | collective-permute-start | bytes 196616 | tf_op jit(solution)/shard_map/ppermute | solution.py:33
  62.5 0.6 collective-permute-start.24
  63.2 1.9 %collective-permute-start.27 = (bf16[32,1024]{1,0:T(8,128)(2,1)S(1)}, bf16[32,1024]{1,0:T(8,128)(2,1)S(1)}, u32[]{:S(2)}, u32[]{:S(2)}) collective-permute-start(bf16[32,1024]{1,0:T(8,128)(2,1)S(1)} %add_convert_fusion.6), channel_id=1, source_target_pairs={{0,1},{1,0},{2,3},{3,2},{4,5},{5,4},{6,7},{7,6},{8,9},{9,8},{10,11... | collective-permute-start | bytes 196616 | tf_op jit(solution)/shard_map/ppermute | solution.py:33
  65.1 1.9 %collective-permute-done.21 = bf16[32,1024]{1,0:T(8,128)(2,1)S(1)} collective-permute-done((bf16[32,1024]{1,0:T(8,128)(2,1)S(1)}, bf16[32,1024]{1,0:T(8,128)(2,1)S(1)}, u32[]{:S(2)}, u32[]{:S(2)}) %collective-permute-start.21) | collective-permute-done | bytes 65568 | tf_op jit(solution)/shard_map/ppermute | solution.py:33
  67.0 2.0 %collective-permute-done.24 = bf16[32,1024]{1,0:T(8,128)(2,1)S(1)} collective-permute-done((bf16[32,1024]{1,0:T(8,128)(2,1)S(1)}, bf16[32,1024]{1,0:T(8,128)(2,1)S(1)}, u32[]{:S(2)}, u32[]{:S(2)}) %collective-permute-start.24) | collective-permute-done | bytes 65568 | tf_op jit(solution)/shard_map/ppermute | solution.py:33
  69.0 0.9 %collective-permute-start.33 = (bf16[16,1024]{1,0:T(8,128)(2,1)S(1)}, bf16[16,1024]{1,0:T(8,128)(2,1)S(1)}, u32[]{:S(2)}, u32[]{:S(2)}) collective-permute-start(bf16[16,1024]{1,0:T(8,128)(2,1)S(1)} %get-tuple-element.51), channel_id=1, source_target_pairs={{0,4},{4,0},{1,5},{5,1},{2,6},{6,2},{3,7},{7,3},{8,12},{12,8},{9,1... | collective-permute-start | bytes 98312 | tf_op jit(solution)/shard_map/ppermute | solution.py:33
  69.9 1.4 %collective-permute-start.31 = (bf16[16,1024]{1,0:T(8,128)(2,1)S(1)}, bf16[16,1024]{1,0:T(8,128)(2,1)S(1)}, u32[]{:S(2)}, u32[]{:S(2)}) collective-permute-start(bf16[16,1024]{1,0:T(8,128)(2,1)S(1)} %get-tuple-element.52.refs_0_), channel_id=1, source_target_pairs={{0,16},{8,24},{16,0},{24,8},{1,17},{9,25},{17,1},{25,9},{2,18},{10... | collective-permute-start | bytes 98312 | tf_op jit(solution)/shard_map/ppermute | solution.py:33
  71.3 0.5 collective-permute-start.32
  71.7 1.3 %collective-permute-done.33.refs_4_ = bf16[16,1024]{1,0:T(8,128)(2,1)S(1)} collective-permute-done((bf16[16,1024]{1,0:T(8,128)(2,1)S(1)}, bf16[16,1024]{1,0:T(8,128)(2,1)S(1)}, u32[]{:S(2)}, u32[]{:S(2)}) %collective-permute-start.33) | collective-permute-done | bytes 32800 | tf_op jit(solution)/shard_map/ppermute | solution.py:33
  73.0 1.0 %collective-permute-start.35 = (bf16[16,1024]{1,0:T(8,128)(2,1)S(1)}, bf16[16,1024]{1,0:T(8,128)(2,1)S(1)}, u32[]{:S(2)}, u32[]{:S(2)}) collective-permute-start(bf16[16,1024]{1,0:T(8,128)(2,1)S(1)} %collective-permute-done.33.refs_4_), channel_id=1, source_target_pairs={{0,16},{8,24},{16,0},{24,8},{1,17},{9,25},{17,1},{25,9},{2,18},{10... | collective-permute-start | bytes 98312 | tf_op jit(solution)/shard_map/ppermute | solution.py:33
  74.0 0.9 %collective-permute-start.36 = (bf16[16,1024]{1,0:T(8,128)(2,1)S(1)}, bf16[16,1024]{1,0:T(8,128)(2,1)S(1)}, u32[]{:S(2)}, u32[]{:S(2)}) collective-permute-start(bf16[16,1024]{1,0:T(8,128)(2,1)S(1)} %collective-permute-done.33.refs_4_), channel_id=1, source_target_pairs={{0,24},{8,16},{16,8},{24,0},{1,25},{9,17},{17,9},{25,1},{2,26},{10... | collective-permute-start | bytes 98312 | tf_op jit(solution)/shard_map/ppermute | solution.py:33
  74.9 0.2 combine.1.combine_ref
  75.1 1.8 %collective-permute-done.35.refs_6_ = bf16[16,1024]{1,0:T(8,128)(2,1)S(1)} collective-permute-done((bf16[16,1024]{1,0:T(8,128)(2,1)S(1)}, bf16[16,1024]{1,0:T(8,128)(2,1)S(1)}, u32[]{:S(2)}, u32[]{:S(2)}) %collective-permute-start.35) | collective-permute-done | bytes 32800 | tf_op jit(solution)/shard_map/ppermute | solution.py:33
  76.9 0.4 collective-permute-done.36.refs_7_
  77.3 1.1 %shard_map.74 = bf16[256,1024]{1,0:T(8,128)(2,1)} custom-call(bf16[256,128]{1,0:T(8,128)(2,1)S(1)} %combine.1.combine_ref, bf16[16,1024]{1,0:T(8,128)(2,1)S(1)} %get-tuple-element.52.refs_0_, bf16[16,1024]{1,0:T(8,128)(2,1)S(1)} %collective-permute-done.30.refs_1_, bf16[16,1024]{1,0:T(8,128)(2,1)S(1)} %collective-permute-done.31.refs_2_, ...), custom_call_target="tpu_custom_call" | custom-call | flops 1073741824 | bytes 4194304 | tf_op jit(solution)/shard_map/pallas_call | solution.py:17
  (49 shorter events, 0.4 us)
Async XLA Ops:
  1.5 7.6 %collective-permute-start = (f32[136,256]{1,0:T(8,128)S(1)}, f32[136,256]{1,0:T(8,128)S(1)}, u32[]{:S(2)}, u32[]{:S(2)}) collective-permute-start(f32[136,256]{1,0:T(8,128)S(1)} %get-tuple-element.28.refs_0_), channel_id=1, source_target_pairs={{0,1},{1,0},{2,3},{3,2},{4,5},{5,4},{6,7},{7,6},{8,9},{9,8},{10,11... | collective-permute-start | bytes 417800 | tf_op jit(solution)/shard_map/ppermute | solution.py:33
  4.6 12.7 %collective-permute-start.2 = (f32[72,256]{1,0:T(8,128)S(1)}, f32[72,256]{1,0:T(8,128)S(1)}, u32[]{:S(2)}, u32[]{:S(2)}) collective-permute-start(f32[72,256]{1,0:T(8,128)S(1)} %get-tuple-element.29), channel_id=1, source_target_pairs={{0,2},{1,3},{2,0},{3,1},{4,6},{5,7},{6,4},{7,5},{8,10},{9,11},{10,... | collective-permute-start | bytes 221192 | tf_op jit(solution)/shard_map/ppermute | solution.py:33
  7.2 10.1 %collective-permute-start.3 = (f32[72,256]{1,0:T(8,128)S(1)}, f32[72,256]{1,0:T(8,128)S(1)}, u32[]{:S(2)}, u32[]{:S(2)}) collective-permute-start(f32[72,256]{1,0:T(8,128)S(1)} %get-tuple-element.29), channel_id=1, source_target_pairs={{0,3},{1,2},{2,1},{3,0},{4,7},{5,6},{6,5},{7,4},{8,11},{9,10},{10,... | collective-permute-start | bytes 221192 | tf_op jit(solution)/shard_map/ppermute | solution.py:33
  9.1 8.2 %collective-permute-start.1 = (f32[64,256]{1,0:T(8,128)S(1)}, f32[64,256]{1,0:T(8,128)S(1)}, u32[]{:S(2)}, u32[]{:S(2)}) collective-permute-start(f32[64,256]{1,0:T(8,128)S(1)} %slice_add_fusion), channel_id=1, source_target_pairs={{0,2},{1,3},{2,0},{3,1},{4,6},{5,7},{6,4},{7,5},{8,10},{9,11},{10,... | collective-permute-start | bytes 196616 | tf_op jit(solution)/shard_map/ppermute | solution.py:33
  17.8 3.2 %collective-permute-start.4 = (bf16[64,1152]{1,0:T(8,128)(2,1)S(1)}, bf16[64,1152]{1,0:T(8,128)(2,1)S(1)}, u32[]{:S(2)}, u32[]{:S(2)}) collective-permute-start(bf16[64,1152]{1,0:T(8,128)(2,1)S(1)} %get-tuple-element.32), channel_id=1, source_target_pairs={{0,8},{8,0},{16,24},{24,16},{1,9},{9,1},{17,25},{25,17},{2,10},{10... | collective-permute-start | bytes 442376 | tf_op jit(solution)/shard_map/ppermute | solution.py:33
  21.2 6.7 %collective-permute-start.5 = (bf16[16,1152]{1,0:T(8,128)(2,1)S(1)}, bf16[16,1152]{1,0:T(8,128)(2,1)S(1)}, u32[]{:S(2)}, u32[]{:S(2)}) collective-permute-start(bf16[16,1152]{1,0:T(8,128)(2,1)S(1)} %get-tuple-element.34), channel_id=1, source_target_pairs={{0,16},{4,20},{8,24},{12,28},{16,0},{20,4},{24,8},{28,12},{1,17},{... | collective-permute-start | bytes 110600 | tf_op jit(solution)/shard_map/ppermute | solution.py:33
  22.8 5.1 %collective-permute-start.6 = (bf16[16,1152]{1,0:T(8,128)(2,1)S(1)}, bf16[16,1152]{1,0:T(8,128)(2,1)S(1)}, u32[]{:S(2)}, u32[]{:S(2)}) collective-permute-start(bf16[16,1152]{1,0:T(8,128)(2,1)S(1)} %get-tuple-element.35), channel_id=1, source_target_pairs={{0,4},{4,0},{8,12},{12,8},{16,20},{20,16},{24,28},{28,24},{1,5},{5... | collective-permute-start | bytes 110600 | tf_op jit(solution)/shard_map/ppermute | solution.py:33
  24.3 4.9 %collective-permute-start.7 = (bf16[16,1152]{1,0:T(8,128)(2,1)S(1)}, bf16[16,1152]{1,0:T(8,128)(2,1)S(1)}, u32[]{:S(2)}, u32[]{:S(2)}) collective-permute-start(bf16[16,1152]{1,0:T(8,128)(2,1)S(1)} %get-tuple-element.36), channel_id=1, source_target_pairs={{0,20},{4,16},{8,28},{12,24},{16,4},{20,0},{24,12},{28,8},{1,21},{... | collective-permute-start | bytes 110600 | tf_op jit(solution)/shard_map/ppermute | solution.py:33
  29.4 8.7 %collective-permute-start.17 = (bf16[32,1024]{1,0:T(8,128)(2,1)S(1)}, bf16[32,1024]{1,0:T(8,128)(2,1)S(1)}, u32[]{:S(2)}, u32[]{:S(2)}) collective-permute-start(bf16[32,1024]{1,0:T(8,128)(2,1)S(1)} %shard_map.65), channel_id=1, source_target_pairs={{0,16},{8,24},{16,0},{24,8},{1,17},{9,25},{17,1},{25,9},{2,18},{10... | collective-permute-start | bytes 196616 | tf_op jit(solution)/shard_map/ppermute | solution.py:33
  33.0 5.1 %collective-permute-start.14 = (bf16[32,1024]{1,0:T(8,128)(2,1)S(1)}, bf16[32,1024]{1,0:T(8,128)(2,1)S(1)}, u32[]{:S(2)}, u32[]{:S(2)}) collective-permute-start(bf16[32,1024]{1,0:T(8,128)(2,1)S(1)} %shard_map.65), channel_id=1, source_target_pairs={{0,1},{1,0},{2,3},{3,2},{4,5},{5,4},{6,7},{7,6},{8,9},{9,8},{10,11... | collective-permute-start | bytes 196616 | tf_op jit(solution)/shard_map/ppermute | solution.py:33
  33.1 5.9 %collective-permute-start.15 = (bf16[32,1024]{1,0:T(8,128)(2,1)S(1)}, bf16[32,1024]{1,0:T(8,128)(2,1)S(1)}, u32[]{:S(2)}, u32[]{:S(2)}) collective-permute-start(bf16[32,1024]{1,0:T(8,128)(2,1)S(1)} %shard_map.65), channel_id=1, source_target_pairs={{0,17},{1,16},{2,19},{3,18},{8,25},{9,24},{10,27},{11,26},{16,1},{... | collective-permute-start | bytes 196616 | tf_op jit(solution)/shard_map/ppermute | solution.py:33
  36.1 6.1 %collective-permute-start.11 = (bf16[32,1024]{1,0:T(8,128)(2,1)S(1)}, bf16[32,1024]{1,0:T(8,128)(2,1)S(1)}, u32[]{:S(2)}, u32[]{:S(2)}) collective-permute-start(bf16[32,1024]{1,0:T(8,128)(2,1)S(1)} %shard_map.65), channel_id=1, source_target_pairs={{0,3},{1,2},{2,1},{3,0},{4,7},{5,6},{6,5},{7,4},{8,11},{9,10},{10,... | collective-permute-start | bytes 196616 | tf_op jit(solution)/shard_map/ppermute | solution.py:33
  38.0 5.5 %collective-permute-start.8 = (bf16[32,1024]{1,0:T(8,128)(2,1)S(1)}, bf16[32,1024]{1,0:T(8,128)(2,1)S(1)}, u32[]{:S(2)}, u32[]{:S(2)}) collective-permute-start(bf16[32,1024]{1,0:T(8,128)(2,1)S(1)} %shard_map.65), channel_id=1, source_target_pairs={{0,2},{1,3},{2,0},{3,1},{4,6},{5,7},{6,4},{7,5},{8,10},{9,11},{10,... | collective-permute-start | bytes 196616 | tf_op jit(solution)/shard_map/ppermute | solution.py:33
  38.1 9.8 %collective-permute-start.18 = (bf16[64,1024]{1,0:T(8,128)(2,1)S(1)}, bf16[64,1024]{1,0:T(8,128)(2,1)S(1)}, u32[]{:S(2)}, u32[]{:S(2)}) collective-permute-start(bf16[64,1024]{1,0:T(8,128)(2,1)S(1)} %pad_maximum_fusion.refs_0_), channel_id=1, source_target_pairs={{0,8},{8,0},{16,24},{24,16},{1,9},{9,1},{17,25},{25,17},{2,10},{10... | collective-permute-start | bytes 393224 | tf_op jit(solution)/shard_map/ppermute | solution.py:33
  39.0 9.5 %collective-permute-start.16 = (bf16[64,1024]{1,0:T(8,128)(2,1)S(1)}, bf16[64,1024]{1,0:T(8,128)(2,1)S(1)}, u32[]{:S(2)}, u32[]{:S(2)}) collective-permute-start(bf16[64,1024]{1,0:T(8,128)(2,1)S(1)} %constant_dynamic-update-slice_fusion.4.refs_0_), channel_id=1, source_target_pairs={{0,8},{8,0},{16,24},{24,16},{1,9},{9,1},{17,25},{25,17},{2,10},{10... | collective-permute-start | bytes 393224 | tf_op jit(solution)/shard_map/ppermute | solution.py:33
  42.1 4.3 %collective-permute-start.12 = (bf16[32,1024]{1,0:T(8,128)(2,1)S(1)}, bf16[32,1024]{1,0:T(8,128)(2,1)S(1)}, u32[]{:S(2)}, u32[]{:S(2)}) collective-permute-start(bf16[32,1024]{1,0:T(8,128)(2,1)S(1)} %collective-permute-done.11), channel_id=1, source_target_pairs={{0,16},{8,24},{16,0},{24,8},{1,17},{9,25},{17,1},{25,9},{2,18},{10... | collective-permute-start | bytes 196616 | tf_op jit(solution)/shard_map/ppermute | solution.py:33
  43.5 4.3 %collective-permute-start.9 = (bf16[32,1024]{1,0:T(8,128)(2,1)S(1)}, bf16[32,1024]{1,0:T(8,128)(2,1)S(1)}, u32[]{:S(2)}, u32[]{:S(2)}) collective-permute-start(bf16[32,1024]{1,0:T(8,128)(2,1)S(1)} %collective-permute-done.8), channel_id=1, source_target_pairs={{0,16},{8,24},{16,0},{24,8},{1,17},{9,25},{17,1},{25,9},{2,18},{10... | collective-permute-start | bytes 196616 | tf_op jit(solution)/shard_map/ppermute | solution.py:33
  46.4 2.9 %collective-permute-start.13 = (bf16[64,1024]{1,0:T(8,128)(2,1)S(1)}, bf16[64,1024]{1,0:T(8,128)(2,1)S(1)}, u32[]{:S(2)}, u32[]{:S(2)}) collective-permute-start(bf16[64,1024]{1,0:T(8,128)(2,1)S(1)} %constant_dynamic-update-slice_fusion.2.refs_0_), channel_id=1, source_target_pairs={{0,8},{8,0},{16,24},{24,16},{1,9},{9,1},{17,25},{25,17},{2,10},{10... | collective-permute-start | bytes 393224 | tf_op jit(solution)/shard_map/ppermute | solution.py:33
  47.8 2.3 %collective-permute-start.10 = (bf16[64,1024]{1,0:T(8,128)(2,1)S(1)}, bf16[64,1024]{1,0:T(8,128)(2,1)S(1)}, u32[]{:S(2)}, u32[]{:S(2)}) collective-permute-start(bf16[64,1024]{1,0:T(8,128)(2,1)S(1)} %constant_dynamic-update-slice_fusion.refs_0_), channel_id=1, source_target_pairs={{0,8},{8,0},{16,24},{24,16},{1,9},{9,1},{17,25},{25,17},{2,10},{10... | collective-permute-start | bytes 393224 | tf_op jit(solution)/shard_map/ppermute | solution.py:33
  51.3 2.7 %collective-permute-start.28 = (bf16[64,1024]{1,0:T(8,128)(2,1)S(1)}, bf16[64,1024]{1,0:T(8,128)(2,1)S(1)}, u32[]{:S(2)}, u32[]{:S(2)}) collective-permute-start(bf16[64,1024]{1,0:T(8,128)(2,1)S(1)} %get-tuple-element.50), channel_id=1, source_target_pairs={{0,8},{8,0},{16,24},{24,16},{1,9},{9,1},{17,25},{25,17},{2,10},{10... | collective-permute-start | bytes 393224 | tf_op jit(solution)/shard_map/ppermute | solution.py:33
  52.3 2.7 %collective-permute-start.19 = (bf16[64,1024]{1,0:T(8,128)(2,1)S(1)}, bf16[64,1024]{1,0:T(8,128)(2,1)S(1)}, u32[]{:S(2)}, u32[]{:S(2)}) collective-permute-start(bf16[64,1024]{1,0:T(8,128)(2,1)S(1)} %get-tuple-element.44), channel_id=1, source_target_pairs={{0,8},{8,0},{16,24},{24,16},{1,9},{9,1},{17,25},{25,17},{2,10},{10... | collective-permute-start | bytes 393224 | tf_op jit(solution)/shard_map/ppermute | solution.py:33
  52.9 3.4 %collective-permute-start.22 = (bf16[64,1024]{1,0:T(8,128)(2,1)S(1)}, bf16[64,1024]{1,0:T(8,128)(2,1)S(1)}, u32[]{:S(2)}, u32[]{:S(2)}) collective-permute-start(bf16[64,1024]{1,0:T(8,128)(2,1)S(1)} %get-tuple-element.46), channel_id=1, source_target_pairs={{0,8},{8,0},{16,24},{24,16},{1,9},{9,1},{17,25},{25,17},{2,10},{10... | collective-permute-start | bytes 393224 | tf_op jit(solution)/shard_map/ppermute | solution.py:33
  53.8 3.4 %collective-permute-start.25 = (bf16[64,1024]{1,0:T(8,128)(2,1)S(1)}, bf16[64,1024]{1,0:T(8,128)(2,1)S(1)}, u32[]{:S(2)}, u32[]{:S(2)}) collective-permute-start(bf16[64,1024]{1,0:T(8,128)(2,1)S(1)} %get-tuple-element.48), channel_id=1, source_target_pairs={{0,8},{8,0},{16,24},{24,16},{1,9},{9,1},{17,25},{25,17},{2,10},{10... | collective-permute-start | bytes 393224 | tf_op jit(solution)/shard_map/ppermute | solution.py:33
  54.0 11.1 %collective-permute-start.29 = (bf16[32,1024]{1,0:T(8,128)(2,1)S(1)}, bf16[32,1024]{1,0:T(8,128)(2,1)S(1)}, u32[]{:S(2)}, u32[]{:S(2)}) collective-permute-start(bf16[32,1024]{1,0:T(8,128)(2,1)S(1)} %slice.56), channel_id=1, source_target_pairs={{0,16},{8,24},{16,0},{24,8},{1,17},{9,25},{17,1},{25,9},{2,18},{10... | collective-permute-start | bytes 196616 | tf_op jit(solution)/shard_map/ppermute | solution.py:33
  55.0 5.4 %collective-permute-start.20 = (bf16[32,1024]{1,0:T(8,128)(2,1)S(1)}, bf16[32,1024]{1,0:T(8,128)(2,1)S(1)}, u32[]{:S(2)}, u32[]{:S(2)}) collective-permute-start(bf16[32,1024]{1,0:T(8,128)(2,1)S(1)} %slice.50), channel_id=1, source_target_pairs={{0,16},{8,24},{16,0},{24,8},{1,17},{9,25},{17,1},{25,9},{2,18},{10... | collective-permute-start | bytes 196616 | tf_op jit(solution)/shard_map/ppermute | solution.py:33
  56.3 6.2 %collective-permute-start.23 = (bf16[32,1024]{1,0:T(8,128)(2,1)S(1)}, bf16[32,1024]{1,0:T(8,128)(2,1)S(1)}, u32[]{:S(2)}, u32[]{:S(2)}) collective-permute-start(bf16[32,1024]{1,0:T(8,128)(2,1)S(1)} %slice.52), channel_id=1, source_target_pairs={{0,16},{8,24},{16,0},{24,8},{1,17},{9,25},{17,1},{25,9},{2,18},{10... | collective-permute-start | bytes 196616 | tf_op jit(solution)/shard_map/ppermute | solution.py:33
  57.3 5.9 %collective-permute-start.26 = (bf16[32,1024]{1,0:T(8,128)(2,1)S(1)}, bf16[32,1024]{1,0:T(8,128)(2,1)S(1)}, u32[]{:S(2)}, u32[]{:S(2)}) collective-permute-start(bf16[32,1024]{1,0:T(8,128)(2,1)S(1)} %slice.54), channel_id=1, source_target_pairs={{0,16},{8,24},{16,0},{24,8},{1,17},{9,25},{17,1},{25,9},{2,18},{10... | collective-permute-start | bytes 196616 | tf_op jit(solution)/shard_map/ppermute | solution.py:33
  60.5 6.5 %collective-permute-start.21 = (bf16[32,1024]{1,0:T(8,128)(2,1)S(1)}, bf16[32,1024]{1,0:T(8,128)(2,1)S(1)}, u32[]{:S(2)}, u32[]{:S(2)}) collective-permute-start(bf16[32,1024]{1,0:T(8,128)(2,1)S(1)} %add_convert_fusion.8), channel_id=1, source_target_pairs={{0,3},{1,2},{2,1},{3,0},{4,7},{5,6},{6,5},{7,4},{8,11},{9,10},{10,... | collective-permute-start | bytes 196616 | tf_op jit(solution)/shard_map/ppermute | solution.py:33
  62.5 6.4 %collective-permute-start.24 = (bf16[32,1024]{1,0:T(8,128)(2,1)S(1)}, bf16[32,1024]{1,0:T(8,128)(2,1)S(1)}, u32[]{:S(2)}, u32[]{:S(2)}) collective-permute-start(bf16[32,1024]{1,0:T(8,128)(2,1)S(1)} %add_convert_fusion.7), channel_id=1, source_target_pairs={{0,2},{1,3},{2,0},{3,1},{4,6},{5,7},{6,4},{7,5},{8,10},{9,11},{10,... | collective-permute-start | bytes 196616 | tf_op jit(solution)/shard_map/ppermute | solution.py:33
  63.2 5.8 %collective-permute-start.27 = (bf16[32,1024]{1,0:T(8,128)(2,1)S(1)}, bf16[32,1024]{1,0:T(8,128)(2,1)S(1)}, u32[]{:S(2)}, u32[]{:S(2)}) collective-permute-start(bf16[32,1024]{1,0:T(8,128)(2,1)S(1)} %add_convert_fusion.6), channel_id=1, source_target_pairs={{0,1},{1,0},{2,3},{3,2},{4,5},{5,4},{6,7},{7,6},{8,9},{9,8},{10,11... | collective-permute-start | bytes 196616 | tf_op jit(solution)/shard_map/ppermute | solution.py:33
  69.0 4.0 %collective-permute-start.33 = (bf16[16,1024]{1,0:T(8,128)(2,1)S(1)}, bf16[16,1024]{1,0:T(8,128)(2,1)S(1)}, u32[]{:S(2)}, u32[]{:S(2)}) collective-permute-start(bf16[16,1024]{1,0:T(8,128)(2,1)S(1)} %get-tuple-element.51), channel_id=1, source_target_pairs={{0,4},{4,0},{1,5},{5,1},{2,6},{6,2},{3,7},{7,3},{8,12},{12,8},{9,1... | collective-permute-start | bytes 98312 | tf_op jit(solution)/shard_map/ppermute | solution.py:33
  69.9 4.1 %collective-permute-start.30 = (bf16[16,1024]{1,0:T(8,128)(2,1)S(1)}, bf16[16,1024]{1,0:T(8,128)(2,1)S(1)}, u32[]{:S(2)}, u32[]{:S(2)}) collective-permute-start(bf16[16,1024]{1,0:T(8,128)(2,1)S(1)} %get-tuple-element.52.refs_0_), channel_id=1, source_target_pairs={{0,8},{8,0},{16,24},{24,16},{1,9},{9,1},{17,25},{25,17},{2,10},{10... | collective-permute-start | bytes 98312 | tf_op jit(solution)/shard_map/ppermute | solution.py:33
  69.9 5.2 %collective-permute-start.31 = (bf16[16,1024]{1,0:T(8,128)(2,1)S(1)}, bf16[16,1024]{1,0:T(8,128)(2,1)S(1)}, u32[]{:S(2)}, u32[]{:S(2)}) collective-permute-start(bf16[16,1024]{1,0:T(8,128)(2,1)S(1)} %get-tuple-element.52.refs_0_), channel_id=1, source_target_pairs={{0,16},{8,24},{16,0},{24,8},{1,17},{9,25},{17,1},{25,9},{2,18},{10... | collective-permute-start | bytes 98312 | tf_op jit(solution)/shard_map/ppermute | solution.py:33
  71.3 3.8 %collective-permute-start.32 = (bf16[16,1024]{1,0:T(8,128)(2,1)S(1)}, bf16[16,1024]{1,0:T(8,128)(2,1)S(1)}, u32[]{:S(2)}, u32[]{:S(2)}) collective-permute-start(bf16[16,1024]{1,0:T(8,128)(2,1)S(1)} %get-tuple-element.52.refs_0_), channel_id=1, source_target_pairs={{0,24},{8,16},{16,8},{24,0},{1,25},{9,17},{17,9},{25,1},{2,26},{10... | collective-permute-start | bytes 98312 | tf_op jit(solution)/shard_map/ppermute | solution.py:33
  73.0 2.1 %collective-permute-start.34 = (bf16[16,1024]{1,0:T(8,128)(2,1)S(1)}, bf16[16,1024]{1,0:T(8,128)(2,1)S(1)}, u32[]{:S(2)}, u32[]{:S(2)}) collective-permute-start(bf16[16,1024]{1,0:T(8,128)(2,1)S(1)} %collective-permute-done.33.refs_4_), channel_id=1, source_target_pairs={{0,8},{8,0},{16,24},{24,16},{1,9},{9,1},{17,25},{25,17},{2,10},{10... | collective-permute-start | bytes 98312 | tf_op jit(solution)/shard_map/ppermute | solution.py:33
  73.0 3.9 %collective-permute-start.35 = (bf16[16,1024]{1,0:T(8,128)(2,1)S(1)}, bf16[16,1024]{1,0:T(8,128)(2,1)S(1)}, u32[]{:S(2)}, u32[]{:S(2)}) collective-permute-start(bf16[16,1024]{1,0:T(8,128)(2,1)S(1)} %collective-permute-done.33.refs_4_), channel_id=1, source_target_pairs={{0,16},{8,24},{16,0},{24,8},{1,17},{9,25},{17,1},{25,9},{2,18},{10... | collective-permute-start | bytes 98312 | tf_op jit(solution)/shard_map/ppermute | solution.py:33
  74.0 3.3 %collective-permute-start.36 = (bf16[16,1024]{1,0:T(8,128)(2,1)S(1)}, bf16[16,1024]{1,0:T(8,128)(2,1)S(1)}, u32[]{:S(2)}, u32[]{:S(2)}) collective-permute-start(bf16[16,1024]{1,0:T(8,128)(2,1)S(1)} %collective-permute-done.33.refs_4_), channel_id=1, source_target_pairs={{0,24},{8,16},{16,8},{24,0},{1,25},{9,17},{17,9},{25,1},{2,26},{10... | collective-permute-start | bytes 98312 | tf_op jit(solution)/shard_map/ppermute | solution.py:33

commit v6 on v5

--- a/solution.py
+++ b/solution.py
@@ -335,7 +335,18 @@
     gathered = []
     for group in groups:
         gathered += [group] + [swap(group, "batch", r) for r in range(1, batches)]
-    return call(output_body, shape((token_count, share), BF16), combine, *gathered)[None]
+    cut = 2 if share % 256 == 0 else 1
+    block = share // cut
+    return pl.pallas_call(
+        output_body,
+        grid=(cut,),
+        out_shape=shape((token_count, share), BF16),
+        in_specs=[pl.BlockSpec(combine.shape, lambda j: (0, 0))]
+        + [pl.BlockSpec((g.shape[0], block), lambda j: (0, j)) for g in gathered],
+        out_specs=pl.BlockSpec((token_count, block), lambda j: (0, j)),
+        compiler_params=pltpu.CompilerParams(vmem_limit_bytes=8 << 20),
+        name="output",
+    )(combine, *gathered)[None]
 
 
 def direct(batches, s):

time: 78.6 us -> 78.8 us (level)
    pallas_call x0 -> x1, Pallas kernels: none -> 1.21 us  [local(): pl.pallas_call(output_body, grid=(cut,), out_shape=shape((token_count, sh...]
    pallas_call x11 -> x10, Pallas kernels: 6.22 us -> 5.15 us  [call(): pl.pallas_call(body, out_shape=shapes, in_specs=[VMEM] * len(args), out_s...]
where the time goes in v6:
time: 78.8 us; the launch traced here: 78.5 us
  starting transfers between devices  34.3 us (44%)
  waiting for transfers between devices  25.7 us (33%)
  Pallas kernels  17.8 us (23%)
    ppermute x37, starting transfers between devices, swap(): return lax.ppermute(x, axes, [(i, i ^ bit) for i in range(count)])  34.3 us
    ppermute x37, waiting for transfers between devices, swap(): return lax.ppermute(x, axes, [(i, i ^ bit) for i in range(count)])  25.7 us
    pallas_call x3, Pallas kernels, fetch(): pl.pallas_call(fetch_body, out_shape=[pltpu.VMEM(a.shape, a.dtype) for a...  9.28 us
    pallas_call x10, Pallas kernels, call(): pl.pallas_call(body, out_shape=shapes, in_specs=[VMEM] * len(args), out_s...  5.15 us
  transfers between devices with their start and end apart: 37, of which 14 were waited for; matrix products, arithmetic and copies ran while one was open for 0% of the time, Pallas kernels for 17%

profile of v6, /device:TPU:0, one launch (start us, length us, event | category | flops | bytes accessed | tf_op | source)
XLA Modules:
  0.0 78.5 jit_solution(13937674820956125335)
XLA Ops:
  0.0 1.5 %logits.1 = (bf16[256,1024]{1,0:T(8,128)(2,1)S(1)}, f32[136,256]{1,0:T(8,128)S(1)}, f32[72,256]{1,0:T(8,128)S(1)}) custom-call(bf16[1,256,1024]{2,1,0:T(8,128)(2,1)} %tok_hbm.1, bf16[1024]{0:T(1024)(128)(2,1)} %gain_hbm.1, bf16[1024,128]{1,0:T(8,128)(2,1)} %phi_hbm.1), custom_call_target="tpu_custom_call" | custom-call | flops 1073741824 | bytes 4194304 | tf_op jit(solution)/shard_map/logits/pallas_call | solution.py:220
  1.5 3.1 %collective-permute-start = (f32[136,256]{1,0:T(8,128)S(1)}, f32[136,256]{1,0:T(8,128)S(1)}, u32[]{:S(2)}, u32[]{:S(2)}) collective-permute-start(f32[136,256]{1,0:T(8,128)S(1)} %get-tuple-element.28.refs_0_), channel_id=1, source_target_pairs={{0,1},{1,0},{2,3},{3,2},{4,5},{5,4},{6,7},{7,6},{8,9},{9,8},{10,11... | collective-permute-start | bytes 417800 | tf_op jit(solution)/shard_map/ppermute | solution.py:33
  4.6 2.6 %collective-permute-start.2 = (f32[72,256]{1,0:T(8,128)S(1)}, f32[72,256]{1,0:T(8,128)S(1)}, u32[]{:S(2)}, u32[]{:S(2)}) collective-permute-start(f32[72,256]{1,0:T(8,128)S(1)} %get-tuple-element.29), channel_id=1, source_target_pairs={{0,2},{1,3},{2,0},{3,1},{4,6},{5,7},{6,4},{7,5},{8,10},{9,11},{10,... | collective-permute-start | bytes 221192 | tf_op jit(solution)/shard_map/ppermute | solution.py:33
  7.2 0.0 collective-permute-start.3
  7.2 1.9 %collective-permute-done.refs_1_ = f32[136,256]{1,0:T(8,128)S(1)} collective-permute-done((f32[136,256]{1,0:T(8,128)S(1)}, f32[136,256]{1,0:T(8,128)S(1)}, u32[]{:S(2)}, u32[]{:S(2)}) %collective-permute-start) | collective-permute-done | bytes 139296 | tf_op jit(solution)/shard_map/ppermute | solution.py:33
  9.1 3.2 %collective-permute-start.1 = (f32[64,256]{1,0:T(8,128)S(1)}, f32[64,256]{1,0:T(8,128)S(1)}, u32[]{:S(2)}, u32[]{:S(2)}) collective-permute-start(f32[64,256]{1,0:T(8,128)S(1)} %slice_add_fusion), channel_id=1, source_target_pairs={{0,2},{1,3},{2,0},{3,1},{4,6},{5,7},{6,4},{7,5},{8,10},{9,11},{10,... | collective-permute-start | bytes 196616 | tf_op jit(solution)/shard_map/ppermute | solution.py:33
  12.3 5.0 %collective-permute-done.1 = f32[64,256]{1,0:T(8,128)S(1)} collective-permute-done((f32[64,256]{1,0:T(8,128)S(1)}, f32[64,256]{1,0:T(8,128)S(1)}, u32[]{:S(2)}, u32[]{:S(2)}) %collective-permute-start.1) | collective-permute-done | bytes 65568 | tf_op jit(solution)/shard_map/ppermute | solution.py:33
  17.3 0.0 collective-permute-done.2.refs_3_
  17.4 0.4 slots.1
  17.8 0.1 collective-permute-start.4
  17.9 3.1 %fetch.3.refs_2_ = bf16[1,4096,896]{2,1,0:T(8,128)(2,1)S(1)} custom-call(bf16[1,4096,896]{2,1,0:T(8,128)(2,1)} %refs_0_.3), custom_call_target="tpu_custom_call" | custom-call | flops 1073741824 | bytes 33554432 | tf_op jit(solution)/shard_map/fetch/pallas_call | solution.py:193
  21.0 0.0 collective-permute-done.4.came_ref
  21.0 0.2 shard_map.64
  21.2 1.6 %collective-permute-start.5 = (bf16[16,1152]{1,0:T(8,128)(2,1)S(1)}, bf16[16,1152]{1,0:T(8,128)(2,1)S(1)}, u32[]{:S(2)}, u32[]{:S(2)}) collective-permute-start(bf16[16,1152]{1,0:T(8,128)(2,1)S(1)} %get-tuple-element.34), channel_id=1, source_target_pairs={{0,16},{4,20},{8,24},{12,28},{16,0},{20,4},{24,8},{28,12},{1,17},{... | collective-permute-start | bytes 110600 | tf_op jit(solution)/shard_map/ppermute | solution.py:33
  22.8 1.5 %collective-permute-start.6 = (bf16[16,1152]{1,0:T(8,128)(2,1)S(1)}, bf16[16,1152]{1,0:T(8,128)(2,1)S(1)}, u32[]{:S(2)}, u32[]{:S(2)}) collective-permute-start(bf16[16,1152]{1,0:T(8,128)(2,1)S(1)} %get-tuple-element.35), channel_id=1, source_target_pairs={{0,4},{4,0},{8,12},{12,8},{16,20},{20,16},{24,28},{28,24},{1,5},{5... | collective-permute-start | bytes 110600 | tf_op jit(solution)/shard_map/ppermute | solution.py:33
  24.3 0.5 collective-permute-start.7
  24.8 3.1 %fetch.4.refs_3_ = bf16[1,4096,896]{2,1,0:T(8,128)(2,1)S(1)} custom-call(bf16[1,4096,896]{2,1,0:T(8,128)(2,1)} %refs_0_.4), custom_call_target="tpu_custom_call" | custom-call | flops 1073741824 | bytes 33554432 | tf_op jit(solution)/shard_map/fetch/pallas_call | solution.py:193
  27.9 1.3 %collective-permute-done.7.refs_3_ = bf16[16,1152]{1,0:T(8,128)(2,1)S(1)} collective-permute-done((bf16[16,1152]{1,0:T(8,128)(2,1)S(1)}, bf16[16,1152]{1,0:T(8,128)(2,1)S(1)}, u32[]{:S(2)}, u32[]{:S(2)}) %collective-permute-start.7) | collective-permute-done | bytes 36896 | tf_op jit(solution)/shard_map/ppermute | solution.py:33
  29.2 0.2 shard_map.65
  29.4 0.6 collective-permute-start.17
  29.9 3.1 %fetch.5.down_ref = bf16[1,896,4096]{2,1,0:T(8,128)(2,1)S(1)} custom-call(bf16[1,896,4096]{2,1,0:T(8,128)(2,1)} %refs_0_.5), custom_call_target="tpu_custom_call" | custom-call | flops 1073741824 | bytes 33554432 | tf_op jit(solution)/shard_map/fetch/pallas_call | solution.py:193
  33.0 0.1 collective-permute-start.14
  33.1 3.0 %collective-permute-start.15 = (bf16[32,1024]{1,0:T(8,128)(2,1)S(1)}, bf16[32,1024]{1,0:T(8,128)(2,1)S(1)}, u32[]{:S(2)}, u32[]{:S(2)}) collective-permute-start(bf16[32,1024]{1,0:T(8,128)(2,1)S(1)} %shard_map.65), channel_id=1, source_target_pairs={{0,17},{1,16},{2,19},{3,18},{8,25},{9,24},{10,27},{11,26},{16,1},{... | collective-permute-start | bytes 196616 | tf_op jit(solution)/shard_map/ppermute | solution.py:33
  36.1 2.0 %collective-permute-start.11 = (bf16[32,1024]{1,0:T(8,128)(2,1)S(1)}, bf16[32,1024]{1,0:T(8,128)(2,1)S(1)}, u32[]{:S(2)}, u32[]{:S(2)}) collective-permute-start(bf16[32,1024]{1,0:T(8,128)(2,1)S(1)} %shard_map.65), channel_id=1, source_target_pairs={{0,3},{1,2},{2,1},{3,0},{4,7},{5,6},{6,5},{7,4},{8,11},{9,10},{10,... | collective-permute-start | bytes 196616 | tf_op jit(solution)/shard_map/ppermute | solution.py:33
  38.1 0.1 collective-permute-start.18
  38.2 0.9 %collective-permute-done.15 = bf16[32,1024]{1,0:T(8,128)(2,1)S(1)} collective-permute-done((bf16[32,1024]{1,0:T(8,128)(2,1)S(1)}, bf16[32,1024]{1,0:T(8,128)(2,1)S(1)}, u32[]{:S(2)}, u32[]{:S(2)}) %collective-permute-start.15) | collective-permute-done | bytes 65568 | tf_op jit(solution)/shard_map/ppermute | solution.py:33
  39.0 3.1 %collective-permute-done.11 = bf16[32,1024]{1,0:T(8,128)(2,1)S(1)} collective-permute-done((bf16[32,1024]{1,0:T(8,128)(2,1)S(1)}, bf16[32,1024]{1,0:T(8,128)(2,1)S(1)}, u32[]{:S(2)}, u32[]{:S(2)}) %collective-permute-start.11) | collective-permute-done | bytes 65568 | tf_op jit(solution)/shard_map/ppermute | solution.py:33
  42.1 0.5 collective-permute-start.12
  42.6 0.9 %collective-permute-done.8 = bf16[32,1024]{1,0:T(8,128)(2,1)S(1)} collective-permute-done((bf16[32,1024]{1,0:T(8,128)(2,1)S(1)}, bf16[32,1024]{1,0:T(8,128)(2,1)S(1)}, u32[]{:S(2)}, u32[]{:S(2)}) %collective-permute-start.8) | collective-permute-done | bytes 65568 | tf_op jit(solution)/shard_map/ppermute | solution.py:33
  43.5 0.9 %collective-permute-start.9 = (bf16[32,1024]{1,0:T(8,128)(2,1)S(1)}, bf16[32,1024]{1,0:T(8,128)(2,1)S(1)}, u32[]{:S(2)}, u32[]{:S(2)}) collective-permute-start(bf16[32,1024]{1,0:T(8,128)(2,1)S(1)} %collective-permute-done.8), channel_id=1, source_target_pairs={{0,16},{8,24},{16,0},{24,8},{1,17},{9,25},{17,1},{25,9},{2,18},{10... | collective-permute-start | bytes 196616 | tf_op jit(solution)/shard_map/ppermute | solution.py:33
  44.5 1.9 %collective-permute-done.12 = bf16[32,1024]{1,0:T(8,128)(2,1)S(1)} collective-permute-done((bf16[32,1024]{1,0:T(8,128)(2,1)S(1)}, bf16[32,1024]{1,0:T(8,128)(2,1)S(1)}, u32[]{:S(2)}, u32[]{:S(2)}) %collective-permute-start.12) | collective-permute-done | bytes 65568 | tf_op jit(solution)/shard_map/ppermute | solution.py:33
  46.4 1.4 %collective-permute-done.9 = bf16[32,1024]{1,0:T(8,128)(2,1)S(1)} collective-permute-done((bf16[32,1024]{1,0:T(8,128)(2,1)S(1)}, bf16[32,1024]{1,0:T(8,128)(2,1)S(1)}, u32[]{:S(2)}, u32[]{:S(2)}) %collective-permute-start.9) | collective-permute-done | bytes 65568 | tf_op jit(solution)/shard_map/ppermute | solution.py:33
  47.8 0.7 shard_map.66
  48.6 0.7 shard_map.67
  49.3 0.7 shard_map.68
  50.1 0.7 shard_map.69.hidden_ref
  50.8 0.5 shard_map.73
  51.3 0.6 collective-permute-start.28
  51.8 0.4 shard_map.70
  52.3 0.1 collective-permute-start.19
  52.4 0.5 shard_map.71
  52.9 0.5 collective-permute-start.22
  53.4 0.4 shard_map.72
  53.8 0.1 collective-permute-start.25
  54.0 1.0 %collective-permute-start.29 = (bf16[32,1024]{1,0:T(8,128)(2,1)S(1)}, bf16[32,1024]{1,0:T(8,128)(2,1)S(1)}, u32[]{:S(2)}, u32[]{:S(2)}) collective-permute-start(bf16[32,1024]{1,0:T(8,128)(2,1)S(1)} %slice.56), channel_id=1, source_target_pairs={{0,16},{8,24},{16,0},{24,8},{1,17},{9,25},{17,1},{25,9},{2,18},{10... | collective-permute-start | bytes 196616 | tf_op jit(solution)/shard_map/ppermute | solution.py:33
  55.0 1.2 %collective-permute-start.20 = (bf16[32,1024]{1,0:T(8,128)(2,1)S(1)}, bf16[32,1024]{1,0:T(8,128)(2,1)S(1)}, u32[]{:S(2)}, u32[]{:S(2)}) collective-permute-start(bf16[32,1024]{1,0:T(8,128)(2,1)S(1)} %slice.50), channel_id=1, source_target_pairs={{0,16},{8,24},{16,0},{24,8},{1,17},{9,25},{17,1},{25,9},{2,18},{10... | collective-permute-start | bytes 196616 | tf_op jit(solution)/shard_map/ppermute | solution.py:33
  56.3 1.0 %collective-permute-start.23 = (bf16[32,1024]{1,0:T(8,128)(2,1)S(1)}, bf16[32,1024]{1,0:T(8,128)(2,1)S(1)}, u32[]{:S(2)}, u32[]{:S(2)}) collective-permute-start(bf16[32,1024]{1,0:T(8,128)(2,1)S(1)} %slice.52), channel_id=1, source_target_pairs={{0,16},{8,24},{16,0},{24,8},{1,17},{9,25},{17,1},{25,9},{2,18},{10... | collective-permute-start | bytes 196616 | tf_op jit(solution)/shard_map/ppermute | solution.py:33
  57.3 1.2 %collective-permute-start.26 = (bf16[32,1024]{1,0:T(8,128)(2,1)S(1)}, bf16[32,1024]{1,0:T(8,128)(2,1)S(1)}, u32[]{:S(2)}, u32[]{:S(2)}) collective-permute-start(bf16[32,1024]{1,0:T(8,128)(2,1)S(1)} %slice.54), channel_id=1, source_target_pairs={{0,16},{8,24},{16,0},{24,8},{1,17},{9,25},{17,1},{25,9},{2,18},{10... | collective-permute-start | bytes 196616 | tf_op jit(solution)/shard_map/ppermute | solution.py:33
  58.5 1.9 %collective-permute-done.20 = bf16[32,1024]{1,0:T(8,128)(2,1)S(1)} collective-permute-done((bf16[32,1024]{1,0:T(8,128)(2,1)S(1)}, bf16[32,1024]{1,0:T(8,128)(2,1)S(1)}, u32[]{:S(2)}, u32[]{:S(2)}) %collective-permute-start.20) | collective-permute-done | bytes 65568 | tf_op jit(solution)/shard_map/ppermute | solution.py:33
  60.5 2.0 %collective-permute-start.21 = (bf16[32,1024]{1,0:T(8,128)(2,1)S(1)}, bf16[32,1024]{1,0:T(8,128)(2,1)S(1)}, u32[]{:S(2)}, u32[]{:S(2)}) collective-permute-start(bf16[32,1024]{1,0:T(8,128)(2,1)S(1)} %add_convert_fusion.8), channel_id=1, source_target_pairs={{0,3},{1,2},{2,1},{3,0},{4,7},{5,6},{6,5},{7,4},{8,11},{9,10},{10,... | collective-permute-start | bytes 196616 | tf_op jit(solution)/shard_map/ppermute | solution.py:33
  62.5 0.6 collective-permute-start.24
  63.2 1.9 %collective-permute-start.27 = (bf16[32,1024]{1,0:T(8,128)(2,1)S(1)}, bf16[32,1024]{1,0:T(8,128)(2,1)S(1)}, u32[]{:S(2)}, u32[]{:S(2)}) collective-permute-start(bf16[32,1024]{1,0:T(8,128)(2,1)S(1)} %add_convert_fusion.6), channel_id=1, source_target_pairs={{0,1},{1,0},{2,3},{3,2},{4,5},{5,4},{6,7},{7,6},{8,9},{9,8},{10,11... | collective-permute-start | bytes 196616 | tf_op jit(solution)/shard_map/ppermute | solution.py:33
  65.1 1.9 %collective-permute-done.21 = bf16[32,1024]{1,0:T(8,128)(2,1)S(1)} collective-permute-done((bf16[32,1024]{1,0:T(8,128)(2,1)S(1)}, bf16[32,1024]{1,0:T(8,128)(2,1)S(1)}, u32[]{:S(2)}, u32[]{:S(2)}) %collective-permute-start.21) | collective-permute-done | bytes 65568 | tf_op jit(solution)/shard_map/ppermute | solution.py:33
  67.0 2.0 %collective-permute-done.24 = bf16[32,1024]{1,0:T(8,128)(2,1)S(1)} collective-permute-done((bf16[32,1024]{1,0:T(8,128)(2,1)S(1)}, bf16[32,1024]{1,0:T(8,128)(2,1)S(1)}, u32[]{:S(2)}, u32[]{:S(2)}) %collective-permute-start.24) | collective-permute-done | bytes 65568 | tf_op jit(solution)/shard_map/ppermute | solution.py:33
  69.0 0.9 %collective-permute-start.33 = (bf16[16,1024]{1,0:T(8,128)(2,1)S(1)}, bf16[16,1024]{1,0:T(8,128)(2,1)S(1)}, u32[]{:S(2)}, u32[]{:S(2)}) collective-permute-start(bf16[16,1024]{1,0:T(8,128)(2,1)S(1)} %get-tuple-element.51), channel_id=1, source_target_pairs={{0,4},{4,0},{1,5},{5,1},{2,6},{6,2},{3,7},{7,3},{8,12},{12,8},{9,1... | collective-permute-start | bytes 98312 | tf_op jit(solution)/shard_map/ppermute | solution.py:33
  69.9 1.4 %collective-permute-start.31 = (bf16[16,1024]{1,0:T(8,128)(2,1)S(1)}, bf16[16,1024]{1,0:T(8,128)(2,1)S(1)}, u32[]{:S(2)}, u32[]{:S(2)}) collective-permute-start(bf16[16,1024]{1,0:T(8,128)(2,1)S(1)} %get-tuple-element.52.refs_0_), channel_id=1, source_target_pairs={{0,16},{8,24},{16,0},{24,8},{1,17},{9,25},{17,1},{25,9},{2,18},{10... | collective-permute-start | bytes 98312 | tf_op jit(solution)/shard_map/ppermute | solution.py:33
  71.3 0.5 collective-permute-start.32
  71.7 1.3 %collective-permute-done.33.refs_4_ = bf16[16,1024]{1,0:T(8,128)(2,1)S(1)} collective-permute-done((bf16[16,1024]{1,0:T(8,128)(2,1)S(1)}, bf16[16,1024]{1,0:T(8,128)(2,1)S(1)}, u32[]{:S(2)}, u32[]{:S(2)}) %collective-permute-start.33) | collective-permute-done | bytes 32800 | tf_op jit(solution)/shard_map/ppermute | solution.py:33
  73.0 1.0 %collective-permute-start.35 = (bf16[16,1024]{1,0:T(8,128)(2,1)S(1)}, bf16[16,1024]{1,0:T(8,128)(2,1)S(1)}, u32[]{:S(2)}, u32[]{:S(2)}) collective-permute-start(bf16[16,1024]{1,0:T(8,128)(2,1)S(1)} %collective-permute-done.33.refs_4_), channel_id=1, source_target_pairs={{0,16},{8,24},{16,0},{24,8},{1,17},{9,25},{17,1},{25,9},{2,18},{10... | collective-permute-start | bytes 98312 | tf_op jit(solution)/shard_map/ppermute | solution.py:33
  74.0 0.9 %collective-permute-start.36 = (bf16[16,1024]{1,0:T(8,128)(2,1)S(1)}, bf16[16,1024]{1,0:T(8,128)(2,1)S(1)}, u32[]{:S(2)}, u32[]{:S(2)}) collective-permute-start(bf16[16,1024]{1,0:T(8,128)(2,1)S(1)} %collective-permute-done.33.refs_4_), channel_id=1, source_target_pairs={{0,24},{8,16},{16,8},{24,0},{1,25},{9,17},{17,9},{25,1},{2,26},{10... | collective-permute-start | bytes 98312 | tf_op jit(solution)/shard_map/ppermute | solution.py:33
  74.9 0.2 combine.1.combine_ref
  75.1 1.8 %collective-permute-done.35.refs_6_ = bf16[16,1024]{1,0:T(8,128)(2,1)S(1)} collective-permute-done((bf16[16,1024]{1,0:T(8,128)(2,1)S(1)}, bf16[16,1024]{1,0:T(8,128)(2,1)S(1)}, u32[]{:S(2)}, u32[]{:S(2)}) %collective-permute-start.35) | collective-permute-done | bytes 32800 | tf_op jit(solution)/shard_map/ppermute | solution.py:33
  76.9 0.4 collective-permute-done.36.refs_7_
  77.3 1.2 %output.1 = bf16[256,1024]{1,0:T(8,128)(2,1)} custom-call(bf16[256,128]{1,0:T(8,128)(2,1)S(1)} %combine.1.combine_ref, bf16[16,1024]{1,0:T(8,128)(2,1)S(1)} %get-tuple-element.52.refs_0_, bf16[16,1024]{1,0:T(8,128)(2,1)S(1)} %collective-permute-done.30.refs_1_, bf16[16,1024]{1,0:T(8,128)(2,1)S(1)} %collective-permute-done.31.refs_2_, ...), custom_call_target="tpu_custom_call" | custom-call | tf_op jit(solution)/shard_map/output/pallas_call | solution.py:340
  (49 shorter events, 0.4 us)
Async XLA Ops:
  1.5 7.6 %collective-permute-start = (f32[136,256]{1,0:T(8,128)S(1)}, f32[136,256]{1,0:T(8,128)S(1)}, u32[]{:S(2)}, u32[]{:S(2)}) collective-permute-start(f32[136,256]{1,0:T(8,128)S(1)} %get-tuple-element.28.refs_0_), channel_id=1, source_target_pairs={{0,1},{1,0},{2,3},{3,2},{4,5},{5,4},{6,7},{7,6},{8,9},{9,8},{10,11... | collective-permute-start | bytes 417800 | tf_op jit(solution)/shard_map/ppermute | solution.py:33
  4.6 12.7 %collective-permute-start.2 = (f32[72,256]{1,0:T(8,128)S(1)}, f32[72,256]{1,0:T(8,128)S(1)}, u32[]{:S(2)}, u32[]{:S(2)}) collective-permute-start(f32[72,256]{1,0:T(8,128)S(1)} %get-tuple-element.29), channel_id=1, source_target_pairs={{0,2},{1,3},{2,0},{3,1},{4,6},{5,7},{6,4},{7,5},{8,10},{9,11},{10,... | collective-permute-start | bytes 221192 | tf_op jit(solution)/shard_map/ppermute | solution.py:33
  7.2 10.1 %collective-permute-start.3 = (f32[72,256]{1,0:T(8,128)S(1)}, f32[72,256]{1,0:T(8,128)S(1)}, u32[]{:S(2)}, u32[]{:S(2)}) collective-permute-start(f32[72,256]{1,0:T(8,128)S(1)} %get-tuple-element.29), channel_id=1, source_target_pairs={{0,3},{1,2},{2,1},{3,0},{4,7},{5,6},{6,5},{7,4},{8,11},{9,10},{10,... | collective-permute-start | bytes 221192 | tf_op jit(solution)/shard_map/ppermute | solution.py:33
  9.1 8.2 %collective-permute-start.1 = (f32[64,256]{1,0:T(8,128)S(1)}, f32[64,256]{1,0:T(8,128)S(1)}, u32[]{:S(2)}, u32[]{:S(2)}) collective-permute-start(f32[64,256]{1,0:T(8,128)S(1)} %slice_add_fusion), channel_id=1, source_target_pairs={{0,2},{1,3},{2,0},{3,1},{4,6},{5,7},{6,4},{7,5},{8,10},{9,11},{10,... | collective-permute-start | bytes 196616 | tf_op jit(solution)/shard_map/ppermute | solution.py:33
  17.8 3.2 %collective-permute-start.4 = (bf16[64,1152]{1,0:T(8,128)(2,1)S(1)}, bf16[64,1152]{1,0:T(8,128)(2,1)S(1)}, u32[]{:S(2)}, u32[]{:S(2)}) collective-permute-start(bf16[64,1152]{1,0:T(8,128)(2,1)S(1)} %get-tuple-element.32), channel_id=1, source_target_pairs={{0,8},{8,0},{16,24},{24,16},{1,9},{9,1},{17,25},{25,17},{2,10},{10... | collective-permute-start | bytes 442376 | tf_op jit(solution)/shard_map/ppermute | solution.py:33
  21.2 6.7 %collective-permute-start.5 = (bf16[16,1152]{1,0:T(8,128)(2,1)S(1)}, bf16[16,1152]{1,0:T(8,128)(2,1)S(1)}, u32[]{:S(2)}, u32[]{:S(2)}) collective-permute-start(bf16[16,1152]{1,0:T(8,128)(2,1)S(1)} %get-tuple-element.34), channel_id=1, source_target_pairs={{0,16},{4,20},{8,24},{12,28},{16,0},{20,4},{24,8},{28,12},{1,17},{... | collective-permute-start | bytes 110600 | tf_op jit(solution)/shard_map/ppermute | solution.py:33
  22.8 5.1 %collective-permute-start.6 = (bf16[16,1152]{1,0:T(8,128)(2,1)S(1)}, bf16[16,1152]{1,0:T(8,128)(2,1)S(1)}, u32[]{:S(2)}, u32[]{:S(2)}) collective-permute-start(bf16[16,1152]{1,0:T(8,128)(2,1)S(1)} %get-tuple-element.35), channel_id=1, source_target_pairs={{0,4},{4,0},{8,12},{12,8},{16,20},{20,16},{24,28},{28,24},{1,5},{5... | collective-permute-start | bytes 110600 | tf_op jit(solution)/shard_map/ppermute | solution.py:33
  24.3 4.9 %collective-permute-start.7 = (bf16[16,1152]{1,0:T(8,128)(2,1)S(1)}, bf16[16,1152]{1,0:T(8,128)(2,1)S(1)}, u32[]{:S(2)}, u32[]{:S(2)}) collective-permute-start(bf16[16,1152]{1,0:T(8,128)(2,1)S(1)} %get-tuple-element.36), channel_id=1, source_target_pairs={{0,20},{4,16},{8,28},{12,24},{16,4},{20,0},{24,12},{28,8},{1,21},{... | collective-permute-start | bytes 110600 | tf_op jit(solution)/shard_map/ppermute | solution.py:33
  29.4 8.7 %collective-permute-start.17 = (bf16[32,1024]{1,0:T(8,128)(2,1)S(1)}, bf16[32,1024]{1,0:T(8,128)(2,1)S(1)}, u32[]{:S(2)}, u32[]{:S(2)}) collective-permute-start(bf16[32,1024]{1,0:T(8,128)(2,1)S(1)} %shard_map.65), channel_id=1, source_target_pairs={{0,16},{8,24},{16,0},{24,8},{1,17},{9,25},{17,1},{25,9},{2,18},{10... | collective-permute-start | bytes 196616 | tf_op jit(solution)/shard_map/ppermute | solution.py:33
  33.0 5.1 %collective-permute-start.14 = (bf16[32,1024]{1,0:T(8,128)(2,1)S(1)}, bf16[32,1024]{1,0:T(8,128)(2,1)S(1)}, u32[]{:S(2)}, u32[]{:S(2)}) collective-permute-start(bf16[32,1024]{1,0:T(8,128)(2,1)S(1)} %shard_map.65), channel_id=1, source_target_pairs={{0,1},{1,0},{2,3},{3,2},{4,5},{5,4},{6,7},{7,6},{8,9},{9,8},{10,11... | collective-permute-start | bytes 196616 | tf_op jit(solution)/shard_map/ppermute | solution.py:33
  33.1 5.9 %collective-permute-start.15 = (bf16[32,1024]{1,0:T(8,128)(2,1)S(1)}, bf16[32,1024]{1,0:T(8,128)(2,1)S(1)}, u32[]{:S(2)}, u32[]{:S(2)}) collective-permute-start(bf16[32,1024]{1,0:T(8,128)(2,1)S(1)} %shard_map.65), channel_id=1, source_target_pairs={{0,17},{1,16},{2,19},{3,18},{8,25},{9,24},{10,27},{11,26},{16,1},{... | collective-permute-start | bytes 196616 | tf_op jit(solution)/shard_map/ppermute | solution.py:33
  36.1 6.1 %collective-permute-start.11 = (bf16[32,1024]{1,0:T(8,128)(2,1)S(1)}, bf16[32,1024]{1,0:T(8,128)(2,1)S(1)}, u32[]{:S(2)}, u32[]{:S(2)}) collective-permute-start(bf16[32,1024]{1,0:T(8,128)(2,1)S(1)} %shard_map.65), channel_id=1, source_target_pairs={{0,3},{1,2},{2,1},{3,0},{4,7},{5,6},{6,5},{7,4},{8,11},{9,10},{10,... | collective-permute-start | bytes 196616 | tf_op jit(solution)/shard_map/ppermute | solution.py:33
  38.0 5.5 %collective-permute-start.8 = (bf16[32,1024]{1,0:T(8,128)(2,1)S(1)}, bf16[32,1024]{1,0:T(8,128)(2,1)S(1)}, u32[]{:S(2)}, u32[]{:S(2)}) collective-permute-start(bf16[32,1024]{1,0:T(8,128)(2,1)S(1)} %shard_map.65), channel_id=1, source_target_pairs={{0,2},{1,3},{2,0},{3,1},{4,6},{5,7},{6,4},{7,5},{8,10},{9,11},{10,... | collective-permute-start | bytes 196616 | tf_op jit(solution)/shard_map/ppermute | solution.py:33
  38.1 9.8 %collective-permute-start.18 = (bf16[64,1024]{1,0:T(8,128)(2,1)S(1)}, bf16[64,1024]{1,0:T(8,128)(2,1)S(1)}, u32[]{:S(2)}, u32[]{:S(2)}) collective-permute-start(bf16[64,1024]{1,0:T(8,128)(2,1)S(1)} %pad_maximum_fusion.refs_0_), channel_id=1, source_target_pairs={{0,8},{8,0},{16,24},{24,16},{1,9},{9,1},{17,25},{25,17},{2,10},{10... | collective-permute-start | bytes 393224 | tf_op jit(solution)/shard_map/ppermute | solution.py:33
  39.0 9.5 %collective-permute-start.16 = (bf16[64,1024]{1,0:T(8,128)(2,1)S(1)}, bf16[64,1024]{1,0:T(8,128)(2,1)S(1)}, u32[]{:S(2)}, u32[]{:S(2)}) collective-permute-start(bf16[64,1024]{1,0:T(8,128)(2,1)S(1)} %constant_dynamic-update-slice_fusion.4.refs_0_), channel_id=1, source_target_pairs={{0,8},{8,0},{16,24},{24,16},{1,9},{9,1},{17,25},{25,17},{2,10},{10... | collective-permute-start | bytes 393224 | tf_op jit(solution)/shard_map/ppermute | solution.py:33
  42.1 4.3 %collective-permute-start.12 = (bf16[32,1024]{1,0:T(8,128)(2,1)S(1)}, bf16[32,1024]{1,0:T(8,128)(2,1)S(1)}, u32[]{:S(2)}, u32[]{:S(2)}) collective-permute-start(bf16[32,1024]{1,0:T(8,128)(2,1)S(1)} %collective-permute-done.11), channel_id=1, source_target_pairs={{0,16},{8,24},{16,0},{24,8},{1,17},{9,25},{17,1},{25,9},{2,18},{10... | collective-permute-start | bytes 196616 | tf_op jit(solution)/shard_map/ppermute | solution.py:33
  43.5 4.3 %collective-permute-start.9 = (bf16[32,1024]{1,0:T(8,128)(2,1)S(1)}, bf16[32,1024]{1,0:T(8,128)(2,1)S(1)}, u32[]{:S(2)}, u32[]{:S(2)}) collective-permute-start(bf16[32,1024]{1,0:T(8,128)(2,1)S(1)} %collective-permute-done.8), channel_id=1, source_target_pairs={{0,16},{8,24},{16,0},{24,8},{1,17},{9,25},{17,1},{25,9},{2,18},{10... | collective-permute-start | bytes 196616 | tf_op jit(solution)/shard_map/ppermute | solution.py:33
  46.4 2.9 %collective-permute-start.13 = (bf16[64,1024]{1,0:T(8,128)(2,1)S(1)}, bf16[64,1024]{1,0:T(8,128)(2,1)S(1)}, u32[]{:S(2)}, u32[]{:S(2)}) collective-permute-start(bf16[64,1024]{1,0:T(8,128)(2,1)S(1)} %constant_dynamic-update-slice_fusion.2.refs_0_), channel_id=1, source_target_pairs={{0,8},{8,0},{16,24},{24,16},{1,9},{9,1},{17,25},{25,17},{2,10},{10... | collective-permute-start | bytes 393224 | tf_op jit(solution)/shard_map/ppermute | solution.py:33
  47.8 2.3 %collective-permute-start.10 = (bf16[64,1024]{1,0:T(8,128)(2,1)S(1)}, bf16[64,1024]{1,0:T(8,128)(2,1)S(1)}, u32[]{:S(2)}, u32[]{:S(2)}) collective-permute-start(bf16[64,1024]{1,0:T(8,128)(2,1)S(1)} %constant_dynamic-update-slice_fusion.refs_0_), channel_id=1, source_target_pairs={{0,8},{8,0},{16,24},{24,16},{1,9},{9,1},{17,25},{25,17},{2,10},{10... | collective-permute-start | bytes 393224 | tf_op jit(solution)/shard_map/ppermute | solution.py:33
  51.3 2.7 %collective-permute-start.28 = (bf16[64,1024]{1,0:T(8,128)(2,1)S(1)}, bf16[64,1024]{1,0:T(8,128)(2,1)S(1)}, u32[]{:S(2)}, u32[]{:S(2)}) collective-permute-start(bf16[64,1024]{1,0:T(8,128)(2,1)S(1)} %get-tuple-element.50), channel_id=1, source_target_pairs={{0,8},{8,0},{16,24},{24,16},{1,9},{9,1},{17,25},{25,17},{2,10},{10... | collective-permute-start | bytes 393224 | tf_op jit(solution)/shard_map/ppermute | solution.py:33
  52.3 2.7 %collective-permute-start.19 = (bf16[64,1024]{1,0:T(8,128)(2,1)S(1)}, bf16[64,1024]{1,0:T(8,128)(2,1)S(1)}, u32[]{:S(2)}, u32[]{:S(2)}) collective-permute-start(bf16[64,1024]{1,0:T(8,128)(2,1)S(1)} %get-tuple-element.44), channel_id=1, source_target_pairs={{0,8},{8,0},{16,24},{24,16},{1,9},{9,1},{17,25},{25,17},{2,10},{10... | collective-permute-start | bytes 393224 | tf_op jit(solution)/shard_map/ppermute | solution.py:33
  52.9 3.4 %collective-permute-start.22 = (bf16[64,1024]{1,0:T(8,128)(2,1)S(1)}, bf16[64,1024]{1,0:T(8,128)(2,1)S(1)}, u32[]{:S(2)}, u32[]{:S(2)}) collective-permute-start(bf16[64,1024]{1,0:T(8,128)(2,1)S(1)} %get-tuple-element.46), channel_id=1, source_target_pairs={{0,8},{8,0},{16,24},{24,16},{1,9},{9,1},{17,25},{25,17},{2,10},{10... | collective-permute-start | bytes 393224 | tf_op jit(solution)/shard_map/ppermute | solution.py:33
  53.8 3.4 %collective-permute-start.25 = (bf16[64,1024]{1,0:T(8,128)(2,1)S(1)}, bf16[64,1024]{1,0:T(8,128)(2,1)S(1)}, u32[]{:S(2)}, u32[]{:S(2)}) collective-permute-start(bf16[64,1024]{1,0:T(8,128)(2,1)S(1)} %get-tuple-element.48), channel_id=1, source_target_pairs={{0,8},{8,0},{16,24},{24,16},{1,9},{9,1},{17,25},{25,17},{2,10},{10... | collective-permute-start | bytes 393224 | tf_op jit(solution)/shard_map/ppermute | solution.py:33
  54.0 11.1 %collective-permute-start.29 = (bf16[32,1024]{1,0:T(8,128)(2,1)S(1)}, bf16[32,1024]{1,0:T(8,128)(2,1)S(1)}, u32[]{:S(2)}, u32[]{:S(2)}) collective-permute-start(bf16[32,1024]{1,0:T(8,128)(2,1)S(1)} %slice.56), channel_id=1, source_target_pairs={{0,16},{8,24},{16,0},{24,8},{1,17},{9,25},{17,1},{25,9},{2,18},{10... | collective-permute-start | bytes 196616 | tf_op jit(solution)/shard_map/ppermute | solution.py:33
  55.0 5.4 %collective-permute-start.20 = (bf16[32,1024]{1,0:T(8,128)(2,1)S(1)}, bf16[32,1024]{1,0:T(8,128)(2,1)S(1)}, u32[]{:S(2)}, u32[]{:S(2)}) collective-permute-start(bf16[32,1024]{1,0:T(8,128)(2,1)S(1)} %slice.50), channel_id=1, source_target_pairs={{0,16},{8,24},{16,0},{24,8},{1,17},{9,25},{17,1},{25,9},{2,18},{10... | collective-permute-start | bytes 196616 | tf_op jit(solution)/shard_map/ppermute | solution.py:33
  56.3 6.2 %collective-permute-start.23 = (bf16[32,1024]{1,0:T(8,128)(2,1)S(1)}, bf16[32,1024]{1,0:T(8,128)(2,1)S(1)}, u32[]{:S(2)}, u32[]{:S(2)}) collective-permute-start(bf16[32,1024]{1,0:T(8,128)(2,1)S(1)} %slice.52), channel_id=1, source_target_pairs={{0,16},{8,24},{16,0},{24,8},{1,17},{9,25},{17,1},{25,9},{2,18},{10... | collective-permute-start | bytes 196616 | tf_op jit(solution)/shard_map/ppermute | solution.py:33
  57.3 5.9 %collective-permute-start.26 = (bf16[32,1024]{1,0:T(8,128)(2,1)S(1)}, bf16[32,1024]{1,0:T(8,128)(2,1)S(1)}, u32[]{:S(2)}, u32[]{:S(2)}) collective-permute-start(bf16[32,1024]{1,0:T(8,128)(2,1)S(1)} %slice.54), channel_id=1, source_target_pairs={{0,16},{8,24},{16,0},{24,8},{1,17},{9,25},{17,1},{25,9},{2,18},{10... | collective-permute-start | bytes 196616 | tf_op jit(solution)/shard_map/ppermute | solution.py:33
  60.5 6.5 %collective-permute-start.21 = (bf16[32,1024]{1,0:T(8,128)(2,1)S(1)}, bf16[32,1024]{1,0:T(8,128)(2,1)S(1)}, u32[]{:S(2)}, u32[]{:S(2)}) collective-permute-start(bf16[32,1024]{1,0:T(8,128)(2,1)S(1)} %add_convert_fusion.8), channel_id=1, source_target_pairs={{0,3},{1,2},{2,1},{3,0},{4,7},{5,6},{6,5},{7,4},{8,11},{9,10},{10,... | collective-permute-start | bytes 196616 | tf_op jit(solution)/shard_map/ppermute | solution.py:33
  62.5 6.4 %collective-permute-start.24 = (bf16[32,1024]{1,0:T(8,128)(2,1)S(1)}, bf16[32,1024]{1,0:T(8,128)(2,1)S(1)}, u32[]{:S(2)}, u32[]{:S(2)}) collective-permute-start(bf16[32,1024]{1,0:T(8,128)(2,1)S(1)} %add_convert_fusion.7), channel_id=1, source_target_pairs={{0,2},{1,3},{2,0},{3,1},{4,6},{5,7},{6,4},{7,5},{8,10},{9,11},{10,... | collective-permute-start | bytes 196616 | tf_op jit(solution)/shard_map/ppermute | solution.py:33
  63.2 5.8 %collective-permute-start.27 = (bf16[32,1024]{1,0:T(8,128)(2,1)S(1)}, bf16[32,1024]{1,0:T(8,128)(2,1)S(1)}, u32[]{:S(2)}, u32[]{:S(2)}) collective-permute-start(bf16[32,1024]{1,0:T(8,128)(2,1)S(1)} %add_convert_fusion.6), channel_id=1, source_target_pairs={{0,1},{1,0},{2,3},{3,2},{4,5},{5,4},{6,7},{7,6},{8,9},{9,8},{10,11... | collective-permute-start | bytes 196616 | tf_op jit(solution)/shard_map/ppermute | solution.py:33
  69.0 4.0 %collective-permute-start.33 = (bf16[16,1024]{1,0:T(8,128)(2,1)S(1)}, bf16[16,1024]{1,0:T(8,128)(2,1)S(1)}, u32[]{:S(2)}, u32[]{:S(2)}) collective-permute-start(bf16[16,1024]{1,0:T(8,128)(2,1)S(1)} %get-tuple-element.51), channel_id=1, source_target_pairs={{0,4},{4,0},{1,5},{5,1},{2,6},{6,2},{3,7},{7,3},{8,12},{12,8},{9,1... | collective-permute-start | bytes 98312 | tf_op jit(solution)/shard_map/ppermute | solution.py:33
  69.9 4.1 %collective-permute-start.30 = (bf16[16,1024]{1,0:T(8,128)(2,1)S(1)}, bf16[16,1024]{1,0:T(8,128)(2,1)S(1)}, u32[]{:S(2)}, u32[]{:S(2)}) collective-permute-start(bf16[16,1024]{1,0:T(8,128)(2,1)S(1)} %get-tuple-element.52.refs_0_), channel_id=1, source_target_pairs={{0,8},{8,0},{16,24},{24,16},{1,9},{9,1},{17,25},{25,17},{2,10},{10... | collective-permute-start | bytes 98312 | tf_op jit(solution)/shard_map/ppermute | solution.py:33
  69.9 5.2 %collective-permute-start.31 = (bf16[16,1024]{1,0:T(8,128)(2,1)S(1)}, bf16[16,1024]{1,0:T(8,128)(2,1)S(1)}, u32[]{:S(2)}, u32[]{:S(2)}) collective-permute-start(bf16[16,1024]{1,0:T(8,128)(2,1)S(1)} %get-tuple-element.52.refs_0_), channel_id=1, source_target_pairs={{0,16},{8,24},{16,0},{24,8},{1,17},{9,25},{17,1},{25,9},{2,18},{10... | collective-permute-start | bytes 98312 | tf_op jit(solution)/shard_map/ppermute | solution.py:33
  71.3 3.8 %collective-permute-start.32 = (bf16[16,1024]{1,0:T(8,128)(2,1)S(1)}, bf16[16,1024]{1,0:T(8,128)(2,1)S(1)}, u32[]{:S(2)}, u32[]{:S(2)}) collective-permute-start(bf16[16,1024]{1,0:T(8,128)(2,1)S(1)} %get-tuple-element.52.refs_0_), channel_id=1, source_target_pairs={{0,24},{8,16},{16,8},{24,0},{1,25},{9,17},{17,9},{25,1},{2,26},{10... | collective-permute-start | bytes 98312 | tf_op jit(solution)/shard_map/ppermute | solution.py:33
  73.0 2.1 %collective-permute-start.34 = (bf16[16,1024]{1,0:T(8,128)(2,1)S(1)}, bf16[16,1024]{1,0:T(8,128)(2,1)S(1)}, u32[]{:S(2)}, u32[]{:S(2)}) collective-permute-start(bf16[16,1024]{1,0:T(8,128)(2,1)S(1)} %collective-permute-done.33.refs_4_), channel_id=1, source_target_pairs={{0,8},{8,0},{16,24},{24,16},{1,9},{9,1},{17,25},{25,17},{2,10},{10... | collective-permute-start | bytes 98312 | tf_op jit(solution)/shard_map/ppermute | solution.py:33
  73.0 3.9 %collective-permute-start.35 = (bf16[16,1024]{1,0:T(8,128)(2,1)S(1)}, bf16[16,1024]{1,0:T(8,128)(2,1)S(1)}, u32[]{:S(2)}, u32[]{:S(2)}) collective-permute-start(bf16[16,1024]{1,0:T(8,128)(2,1)S(1)} %collective-permute-done.33.refs_4_), channel_id=1, source_target_pairs={{0,16},{8,24},{16,0},{24,8},{1,17},{9,25},{17,1},{25,9},{2,18},{10... | collective-permute-start | bytes 98312 | tf_op jit(solution)/shard_map/ppermute | solution.py:33
  74.0 3.3 %collective-permute-start.36 = (bf16[16,1024]{1,0:T(8,128)(2,1)S(1)}, bf16[16,1024]{1,0:T(8,128)(2,1)S(1)}, u32[]{:S(2)}, u32[]{:S(2)}) collective-permute-start(bf16[16,1024]{1,0:T(8,128)(2,1)S(1)} %collective-permute-done.33.refs_4_), channel_id=1, source_target_pairs={{0,24},{8,16},{16,8},{24,0},{1,25},{9,17},{17,9},{25,1},{2,26},{10... | collective-permute-start | bytes 98312 | tf_op jit(solution)/shard_map/ppermute | solution.py:33
